TPU v7x, 32 devices: a whole 2x2x4 slice. The times are simulated.
32 devices in a mesh: unit: 16 (over z, y, x), week: 2 (over core).
Axes of the slice: x: 2, y: 2, z: 4, core: 2. Of those that a mesh axis runs over, the one named last changes fastest.
Arguments:
- panel: bfloat16 [24576, 1024], P('unit', 'week'), may hold values from -6 to 6
- start_week: int32 [24576], P('unit'), may hold values from 256 to 1024
- left_in: float32 [24576, 256], P('unit'), may hold values from -6 to 6
- right_in: float32 [256, 1024], P(None, 'week'), may hold values from -0.375 to 0.375
- sketch: bfloat16 [1024, 256], P('week'), may hold values from -0.1875 to 0.1875
Outputs:
- left_out: float32 [24576, 256], P('unit')
- estimate: bfloat16 [24576, 1024], P('unit', 'week')
All inputs are finite; a program needn't handle non-finite values.
Results may differ from a plain program's by a relative error of at most 0.0098.
Values may be sent and summed in bfloat16 or wider, within the bound.
No kernel may reach another device: no remote copies, remote signals or barrier semaphores. Data moves between devices by JAX's collectives and lax.ppermute only.
A program may use at most 64 MiB of HBM per device.

v0:
```python
import jax
import jax.numpy as jnp
from jax import lax
from jax.sharding import PartitionSpec as P


def right_solve(factor, values):
    return lax.linalg.triangular_solve(
        factor, values, left_side=False, lower=True, transpose_a=True
    )


def left_solve(factor, values):
    return lax.linalg.triangular_solve(factor, values, left_side=True, lower=True)


def chol_solve(factor, values):
    middle = lax.linalg.triangular_solve(factor, values, left_side=True, lower=True)
    return lax.linalg.triangular_solve(factor, middle, left_side=True, lower=True, transpose_a=True)


def on_device(panel, start_week, left_in, right_in, sketch):
    rows, cols = panel.shape
    rank = left_in.shape[1]
    offset = lax.axis_index("week") * cols
    weeks = offset + lax.broadcasted_iota(jnp.int32, (rows, cols), 1)
    observed = weeks < start_week[:, None]
    current = jnp.dot(
        left_in, right_in, precision=lax.Precision.HIGHEST, preferred_element_type=jnp.float32
    )
    filled = jnp.where(observed, panel.astype(jnp.float32), current).astype(jnp.bfloat16)
    partial_range = jnp.dot(filled, sketch, preferred_element_type=jnp.float32)
    ranged = lax.psum(partial_range, "week").astype(jnp.bfloat16)
    gram_part = lax.dot_general(
        ranged, ranged, (((0,), (0,)), ((), ())), preferred_element_type=jnp.float32
    )
    proj_part = lax.dot_general(
        ranged, filled, (((0,), (0,)), ((), ())), preferred_element_type=jnp.float32
    )
    gram, projected = lax.psum((gram_part, proj_part), "unit")
    factor = jnp.linalg.cholesky(gram)
    basis = right_solve(factor, ranged.astype(jnp.float32))
    coeffs = left_solve(factor, projected)
    collected = lax.all_gather(coeffs.astype(jnp.bfloat16), "week", axis=1, tiled=True).astype(
        coeffs.dtype
    )
    spectrum = jnp.dot(
        collected, collected.T, precision=lax.Precision.HIGHEST, preferred_element_type=jnp.float32
    )
    level = jnp.trace(spectrum) / rank
    shifted = jnp.linalg.cholesky(spectrum + level * jnp.eye(rank, dtype=jnp.float32))
    shrunk = coeffs - level * chol_solve(shifted, coeffs)
    total_units = rows * lax.axis_size("unit")
    left_out = basis * jnp.sqrt(jnp.float32(total_units))
    estimate = jnp.dot(
        basis, shrunk, precision=lax.Precision.HIGHEST, preferred_element_type=jnp.float32
    ).astype(jnp.bfloat16)
    return (left_out, estimate)


def solution(mesh):
    return jax.shard_map(
        on_device,
        mesh=mesh,
        in_specs=(P("unit", "week"), P("unit"), P("unit", None), P(None, "week"), P("week", None)),
        out_specs=(P("unit", None), P("unit", "week")),
        check_vma=False,
    )
```

profile of v0, /device:TPU:0, one launch (start us, length us, event | category | flops | bytes accessed | tf_op | source)
XLA Modules:
  0.0 304.5 jit_solution(14682188984229218693)
XLA Ops:
  8.6 4.4 %fusion = bf16[1536,512]{1,0:T(8,128)(2,1)S(1)} fusion(f32[1536,256]{1,0:T(8,128)S(1)} %copy-done, f32[256,512]{1,0:T(8,128)} %param.11, bf16[1536,512]{1,0:T(8,128)(2,1)} %param.8, s32[512]{0:T(512)S(1)} %iota_add_fusion, s32[1536]{0:T(1024)} %param.9), kind=kOutput, calls=%fused_computation.5 | convolution fusion | flops 2419064832 | bytes 5251072 | tf_op jit(solution)/shard_map/dot_general | solution.py:28
  14.1 1.7 fusion.33
  15.9 8.8 %all-reduce.6 = bf16[1536,256]{1,0:T(8,128)(2,1)S(1)} all-reduce(f32[1536,256]{1,0:T(8,128)} %fusion.33), channel_id=1, replica_groups=mesh['unit'=16,'week'=2] {'week'}, use_global_device_ids=true, to_apply=%region_0.1 | all-reduce | flops 393216 | bytes 2359296 | tf_op jit(solution)/shard_map/psum | solution.py:33
  24.6 2.8 fusion.35
  28.6 113.6 %all-reduce.5.cloned.1.call-done = (f32[256,256]{0,1:T(8,128)}, f32[256,512]{1,0:T(8,128)}) async-done(((f32[256,256]{0,1:T(8,128)}, f32[256,512]{1,0:T(8,128)}), (f32[256,256]{0,1:T(8,128)}, f32[256,512]{1,0:T(8,128)})) %all-reduce.5.cloned.1.call-update) | async-done | bytes 786448 | tf_op jit(solution)/shard_map/psum | solution.py:40
  144.3 11.7 %cholesky.130 = f32[128,128]{1,0:T(8,128)S(1)} custom-call(f32[128,128]{1,0:T(8,128)S(1)} %cholesky.194), custom_call_target="Cholesky" | custom-call | tf_op jit(solution)/shard_map/jit(cholesky)/cholesky | solution.py:41
  156.0 9.8 %custom-call.21 = f32[1,128,128]{1,2,0:T(8,128)S(1)} custom-call(f32[1,128,128]{2,1,0:T(8,128)S(1)} %get-tuple-element.79), custom_call_target="InvertDiagBlocksLowerTriangular" | custom-call | tf_op jit(solution)/shard_map/jit(cholesky)/cholesky | solution.py:41
  166.3 11.7 %cholesky.147 = f32[128,128]{1,0:T(8,128)S(1)} custom-call(f32[128,128]{1,0:T(8,128)S(1)} %convolution_subtract_fusion.5), custom_call_target="Cholesky" | custom-call | tf_op jit(solution)/shard_map/jit(cholesky)/cholesky | solution.py:41
  180.5 4.4 %while.6 = (s32[]{:T(128)}, f32[256,256]{0,1:T(8,128)S(1)}, s32[2,2]{1,0:T(2,128)S(1)}, f32[2,128,128]{2,1,0:T(8,128)S(1)}, s32[]{:T(128)}) while((s32[]{:T(128)}, f32[256,256]{0,1:T(8,128)S(1)}, s32[2,2]{1,0:T(2,128)S(1)}, f32[2,128,128]{2,1,0:T(8,128)S(1)}, s32[]{:T(128)}) %tuple.55), condition=%wide.while_cond.1, body=%wide.while_body.1.sunk | while | flops 2 | bytes 393321 | solution.py:8
  181.3 1.4 dynamic-slice.18
  183.4 1.4 dynamic-slice.18
  185.0 19.7 %custom-call.17 = f32[2,128,128]{1,2,0:T(8,128)S(1)} custom-call(f32[2,128,128]{2,1,0:T(8,128)S(1)} %get-tuple-element.19), custom_call_target="InvertDiagBlocksLowerTriangular" | custom-call | tf_op jit(solution)/shard_map/triangular_solve | solution.py:8
  206.7 2.2 all_gather.3
  210.7 11.7 %cholesky.164 = f32[128,128]{1,0:T(8,128)S(1)} custom-call(f32[128,128]{1,0:T(8,128)S(1)} %cholesky.197), custom_call_target="Cholesky" | custom-call | tf_op jit(solution)/shard_map/jit(cholesky)/cholesky | solution.py:51
  222.4 9.8 %custom-call.23 = f32[1,128,128]{1,2,0:T(8,128)S(1)} custom-call(f32[1,128,128]{2,1,0:T(8,128)S(1)} %get-tuple-element.77), custom_call_target="InvertDiagBlocksLowerTriangular" | custom-call | tf_op jit(solution)/shard_map/jit(cholesky)/cholesky | solution.py:51
  232.7 11.7 %cholesky.181 = f32[128,128]{1,0:T(8,128)S(1)} custom-call(f32[128,128]{1,0:T(8,128)S(1)} %convolution_subtract_fusion.4), custom_call_target="Cholesky" | custom-call | tf_op jit(solution)/shard_map/jit(cholesky)/cholesky | solution.py:51
  253.7 7.4 %while.7 = (s32[]{:T(128)}, f32[256,256]{0,1:T(8,128)}, s32[2,2]{1,0:T(2,128)S(1)}, f32[2,128,128]{2,1,0:T(8,128)}, s32[]{:T(128)}) while((s32[]{:T(128)}, f32[256,256]{0,1:T(8,128)}, s32[2,2]{1,0:T(2,128)S(1)}, f32[2,128,128]{2,1,0:T(8,128)}, s32[]{:T(128)}) %tuple.64), condition=%wide.while_cond.2, body=%wide.while_body.2.sunk | while | flops 2 | bytes 393829 | solution.py:19
  254.6 2.2 dynamic-slice.20
  258.2 2.2 dynamic-slice.20
  261.1 20.5 %custom-call.18 = f32[2,128,128]{1,2,0:T(8,128)S(1)} custom-call(f32[2,128,128]{2,1,0:T(8,128)} %get-tuple-element.27), custom_call_target="InvertDiagBlocksLowerTriangular" | custom-call | tf_op jit(solution)/shard_map/triangular_solve | solution.py:19
  282.1 1.4 convolution_subtract_fusion.2
  285.9 2.2 convolution_subtract_fusion
  290.4 3.8 %convolution_convert_fusion = bf16[1536,512]{1,0:T(8,128)(2,1)} fusion(f32[1536,128]{0,1:T(8,128)S(1)} %fusion.21, f32[1536,128]{0,1:T(8,128)S(1)} %fusion.7, f32[128,512]{1,0:T(8,128)S(1)} %fusion.25, f32[128,512]{1,0:T(8,128)S(1)} %fusion.23, f32[128,512]{1,0:T(8,128)S(1)} %copy-done.3, f32[128,512]{1,0:T(8,128)S(1)} %fusion.9, f32[]{:T(128)S(6)} %div.9), kind=kOutput, calls=%fused_computation.6 | convolution fusion | flops 2417623040 | bytes 4194308 | tf_op jit(solution)/shard_map/dot_general | solution.py:55
  294.2 3.0 copy.22
  (87 shorter events, 28.1 us)
Async XLA Ops:
  7.2 1.4 copy-start
  7.2 135.0 %all-reduce.5.cloned.1.call-start = ((), (), s32[]{:S(2)}) async-start(), calls=%async_computation | async-start | bytes 1572864 | tf_op jit(solution)/shard_map/psum | solution.py:40
  8.6 5.6 %copy-start.8 = (bf16[512,256]{1,0:T(8,128)(2,1)S(1)}, bf16[512,256]{1,0:T(8,128)(2,1)}, u32[]{:S(2)}) copy-start(bf16[512,256]{1,0:T(8,128)(2,1)} %param.12) | copy-start | bytes 786436
  13.0 1.1 copy-start.1
  180.3 24.3 %copy-start.7 = (f32[256,512]{1,0:T(8,128)S(1)}, f32[256,512]{1,0:T(8,128)}, u32[]{:S(2)}) copy-start(f32[256,512]{1,0:T(8,128)} %get-tuple-element.71) | copy-start | bytes 1572868
  185.0 21.8 %copy-start.4 = (f32[256,256]{0,1:T(8,128)}, f32[256,256]{0,1:T(8,128)S(1)}, u32[]{:S(2)}) copy-start(f32[256,256]{0,1:T(8,128)S(1)} %get-tuple-element.178) | copy-start | bytes 786436
  204.7 42.0 %copy-start.5 = (f32[2,128,128]{1,2,0:T(8,128)}, f32[2,128,128]{1,2,0:T(8,128)S(1)}, u32[]{:S(2)}) copy-start(f32[2,128,128]{1,2,0:T(8,128)S(1)} %custom-call.17) | copy-start | bytes 393220
  206.0 0.7 copy-start.2
  284.3 3.9 %copy-start.6 = (f32[2,128,128]{1,2,0:T(8,128)S(1)}, f32[2,128,128]{1,2,0:T(8,128)}, u32[]{:S(2)}) copy-start(f32[2,128,128]{1,2,0:T(8,128)} %copy-done.5) | copy-start | bytes 393220
  289.0 1.3 copy-start.3
Sparse Core Ops, SparseCore 0:
  28.7 113.4 all-reduce.4
where the time goes:
time: 308 us; the launch traced here: 305 us
  waiting for transfers between devices  114 us (37%)
  other arithmetic  112 us (36%)
  matrix products  24.9 us (8%)
  local copies, waits for them, and re-layouts  24.5 us (8%)
  between operations  18 us (6%)
  blocking collectives  11 us (4%)
    psum x1, waiting for transfers between devices, on_device(): gram, projected = lax.psum((gram_part, proj_part), 'unit')  114 us
    another operation x7, other arithmetic, on_device(): jnp.linalg.cholesky(spectrum + level * jnp.eye(rank, dtype=jnp.float32))  34.6 us
    another operation x6, other arithmetic, on_device(): factor = jnp.linalg.cholesky(gram)  34 us
    another operation x2, other arithmetic, chol_solve(): lax.linalg.triangular_solve(factor, middle, left_side=True, lower=True, t...  21.2 us
    another operation x3, other arithmetic, right_solve(): lax.linalg.triangular_solve(factor, values, left_side=False, lower=True,...  19.7 us
    another operation x20, local copies, waits for them, and re-layouts  11.3 us
    psum x1, blocking collectives, on_device(): ranged = lax.psum(partial_range, 'week').astype(jnp.bfloat16)  8.78 us
    unnamed x21, local copies, waits for them, and re-layouts  6.91 us
  transfers between devices with their start and end apart: 1, of which 1 were waited for; matrix products, arithmetic and copies ran while one was open for 0% of the time, Pallas kernels for 0%

commit v1 on v0

v1 whole, which is shorter than its diff:
```python
import functools

import jax
import jax.numpy as jnp
from jax import lax
from jax.experimental import pallas as pl
from jax.experimental.pallas import tpu as pltpu
from jax.sharding import PartitionSpec as P

f32 = jnp.float32
bf16 = jnp.bfloat16
LANES = 128
PANEL = 16
VMEM = pl.BlockSpec(memory_space=pltpu.VMEM)


def split2(x):
    high = x.astype(bf16)
    return high, (x - high.astype(f32)).astype(bf16)


def split3(x):
    high = x.astype(bf16)
    rest = x - high.astype(f32)
    mid = rest.astype(bf16)
    return high, mid, (rest - mid.astype(f32)).astype(bf16)


NN = (((1,), (0,)), ((), ()))
NT = (((1,), (1,)), ((), ()))
TN = (((0,), (0,)), ((), ()))


def dot(a, b, dims=NN):
    return lax.dot_general(a, b, dims, preferred_element_type=f32)


def dot3(a, b, dims=NN):
    ah, al = split2(a)
    bh, bl = split2(b)
    return dot(ah, bh, dims) + (dot(ah, bl, dims) + dot(al, bh, dims))


def dot6(a, b, dims=NN):
    ah, am, al = split3(a)
    bh, bm, bl = split3(b)
    small = dot(ah, bl, dims) + dot(al, bh, dims) + dot(am, bm, dims)
    return dot(ah, bh, dims) + (dot(ah, bm, dims) + dot(am, bh, dims) + small)


def front_body(panel, start, left, right, sketch, filled_out, range_out, right_hi, right_lo):
    block, cols = panel.shape

    @pl.when(pl.program_id(0) == 0)
    def _():
        hi, lo = split2(right[...])
        right_hi[...] = hi
        right_lo[...] = lo

    lh, ll = split2(left[...])
    current = dot(lh, right_hi[...]) + (dot(lh, right_lo[...]) + dot(ll, right_hi[...]))
    offset = lax.axis_index("week") * cols
    weeks = offset + lax.broadcasted_iota(jnp.int32, (LANES, cols), 1)
    tiles = []
    for t in range(block // LANES):
        row = start[0, t : t + 1, :].astype(f32)
        limit = jnp.broadcast_to(row, (LANES, LANES)).T.astype(jnp.int32)
        limit = jnp.concatenate([limit] * (cols // LANES), axis=1)
        span = slice(t * LANES, (t + 1) * LANES)
        tiles.append(
            jnp.where(weeks < limit, panel[span, :].astype(f32), current[span, :]).astype(bf16)
        )
    filled = jnp.concatenate(tiles, axis=0)
    filled_out[...] = filled
    range_out[...] = dot(filled, sketch[...]).astype(range_out.dtype)


def front(panel, start_week, left_in, right_in, sketch, range_type):
    rows, cols = panel.shape
    rank = left_in.shape[1]
    block = next(b for b in (256, 128) if rows % b == 0)
    per = block // LANES
    start = start_week.reshape(rows // block, per, LANES)
    return pl.pallas_call(
        front_body,
        grid=(rows // block,),
        in_specs=[
            pl.BlockSpec((block, cols), lambda i: (i, 0)),
            pl.BlockSpec((1, per, LANES), lambda i: (i, 0, 0)),
            pl.BlockSpec((block, rank), lambda i: (i, 0)),
            pl.BlockSpec((rank, cols), lambda i: (0, 0)),
            pl.BlockSpec((cols, rank), lambda i: (0, 0)),
        ],
        out_specs=[
            pl.BlockSpec((block, cols), lambda i: (i, 0)),
            pl.BlockSpec((block, rank), lambda i: (i, 0)),
        ],
        out_shape=[
            jax.ShapeDtypeStruct((rows, cols), bf16),
            jax.ShapeDtypeStruct((rows, rank), range_type),
        ],
        scratch_shapes=[pltpu.VMEM((rank, cols), bf16), pltpu.VMEM((rank, cols), bf16)],
        name="front",
    )(panel, start, left_in, right_in, sketch)


def digits_of(size):
    radices, stride = [], 1
    while stride < size:
        radix = 4 if (size // stride) % 4 == 0 else 2
        radices.append((stride, radix))
        stride *= radix
    return radices


def exchange(value, stride, radix, step, size):
    def partner(u):
        digit = (u // stride) % radix
        return u + ((digit ^ step) - digit) * stride

    return lax.ppermute(value, "unit", [(u, partner(u)) for u in range(size)])


def unpack(piece, half):
    gram = piece[:, :half].astype(f32) + piece[:, half : 2 * half].astype(f32)
    return gram, piece[:, 2 * half :].astype(f32)


def pack(gram, projected):
    hi, lo = split2(gram)
    return jnp.concatenate([hi, lo, projected.astype(bf16)], axis=1)


def sum_pieces(pieces, half):
    gram, projected = unpack(pieces[0][...], half)
    for piece in pieces[1:]:
        g, p = unpack(piece[...], half)
        gram, projected = gram + g, projected + p
    return pack(gram, projected)


def scatter_rows(packed, outs, stride, radix, scratch):
    digit = (lax.axis_index("unit") // stride) % radix
    length = packed.shape[0] // radix
    scratch[...] = packed
    for step, out in enumerate(outs):
        at = pl.multiple_of((digit ^ step) * length, length)
        out[...] = scratch[pl.ds(at, length), :]


def gather_rows(pieces, stride, radix, scratch):
    digit = (lax.axis_index("unit") // stride) % radix
    length = pieces[0].shape[0]
    for step, piece in enumerate(pieces):
        at = pl.multiple_of((digit ^ step) * length, length)
        scratch[pl.ds(at, length), :] = piece[...]


def moments_body(stride, radix, half, *refs):
    mine, other, filled, ranged_out, *rest = refs
    outs, scratch = rest[:radix], rest[radix]
    ranged = (mine[...].astype(f32) + other[...].astype(f32)).astype(bf16)
    ranged_out[...] = ranged
    week = lax.axis_index("week")
    share = jnp.where(week == 0, ranged[:, :half], ranged[:, half:])
    gram = dot(ranged, share, TN)
    projected = dot(ranged, filled[...], TN)
    scatter_rows(pack(gram, projected), outs, stride, radix, scratch)


def reduce_body(count, stride, radix, half, *refs):
    pieces, outs, scratch = refs[:count], refs[count : count + radix], refs[count + radix]
    scatter_rows(sum_pieces(pieces, half), outs, stride, radix, scratch)


def last_reduce_body(count, half, *refs):
    refs[count][...] = sum_pieces(refs[:count], half)


def join_body(count, stride, radix, *refs):
    gather_rows(refs[:count], stride, radix, refs[count])


def last_join_body(count, stride, radix, half, *refs):
    pieces, (gram_out, projected_out, outer_out, scratch) = refs[:count], refs[count:]
    gather_rows(pieces, stride, radix, scratch)
    packed = scratch[...]
    gram_out[...] = packed[:, :half].astype(f32) + packed[:, half : 2 * half].astype(f32)
    projected = packed[:, 2 * half :]
    projected_out[...] = projected
    outer_out[...] = dot(projected, projected, NT)


def call(body, ins, outs, name, scratch=()):
    return pl.pallas_call(
        body,
        in_specs=[VMEM] * len(ins),
        out_specs=[VMEM] * len(outs),
        out_shape=[jax.ShapeDtypeStruct(shape, kind) for shape, kind in outs],
        scratch_shapes=[pltpu.VMEM(shape, kind) for shape, kind in scratch],
        name=name,
    )(*ins)


def sums_by_exchange(part, filled, units):
    rows, cols = filled.shape
    rank = part.shape[1]
    half = rank // 2
    width = 2 * half + cols
    swap = [(0, 1), (1, 0)]
    digits = digits_of(units)
    other = lax.ppermute(part, "week", swap)
    stride, radix = digits[0]
    length = rank // radix
    ranged, *pieces = call(
        functools.partial(moments_body, stride, radix, half),
        (part, other, filled),
        [((rows, rank), bf16)] + [((length, width), bf16)] * radix,
        "moments",
        [((rank, width), bf16)],
    )
    for at, (stride, radix) in enumerate(digits):
        pieces = [pieces[0]] + [
            exchange(pieces[step], stride, radix, step, units) for step in range(1, radix)
        ]
        if at + 1 < len(digits):
            stride2, radix2 = digits[at + 1]
            shorter = length // radix2
            pieces = call(
                functools.partial(reduce_body, radix, stride2, radix2, half),
                pieces,
                [((shorter, width), bf16)] * radix2,
                f"reduce{at}",
                [((length, width), bf16)],
            )
            length = shorter
        else:
            (packed,) = call(
                functools.partial(last_reduce_body, radix, half),
                pieces,
                [((length, width), bf16)],
                f"reduce{at}",
            )
    for stride, radix in reversed(digits):
        pieces = [packed] + [
            exchange(packed, stride, radix, step, units) for step in range(1, radix)
        ]
        if length * radix < rank:
            (packed,) = call(
                functools.partial(join_body, radix, stride, radix),
                pieces,
                [((length * radix, width), bf16)],
                "join",
            )
            length *= radix
    gram, projected, outer = call(
        functools.partial(last_join_body, radix, stride, radix, half),
        pieces,
        [((rank, half), f32), ((rank, cols), bf16), ((rank, rank), f32)],
        "last_join",
        [((rank, width), bf16)],
    )
    gram_other = lax.ppermute(gram, "week", swap)
    outer_other = lax.ppermute(outer, "week", swap)
    return ranged, (gram, gram_other), projected, (outer, outer_other)


def sums_by_psum(part, filled):
    ranged = lax.psum(part, "week").astype(bf16)
    gram_part = dot(ranged, ranged, TN)
    projected_part = dot(ranged, filled, TN)
    gram, projected = lax.psum((gram_part, projected_part), "unit")
    projected = projected.astype(bf16)
    outer = lax.psum(dot(projected, projected, NT), "week")
    return ranged, (gram,), projected, (outer,)


def inverse_factor_body(*refs):
    *grams, out, work = refs
    n = out.shape[0]
    tiles = n // LANES
    sub = lax.broadcasted_iota(jnp.int32, (8, LANES), 0)
    if len(grams) == 1:
        work[:, :n] = grams[0][...]
    else:
        mine, other = grams
        week = lax.axis_index("week")
        a, b = mine[...], other[...]
        work[:, : n // 2] = jnp.where(week == 0, a, b)
        work[:, n // 2 : n] = jnp.where(week == 0, b, a)
    square = (n, n)
    same = lax.broadcasted_iota(jnp.int32, square, 0) == lax.broadcasted_iota(jnp.int32, square, 1)
    work[:, n:] = jnp.where(same, 1.0, 0.0).astype(f32)
    out[...] = jnp.zeros(square, f32)
    parts = PANEL // 8
    for r0 in range(0, n, PANEL):
        r1 = r0 + PANEL
        first = r0 // LANES
        places = list(range(first, tiles)) + [tiles + k for k in range(first + 1)]
        rows = [
            [work[r0 + 8 * t : r0 + 8 * t + 8, LANES * p : LANES * (p + 1)] for p in places]
            for t in range(parts)
        ]
        at = r0 - first * LANES
        pivots = [
            [jnp.broadcast_to(rows[t][0][:, at + j : at + j + 1], (8, LANES)) for t in range(parts)]
            for j in range(PANEL)
        ]
        for j in range(PANEL):
            tj, sj = divmod(j, 8)
            scale = lax.rsqrt(jnp.broadcast_to(pivots[j][tj][sj : sj + 1, :], (8, LANES)))
            times = {}
            for t in range(tj, parts):
                value = pivots[j][t] * scale
                times[t] = jnp.where(sub > sj, value, 0.0) if t == tj else value
            for k in range(j + 1, PANEL):
                line = jnp.broadcast_to(pivots[k][tj][sj : sj + 1, :], (8, LANES)) * scale
                for t in range(tj, parts):
                    if t > tj or sj < 7:
                        pivots[k][t] = pivots[k][t] - times[t] * line
            for p in range(len(places)):
                line = jnp.broadcast_to(rows[tj][p][sj : sj + 1, :], (8, LANES)) * scale
                for t in range(tj, parts):
                    updated = rows[t][p] - times[t] * line
                    rows[t][p] = jnp.where(sub == sj, line, updated) if t == tj else updated
        done = jnp.concatenate([jnp.concatenate(r, axis=1) for r in rows], axis=0)
        ahead = tiles - first
        for k in range(first + 1):
            out[r0:r1, LANES * k : LANES * (k + 1)] = done[
                :, LANES * (ahead + k) : LANES * (ahead + k + 1)
            ]
        if r1 < n:
            nxt = r1 // LANES
            hi, mid, lo = split3(done)
            skip = (nxt - first) * LANES
            lhs = jnp.concatenate([hi, hi, mid, mid, hi, lo], axis=0)[:, skip : LANES * ahead]
            rhs = jnp.concatenate([hi, mid, hi, mid, lo, hi], axis=0)[:, skip:]
            change = dot(lhs, rhs, TN)
            top = r1 - nxt * LANES
            wide = LANES * (tiles - nxt)
            end = n + LANES * (first + 1)
            work[r1:, LANES * nxt : n] = work[r1:, LANES * nxt : n] - change[top:, :wide]
            work[r1:, n:end] = work[r1:, n:end] - change[top:, wide:]


def shrink_map(inverse, outer, projected):
    n = inverse.shape[0]
    spectrum = dot6(dot6(inverse, outer), inverse, NT)
    square = (n, n)
    same = lax.broadcasted_iota(jnp.int32, square, 0) == lax.broadcasted_iota(jnp.int32, square, 1)
    trace = jnp.sum(jnp.where(same, spectrum, 0.0), axis=1, keepdims=True)
    level = jnp.sum(trace, axis=0, keepdims=True) / n
    low, high = 1.0, n + 1.0
    top = (high + low) / (high - low)
    eye = jnp.where(same, 1.0, 0.0).astype(f32)
    residual = eye - (eye + spectrum / level) * (2.0 / (high + low))
    solve = None
    while True:
        gain = 2.0 * top * top / (2.0 * top * top - 1.0)
        if solve is None:
            solve = (eye + residual) * (gain * 2.0 / (high + low))
        else:
            solve = gain * (solve + dot3(solve, residual))
        if 2.0 * top * top - 1.0 > 1.0e6:
            break
        residual = gain * dot3(residual, residual) - eye * (1.0 / (2.0 * top * top - 1.0))
        top = 2.0 * top * top - 1.0
    kept = inverse - dot3(solve, inverse)
    kh, kl = split2(kept)
    middle = dot(kh, projected) + dot(kl, projected)
    return dot3(inverse, middle, TN)


def final_body(count, total, *refs):
    inverse, *rest = refs
    outers, rest = rest[:count], rest[count:]
    projected, ranged, left_out, estimate, basis_hi, basis_lo, map_hi, map_lo = rest

    @pl.when(pl.program_id(0) == 0)
    def _():
        scaled = inverse[...] * jnp.sqrt(f32(total))
        basis_hi[...], basis_lo[...] = split2(scaled)
        outer = outers[0][...]
        if count == 2:
            outer = outer + outers[1][...]
        map_hi[...], map_lo[...] = split2(shrink_map(inverse[...], outer, projected[...]))

    rows = ranged[...]
    left_out[...] = dot(rows, basis_hi[...], NT) + dot(rows, basis_lo[...], NT)
    estimate[...] = (dot(rows, map_hi[...]) + dot(rows, map_lo[...])).astype(bf16)


def final(inverse, outers, projected, ranged, total):
    rows, rank = ranged.shape
    cols = projected.shape[1]
    block = next(b for b in (256, 128) if rows % b == 0)
    count = len(outers)
    whole = lambda i: (0, 0)
    return pl.pallas_call(
        functools.partial(final_body, count, total),
        grid=(rows // block,),
        in_specs=[pl.BlockSpec((rank, rank), whole)] * (1 + count)
        + [pl.BlockSpec((rank, cols), whole), pl.BlockSpec((block, rank), lambda i: (i, 0))],
        out_specs=[
            pl.BlockSpec((block, rank), lambda i: (i, 0)),
            pl.BlockSpec((block, cols), lambda i: (i, 0)),
        ],
        out_shape=[
            jax.ShapeDtypeStruct((rows, rank), f32),
            jax.ShapeDtypeStruct((rows, cols), bf16),
        ],
        scratch_shapes=[
            pltpu.VMEM((rank, rank), bf16),
            pltpu.VMEM((rank, rank), bf16),
            pltpu.VMEM((rank, cols), bf16),
            pltpu.VMEM((rank, cols), bf16),
        ],
        name="final",
    )(inverse, *outers, projected, ranged)


def on_device(panel, start_week, left_in, right_in, sketch):
    rows = panel.shape[0]
    rank = left_in.shape[1]
    units, weeks = lax.axis_size("unit"), lax.axis_size("week")
    small = weeks == 2 and units & (units - 1) == 0 and rank // units >= 16
    filled, part = front(panel, start_week, left_in, right_in, sketch, bf16 if small else f32)
    if small:
        sums = sums_by_exchange(part, filled, units)
    else:
        sums = sums_by_psum(part, filled)
    ranged, grams, projected, outers = sums
    (inverse,) = call(
        inverse_factor_body, grams, [((rank, rank), f32)], "factor", [((rank, 2 * rank), f32)]
    )
    return tuple(final(inverse, outers, projected, ranged, rows * units))


def solution(mesh):
    return jax.shard_map(
        on_device,
        mesh=mesh,
        in_specs=(P("unit", "week"), P("unit"), P("unit", None), P(None, "week"), P("week", None)),
        out_specs=(P("unit", None), P("unit", "week")),
        check_vma=False,
    )
```

time: 308 us -> 82.3 us (0.27)
  other arithmetic: 112 us -> 0 us
  waiting for transfers between devices: 114 us -> 20.6 us
  Pallas kernels: 0 us -> 36.4 us
  matrix products: 24.9 us -> 0 us
  local copies, waits for them, and re-layouts: 24.5 us -> 6.38 us
  starting transfers between devices: 0.04 us -> 17.6 us
  between operations: 18 us -> 0.67 us
  blocking collectives: 11 us -> 0 us
    psum x1 -> x0, waiting for transfers between devices: 114 us -> none  [on_device(): gram, projected = lax.psum((gram_part, proj_part), 'unit')]
    another operation x18 -> x0, other arithmetic: 110 us -> none  [the longest x7 34.6 us: on_device(): jnp.linalg.cholesky(spectrum + level * jnp.eye(rank, dtype=jnp.float32))]
    pallas_call x0 -> x8, Pallas kernels: none -> 36.4 us  [the longest x6 19.4 us: call(): pl.pallas_call(body, in_specs=[VMEM] * len(ins), out_specs=[VMEM] * len(o...]
    ppermute x0 -> x15, waiting for transfers between devices: none -> 20.6 us  [the longest x12 17 us: exchange(): return lax.ppermute(value, 'unit', [(u, partner(u)) for u in range(size)])]
    ppermute x0 -> x15, starting transfers between devices: none -> 17.6 us  [the longest x12 16.6 us: exchange(): return lax.ppermute(value, 'unit', [(u, partner(u)) for u in range(size)])]
    another operation x35 -> x0, local copies, waits for them, and re-layouts: 16.4 us -> none
    dot_general x6 -> x0, matrix products: 14.8 us -> none  [the longest x1 4.41 us: on_device(): jnp.dot(left_in, right_in, precision=lax.Precision.HIGHEST, preferred_ele...]
    another operation x16 -> x0, matrix products: 10 us -> none  [the longest x3 3.61 us: right_solve(): lax.linalg.triangular_solve(factor, values, left_side=False, lower=True,...]
  transfers between devices with their start and end apart: 1 -> 15, of which waited for: 1 -> 12; matrix products, arithmetic and copies ran while one was open for 0% -> 0% of each run, Pallas kernels for 0% -> 11%
where the time goes in v1:
time: 82.3 us; the launch traced here: 81.7 us
  Pallas kernels  36.4 us (44%)
  waiting for transfers between devices  20.6 us (25%)
  starting transfers between devices  17.6 us (21%)
  local copies, waits for them, and re-layouts  6.38 us (8%)
    pallas_call x6, Pallas kernels, call(): pl.pallas_call(body, in_specs=[VMEM] * len(ins), out_specs=[VMEM] * len(o...  19.4 us
    ppermute x12, waiting for transfers between devices, exchange(): return lax.ppermute(value, 'unit', [(u, partner(u)) for u in range(size)])  17 us
    ppermute x12, starting transfers between devices, exchange(): return lax.ppermute(value, 'unit', [(u, partner(u)) for u in range(size)])  16.6 us
    pallas_call x1, Pallas kernels, final(): pl.pallas_call(functools.partial(final_body, count, total), grid=(rows //...  10.4 us
    pallas_call x1, Pallas kernels, front(): pl.pallas_call(front_body, grid=(rows // block,), in_specs=[pl.BlockSpec(...  6.6 us
    unnamed x30, local copies, waits for them, and re-layouts  5.08 us
    ppermute x1, waiting for transfers between devices, sums_by_exchange(): other = lax.ppermute(part, 'week', swap)  2.12 us
  transfers between devices with their start and end apart: 15, of which 12 were waited for; matrix products, arithmetic and copies ran while one was open for 0% of the time, Pallas kernels for 11%

profile of v1, /device:TPU:0, one launch (start us, length us, event | category | flops | bytes accessed | tf_op | source)
XLA Modules:
  0.0 81.7 jit_solution(10151696695706137076)
XLA Ops:
  0.6 1.3 %reshape.7.start = s32[6,2,128]{2,1,0:T(2,128)} reshape(s32[1536]{0:T(1024)} %param.6) | data formatting | bytes 12288 | tf_op jit(solution)/shard_map/reshape | solution.py:83
  1.9 6.6 %front.1 = (bf16[1536,512]{1,0:T(8,128)(2,1)}, bf16[1536,256]{1,0:T(8,128)(2,1)}) custom-call(bf16[1536,512]{1,0:T(8,128)(2,1)} %panel.1, s32[6,2,128]{2,1,0:T(2,128)} %reshape.7.start, f32[1536,256]{1,0:T(8,128)} %left.1, f32[256,512]{1,0:T(8,128)} %right.1, bf16[512,256]{1,0:T(8,128)(2,1)} %sketch.1), custom_call_target="tpu_custom_call" | custom-call | tf_op jit(solution)/shard_map/front/pallas_call | solution.py:84
  9.0 2.1 %collective-permute-done.refs_1_ = bf16[1536,256]{1,0:T(8,128)(2,1)S(1)} collective-permute-done((bf16[1536,256]{1,0:T(8,128)(2,1)}, bf16[1536,256]{1,0:T(8,128)(2,1)S(1)}, u32[]{:S(2)}, u32[]{:S(2)}) %collective-permute-start) | collective-permute-done | bytes 786464 | tf_op jit(solution)/shard_map/ppermute | solution.py:212
  12.1 3.5 %moments.1 = (bf16[1536,256]{1,0:T(8,128)(2,1)}, bf16[64,768]{1,0:T(8,128)(2,1)}, bf16[64,768]{1,0:T(8,128)(2,1)}, bf16[64,768]{1,0:T(8,128)(2,1)}, bf16[64,768]{1,0:T(8,128)(2,1)}) custom-call(bf16[1536,256]{1,0:T(8,128)(2,1)} %get-tuple-element.16.refs_0_, bf16[1536,256]{1,0:T(8,128)(2,1)} %copy-done, bf16[1536,512]{1,0:T(8,128)(2,1)} %get-tuple-element.17.refs_2_), custom_call_target="tpu_custom_call" | custom-call | tf_op jit(solution)/shard_map/moments/pallas_call | solution.py:195
  15.6 2.9 %collective-permute-start.1 = (bf16[64,768]{1,0:T(8,128)(2,1)}, bf16[64,768]{1,0:T(8,128)(2,1)S(1)}, u32[]{:S(2)}, u32[]{:S(2)}) collective-permute-start(bf16[64,768]{1,0:T(8,128)(2,1)} %get-tuple-element.19), channel_id=1, source_target_pairs={{0,2},{2,0},{4,6},{6,4},{8,10},{10,8},{12,14},{14,12},{16,18},{18,... | collective-permute-start | bytes 294920 | tf_op jit(solution)/shard_map/ppermute | solution.py:121
  18.5 1.5 %collective-permute-start.2 = (bf16[64,768]{1,0:T(8,128)(2,1)}, bf16[64,768]{1,0:T(8,128)(2,1)S(1)}, u32[]{:S(2)}, u32[]{:S(2)}) collective-permute-start(bf16[64,768]{1,0:T(8,128)(2,1)} %get-tuple-element.20), channel_id=1, source_target_pairs={{0,4},{2,6},{4,0},{6,2},{8,12},{10,14},{12,8},{14,10},{16,20},{18,... | collective-permute-start | bytes 294920 | tf_op jit(solution)/shard_map/ppermute | solution.py:121
  20.0 2.0 %collective-permute-done.1.refs_1_ = bf16[64,768]{1,0:T(8,128)(2,1)S(1)} collective-permute-done((bf16[64,768]{1,0:T(8,128)(2,1)}, bf16[64,768]{1,0:T(8,128)(2,1)S(1)}, u32[]{:S(2)}, u32[]{:S(2)}) %collective-permute-start.1) | collective-permute-done | bytes 98336 | tf_op jit(solution)/shard_map/ppermute | solution.py:121
  22.0 2.6 %collective-permute-done.2.refs_2_ = bf16[64,768]{1,0:T(8,128)(2,1)S(1)} collective-permute-done((bf16[64,768]{1,0:T(8,128)(2,1)}, bf16[64,768]{1,0:T(8,128)(2,1)S(1)}, u32[]{:S(2)}, u32[]{:S(2)}) %collective-permute-start.2) | collective-permute-done | bytes 98336 | tf_op jit(solution)/shard_map/ppermute | solution.py:121
  24.5 1.2 %collective-permute-done.3.refs_3_ = bf16[64,768]{1,0:T(8,128)(2,1)S(1)} collective-permute-done((bf16[64,768]{1,0:T(8,128)(2,1)}, bf16[64,768]{1,0:T(8,128)(2,1)S(1)}, u32[]{:S(2)}, u32[]{:S(2)}) %collective-permute-start.3) | collective-permute-done | bytes 98336 | tf_op jit(solution)/shard_map/ppermute | solution.py:121
  26.3 1.7 %reduce0.1 = (bf16[16,768]{1,0:T(8,128)(2,1)}, bf16[16,768]{1,0:T(8,128)(2,1)}, bf16[16,768]{1,0:T(8,128)(2,1)}, bf16[16,768]{1,0:T(8,128)(2,1)}) custom-call(bf16[64,768]{1,0:T(8,128)(2,1)} %get-tuple-element.18.refs_0_, bf16[64,768]{1,0:T(8,128)(2,1)} %copy-done.3, bf16[64,768]{1,0:T(8,128)(2,1)} %copy-done.4, bf16[64,768]{1,0:T(8,128)(2,1)} %copy-done.6), custom_call_target="tpu_custom_call" | custom-call | tf_op jit(solution)/shard_map/reduce0/pallas_call | solution.py:195
  28.1 1.6 %collective-permute-start.4 = (bf16[16,768]{1,0:T(8,128)(2,1)}, bf16[16,768]{1,0:T(8,128)(2,1)S(1)}, u32[]{:S(2)}, u32[]{:S(2)}) collective-permute-start(bf16[16,768]{1,0:T(8,128)(2,1)} %get-tuple-element.23), channel_id=1, source_target_pairs={{0,8},{2,10},{4,12},{6,14},{8,0},{10,2},{12,4},{14,6},{16,24},{18,... | collective-permute-start | bytes 73736 | tf_op jit(solution)/shard_map/ppermute | solution.py:121
  29.6 2.6 %collective-permute-start.5 = (bf16[16,768]{1,0:T(8,128)(2,1)}, bf16[16,768]{1,0:T(8,128)(2,1)S(1)}, u32[]{:S(2)}, u32[]{:S(2)}) collective-permute-start(bf16[16,768]{1,0:T(8,128)(2,1)} %get-tuple-element.24), channel_id=1, source_target_pairs={{0,16},{2,18},{4,20},{6,22},{8,24},{10,26},{12,28},{14,30},{16,0},... | collective-permute-start | bytes 73736 | tf_op jit(solution)/shard_map/ppermute | solution.py:121
  32.5 2.3 %collective-permute-done.5.refs_2_ = bf16[16,768]{1,0:T(8,128)(2,1)S(1)} collective-permute-done((bf16[16,768]{1,0:T(8,128)(2,1)}, bf16[16,768]{1,0:T(8,128)(2,1)S(1)}, u32[]{:S(2)}, u32[]{:S(2)}) %collective-permute-start.5) | collective-permute-done | bytes 24608 | tf_op jit(solution)/shard_map/ppermute | solution.py:121
  34.7 3.3 %collective-permute-done.6.refs_3_ = bf16[16,768]{1,0:T(8,128)(2,1)S(1)} collective-permute-done((bf16[16,768]{1,0:T(8,128)(2,1)}, bf16[16,768]{1,0:T(8,128)(2,1)S(1)}, u32[]{:S(2)}, u32[]{:S(2)}) %collective-permute-start.6) | collective-permute-done | bytes 24608 | tf_op jit(solution)/shard_map/ppermute | solution.py:121
  38.7 1.4 %reduce1.1.refs_0_ = bf16[16,768]{1,0:T(8,128)(2,1)} custom-call(bf16[16,768]{1,0:T(8,128)(2,1)} %get-tuple-element.22.refs_0_, bf16[16,768]{1,0:T(8,128)(2,1)} %copy-done.12, bf16[16,768]{1,0:T(8,128)(2,1)} %copy-done.13, bf16[16,768]{1,0:T(8,128)(2,1)} %copy-done.14), custom_call_target="tpu_custom_call" | custom-call | tf_op jit(solution)/shard_map/reduce1/pallas_call | solution.py:195
  40.4 4.1 %collective-permute-start.7 = (bf16[16,768]{1,0:T(8,128)(2,1)}, bf16[16,768]{1,0:T(8,128)(2,1)S(1)}, u32[]{:S(2)}, u32[]{:S(2)}) collective-permute-start(bf16[16,768]{1,0:T(8,128)(2,1)} %reduce1.1.refs_0_), channel_id=1, source_target_pairs={{0,8},{2,10},{4,12},{6,14},{8,0},{10,2},{12,4},{14,6},{16,24},{18,... | collective-permute-start | bytes 73736 | tf_op jit(solution)/shard_map/ppermute | solution.py:121
  44.5 1.4 %collective-permute-done.9.refs_3_ = bf16[16,768]{1,0:T(8,128)(2,1)S(1)} collective-permute-done((bf16[16,768]{1,0:T(8,128)(2,1)}, bf16[16,768]{1,0:T(8,128)(2,1)S(1)}, u32[]{:S(2)}, u32[]{:S(2)}) %collective-permute-start.9) | collective-permute-done | bytes 24608 | tf_op jit(solution)/shard_map/ppermute | solution.py:121
  47.1 1.4 %join.1.refs_0_ = bf16[64,768]{1,0:T(8,128)(2,1)} custom-call(bf16[16,768]{1,0:T(8,128)(2,1)} %reduce1.1.refs_0_, bf16[16,768]{1,0:T(8,128)(2,1)} %copy-done.11, bf16[16,768]{1,0:T(8,128)(2,1)} %copy-done.10, bf16[16,768]{1,0:T(8,128)(2,1)} %copy-done.9), custom_call_target="tpu_custom_call" | custom-call | tf_op jit(solution)/shard_map/join/pallas_call | solution.py:195
  48.6 1.2 %collective-permute-start.12 = (bf16[64,768]{1,0:T(8,128)(2,1)}, bf16[64,768]{1,0:T(8,128)(2,1)S(1)}, u32[]{:S(2)}, u32[]{:S(2)}) collective-permute-start(bf16[64,768]{1,0:T(8,128)(2,1)} %join.1.refs_0_), channel_id=1, source_target_pairs={{0,6},{2,4},{4,2},{6,0},{8,14},{10,12},{12,10},{14,8},{16,22},{18,... | collective-permute-start | bytes 294920 | tf_op jit(solution)/shard_map/ppermute | solution.py:121
  52.1 2.3 %collective-permute-done.12.refs_3_ = bf16[64,768]{1,0:T(8,128)(2,1)S(1)} collective-permute-done((bf16[64,768]{1,0:T(8,128)(2,1)}, bf16[64,768]{1,0:T(8,128)(2,1)S(1)}, u32[]{:S(2)}, u32[]{:S(2)}) %collective-permute-start.12) | collective-permute-done | bytes 98336 | tf_op jit(solution)/shard_map/ppermute | solution.py:121
  56.6 2.0 %last_join.1 = (f32[256,128]{1,0:T(8,128)}, bf16[256,512]{1,0:T(8,128)(2,1)}, f32[256,256]{1,0:T(8,128)}) custom-call(bf16[64,768]{1,0:T(8,128)(2,1)} %join.1.refs_0_, bf16[64,768]{1,0:T(8,128)(2,1)} %copy-done.8, bf16[64,768]{1,0:T(8,128)(2,1)} %copy-done.7, bf16[64,768]{1,0:T(8,128)(2,1)} %copy-done.5), custom_call_target="tpu_custom_call" | custom-call | tf_op jit(solution)/shard_map/last_join/pallas_call | solution.py:195
  59.2 1.4 %collective-permute-done.13.refs_1_ = f32[256,128]{1,0:T(8,128)S(1)} collective-permute-done((f32[256,128]{1,0:T(8,128)}, f32[256,128]{1,0:T(8,128)S(1)}, u32[]{:S(2)}, u32[]{:S(2)}) %collective-permute-start.13) | collective-permute-done | bytes 131104 | tf_op jit(solution)/shard_map/ppermute | solution.py:263
  61.3 9.3 %factor.1.refs_0_ = f32[256,256]{1,0:T(8,128)} custom-call(f32[256,128]{1,0:T(8,128)} %get-tuple-element.26.refs_0_, f32[256,128]{1,0:T(8,128)} %copy-done.2), custom_call_target="tpu_custom_call" | custom-call | tf_op jit(solution)/shard_map/factor/pallas_call | solution.py:195
  71.3 10.4 %final.1 = (f32[1536,256]{1,0:T(8,128)}, bf16[1536,512]{1,0:T(8,128)(2,1)}) custom-call(f32[256,256]{1,0:T(8,128)} %factor.1.refs_0_, f32[256,256]{1,0:T(8,128)} %get-tuple-element.27.refs_1_, f32[256,256]{1,0:T(8,128)} %copy-done.1, bf16[256,512]{1,0:T(8,128)(2,1)} %get-tuple-element.28.refs_3_, bf16[1536,256]{1,0:T(8,128)(2,1)} %get-tuple-element.29.refs_4_), custom_call_target="tpu_custom_call" | custom-call | tf_op jit(solution)/shard_map/final/pallas_call | solution.py:399
  (45 shorter events, 10.8 us)
Async XLA Ops:
  8.5 2.6 %collective-permute-start = (bf16[1536,256]{1,0:T(8,128)(2,1)}, bf16[1536,256]{1,0:T(8,128)(2,1)S(1)}, u32[]{:S(2)}, u32[]{:S(2)}) collective-permute-start(bf16[1536,256]{1,0:T(8,128)(2,1)} %get-tuple-element.16.refs_0_), channel_id=1, source_target_pairs={{0,1},{1,0},{2,3},{3,2},{4,5},{5,4},{6,7},{7,6},{8,9},{9,8},{10,11... | collective-permute-start | bytes 2359304 | tf_op jit(solution)/shard_map/ppermute | solution.py:212
  11.1 0.9 %copy-start = (bf16[1536,256]{1,0:T(8,128)(2,1)}, bf16[1536,256]{1,0:T(8,128)(2,1)S(1)}, u32[]{:S(2)}) copy-start(bf16[1536,256]{1,0:T(8,128)(2,1)S(1)} %collective-permute-done.refs_1_) | copy-start | bytes 2359300
  15.6 6.4 %collective-permute-start.1 = (bf16[64,768]{1,0:T(8,128)(2,1)}, bf16[64,768]{1,0:T(8,128)(2,1)S(1)}, u32[]{:S(2)}, u32[]{:S(2)}) collective-permute-start(bf16[64,768]{1,0:T(8,128)(2,1)} %get-tuple-element.19), channel_id=1, source_target_pairs={{0,2},{2,0},{4,6},{6,4},{8,10},{10,8},{12,14},{14,12},{16,18},{18,... | collective-permute-start | bytes 294920 | tf_op jit(solution)/shard_map/ppermute | solution.py:121
  18.5 6.1 %collective-permute-start.2 = (bf16[64,768]{1,0:T(8,128)(2,1)}, bf16[64,768]{1,0:T(8,128)(2,1)S(1)}, u32[]{:S(2)}, u32[]{:S(2)}) collective-permute-start(bf16[64,768]{1,0:T(8,128)(2,1)} %get-tuple-element.20), channel_id=1, source_target_pairs={{0,4},{2,6},{4,0},{6,2},{8,12},{10,14},{12,8},{14,10},{16,20},{18,... | collective-permute-start | bytes 294920 | tf_op jit(solution)/shard_map/ppermute | solution.py:121
  20.0 5.7 %collective-permute-start.3 = (bf16[64,768]{1,0:T(8,128)(2,1)}, bf16[64,768]{1,0:T(8,128)(2,1)S(1)}, u32[]{:S(2)}, u32[]{:S(2)}) collective-permute-start(bf16[64,768]{1,0:T(8,128)(2,1)} %get-tuple-element.21), channel_id=1, source_target_pairs={{0,6},{2,4},{4,2},{6,0},{8,14},{10,12},{12,10},{14,8},{16,22},{18,... | collective-permute-start | bytes 294920 | tf_op jit(solution)/shard_map/ppermute | solution.py:121
  22.0 3.7 %copy-start.3 = (bf16[64,768]{1,0:T(8,128)(2,1)}, bf16[64,768]{1,0:T(8,128)(2,1)S(1)}, u32[]{:S(2)}) copy-start(bf16[64,768]{1,0:T(8,128)(2,1)S(1)} %collective-permute-done.1.refs_1_) | copy-start | bytes 294916
  24.5 1.2 %copy-start.4 = (bf16[64,768]{1,0:T(8,128)(2,1)}, bf16[64,768]{1,0:T(8,128)(2,1)S(1)}, u32[]{:S(2)}) copy-start(bf16[64,768]{1,0:T(8,128)(2,1)S(1)} %collective-permute-done.2.refs_2_) | copy-start | bytes 294916
  28.1 4.4 %collective-permute-start.4 = (bf16[16,768]{1,0:T(8,128)(2,1)}, bf16[16,768]{1,0:T(8,128)(2,1)S(1)}, u32[]{:S(2)}, u32[]{:S(2)}) collective-permute-start(bf16[16,768]{1,0:T(8,128)(2,1)} %get-tuple-element.23), channel_id=1, source_target_pairs={{0,8},{2,10},{4,12},{6,14},{8,0},{10,2},{12,4},{14,6},{16,24},{18,... | collective-permute-start | bytes 73736 | tf_op jit(solution)/shard_map/ppermute | solution.py:121
  29.6 5.1 %collective-permute-start.5 = (bf16[16,768]{1,0:T(8,128)(2,1)}, bf16[16,768]{1,0:T(8,128)(2,1)S(1)}, u32[]{:S(2)}, u32[]{:S(2)}) collective-permute-start(bf16[16,768]{1,0:T(8,128)(2,1)} %get-tuple-element.24), channel_id=1, source_target_pairs={{0,16},{2,18},{4,20},{6,22},{8,24},{10,26},{12,28},{14,30},{16,0},... | collective-permute-start | bytes 73736 | tf_op jit(solution)/shard_map/ppermute | solution.py:121
  32.2 5.8 %collective-permute-start.6 = (bf16[16,768]{1,0:T(8,128)(2,1)}, bf16[16,768]{1,0:T(8,128)(2,1)S(1)}, u32[]{:S(2)}, u32[]{:S(2)}) collective-permute-start(bf16[16,768]{1,0:T(8,128)(2,1)} %get-tuple-element.25), channel_id=1, source_target_pairs={{0,24},{2,26},{4,28},{6,30},{8,16},{10,18},{12,20},{14,22},{16,8},... | collective-permute-start | bytes 73736 | tf_op jit(solution)/shard_map/ppermute | solution.py:121
  32.5 5.6 %copy-start.12 = (bf16[16,768]{1,0:T(8,128)(2,1)}, bf16[16,768]{1,0:T(8,128)(2,1)S(1)}, u32[]{:S(2)}) copy-start(bf16[16,768]{1,0:T(8,128)(2,1)S(1)} %collective-permute-done.4.refs_1_) | copy-start | bytes 73732
  34.7 3.3 %copy-start.13 = (bf16[16,768]{1,0:T(8,128)(2,1)}, bf16[16,768]{1,0:T(8,128)(2,1)S(1)}, u32[]{:S(2)}) copy-start(bf16[16,768]{1,0:T(8,128)(2,1)S(1)} %collective-permute-done.5.refs_2_) | copy-start | bytes 73732
  40.1 5.8 %collective-permute-start.9 = (bf16[16,768]{1,0:T(8,128)(2,1)}, bf16[16,768]{1,0:T(8,128)(2,1)S(1)}, u32[]{:S(2)}, u32[]{:S(2)}) collective-permute-start(bf16[16,768]{1,0:T(8,128)(2,1)} %reduce1.1.refs_0_), channel_id=1, source_target_pairs={{0,24},{2,26},{4,28},{6,30},{8,16},{10,18},{12,20},{14,22},{16,8},... | collective-permute-start | bytes 73736 | tf_op jit(solution)/shard_map/ppermute | solution.py:121
  40.3 5.6 %collective-permute-start.8 = (bf16[16,768]{1,0:T(8,128)(2,1)}, bf16[16,768]{1,0:T(8,128)(2,1)S(1)}, u32[]{:S(2)}, u32[]{:S(2)}) collective-permute-start(bf16[16,768]{1,0:T(8,128)(2,1)} %reduce1.1.refs_0_), channel_id=1, source_target_pairs={{0,16},{2,18},{4,20},{6,22},{8,24},{10,26},{12,28},{14,30},{16,0},... | collective-permute-start | bytes 73736 | tf_op jit(solution)/shard_map/ppermute | solution.py:121
  40.4 6.2 %collective-permute-start.7 = (bf16[16,768]{1,0:T(8,128)(2,1)}, bf16[16,768]{1,0:T(8,128)(2,1)S(1)}, u32[]{:S(2)}, u32[]{:S(2)}) collective-permute-start(bf16[16,768]{1,0:T(8,128)(2,1)} %reduce1.1.refs_0_), channel_id=1, source_target_pairs={{0,8},{2,10},{4,12},{6,14},{8,0},{10,2},{12,4},{14,6},{16,24},{18,... | collective-permute-start | bytes 73736 | tf_op jit(solution)/shard_map/ppermute | solution.py:121
  48.6 5.8 %collective-permute-start.12 = (bf16[64,768]{1,0:T(8,128)(2,1)}, bf16[64,768]{1,0:T(8,128)(2,1)S(1)}, u32[]{:S(2)}, u32[]{:S(2)}) collective-permute-start(bf16[64,768]{1,0:T(8,128)(2,1)} %join.1.refs_0_), channel_id=1, source_target_pairs={{0,6},{2,4},{4,2},{6,0},{8,14},{10,12},{12,10},{14,8},{16,22},{18,... | collective-permute-start | bytes 294920 | tf_op jit(solution)/shard_map/ppermute | solution.py:121
  49.8 5.6 %collective-permute-start.11 = (bf16[64,768]{1,0:T(8,128)(2,1)}, bf16[64,768]{1,0:T(8,128)(2,1)S(1)}, u32[]{:S(2)}, u32[]{:S(2)}) collective-permute-start(bf16[64,768]{1,0:T(8,128)(2,1)} %join.1.refs_0_), channel_id=1, source_target_pairs={{0,4},{2,6},{4,0},{6,2},{8,12},{10,14},{12,8},{14,10},{16,20},{18,... | collective-permute-start | bytes 294920 | tf_op jit(solution)/shard_map/ppermute | solution.py:121
  50.9 4.8 %collective-permute-start.10 = (bf16[64,768]{1,0:T(8,128)(2,1)}, bf16[64,768]{1,0:T(8,128)(2,1)S(1)}, u32[]{:S(2)}, u32[]{:S(2)}) collective-permute-start(bf16[64,768]{1,0:T(8,128)(2,1)} %join.1.refs_0_), channel_id=1, source_target_pairs={{0,2},{2,0},{4,6},{6,4},{8,10},{10,8},{12,14},{14,12},{16,18},{18,... | collective-permute-start | bytes 294920 | tf_op jit(solution)/shard_map/ppermute | solution.py:121
  54.4 1.4 %copy-start.5 = (bf16[64,768]{1,0:T(8,128)(2,1)}, bf16[64,768]{1,0:T(8,128)(2,1)S(1)}, u32[]{:S(2)}) copy-start(bf16[64,768]{1,0:T(8,128)(2,1)S(1)} %collective-permute-done.12.refs_3_) | copy-start | bytes 294916
  55.4 0.6 copy-start.7
  58.7 11.9 %collective-permute-start.14 = (f32[256,256]{1,0:T(8,128)}, f32[256,256]{1,0:T(8,128)S(1)}, u32[]{:S(2)}, u32[]{:S(2)}) collective-permute-start(f32[256,256]{1,0:T(8,128)} %get-tuple-element.27.refs_1_), channel_id=1, source_target_pairs={{0,1},{1,0},{2,3},{3,2},{4,5},{5,4},{6,7},{7,6},{8,9},{9,8},{10,11... | collective-permute-start | bytes 786440 | tf_op jit(solution)/shard_map/ppermute | solution.py:264
  58.7 1.9 %collective-permute-start.13 = (f32[256,128]{1,0:T(8,128)}, f32[256,128]{1,0:T(8,128)S(1)}, u32[]{:S(2)}, u32[]{:S(2)}) collective-permute-start(f32[256,128]{1,0:T(8,128)} %get-tuple-element.26.refs_0_), channel_id=1, source_target_pairs={{0,1},{1,0},{2,3},{3,2},{4,5},{5,4},{6,7},{7,6},{8,9},{9,8},{10,11... | collective-permute-start | bytes 393224 | tf_op jit(solution)/shard_map/ppermute | solution.py:263
  60.6 0.7 copy-start.2
  70.6 0.7 copy-start.1
  (6 other events, 3.7 us)

commit v2 on v1

--- a/solution.py
+++ b/solution.py
@@ -12,6 +12,7 @@
 LANES = 128
 PANEL = 16
 VMEM = pl.BlockSpec(memory_space=pltpu.VMEM)
+GRANT = pltpu.CompilerParams(vmem_limit_bytes=24 << 20)
 
 
 def split2(x):
@@ -48,60 +49,89 @@
     return dot(ah, bh, dims) + (dot(ah, bm, dims) + dot(am, bh, dims) + small)
 
 
-def front_body(panel, start, left, right, sketch, filled_out, range_out, right_hi, right_lo):
-    block, cols = panel.shape
-
-    @pl.when(pl.program_id(0) == 0)
-    def _():
-        hi, lo = split2(right[...])
-        right_hi[...] = hi
-        right_lo[...] = lo
-
-    lh, ll = split2(left[...])
-    current = dot(lh, right_hi[...]) + (dot(lh, right_lo[...]) + dot(ll, right_hi[...]))
+def resident(x):
+    return pltpu.with_memory_space_constraint(x, pltpu.VMEM)
+
+
+def far(x):
+    return pltpu.with_memory_space_constraint(x, pltpu.HBM)
+
+
+def front_body(
+    panel, start, left, right, sketch, filled_out, range_out,
+    panel_in, left_buf, right_buf, sketch_buf, right_hi, right_lo, small_sems, panel_sems, left_sems,
+):
+    rows, cols = panel.shape
+    block = left_buf.shape[0] // panel_sems.shape[0]
+    count = rows // block
+    copies = [
+        pltpu.make_async_copy(right, right_buf, small_sems.at[0]),
+        pltpu.make_async_copy(sketch, sketch_buf, small_sems.at[1]),
+    ]
+    spans = [pl.ds(i * block, block) for i in range(count)]
+    lefts = [
+        pltpu.make_async_copy(left.at[s], left_buf.at[s], left_sems.at[i])
+        for i, s in enumerate(spans)
+    ]
+    panels = [
+        pltpu.make_async_copy(panel.at[s], panel_in.at[s], panel_sems.at[i])
+        for i, s in enumerate(spans)
+    ]
+    copies[0].start()
+    lefts[0].start()
+    panels[0].start()
+    copies[1].start()
+    for i in range(1, count):
+        lefts[i].start()
+        panels[i].start()
+    copies[0].wait()
+    right_hi[...], right_lo[...] = split2(right_buf[...])
     offset = lax.axis_index("week") * cols
     weeks = offset + lax.broadcasted_iota(jnp.int32, (LANES, cols), 1)
-    tiles = []
-    for t in range(block // LANES):
-        row = start[0, t : t + 1, :].astype(f32)
-        limit = jnp.broadcast_to(row, (LANES, LANES)).T.astype(jnp.int32)
-        limit = jnp.concatenate([limit] * (cols // LANES), axis=1)
-        span = slice(t * LANES, (t + 1) * LANES)
-        tiles.append(
-            jnp.where(weeks < limit, panel[span, :].astype(f32), current[span, :]).astype(bf16)
-        )
-    filled = jnp.concatenate(tiles, axis=0)
-    filled_out[...] = filled
-    range_out[...] = dot(filled, sketch[...]).astype(range_out.dtype)
+    for i, span in enumerate(spans):
+        lefts[i].wait()
+        lh, ll = split2(left_buf[span, :])
+        current = dot(lh, right_hi[...]) + (dot(lh, right_lo[...]) + dot(ll, right_hi[...]))
+        panels[i].wait()
+        for t in range(block // LANES):
+            row = start[pl.ds(i * block + t * LANES, LANES)].reshape(1, LANES).astype(f32)
+            limit = jnp.broadcast_to(row, (LANES, LANES)).T.astype(jnp.int32)
+            limit = jnp.concatenate([limit] * (cols // LANES), axis=1)
+            at = pl.ds(i * block + t * LANES, LANES)
+            known = panel_in[at, :].astype(f32)
+            filled_out[at, :] = jnp.where(
+                weeks < limit, known, current[t * LANES : (t + 1) * LANES, :]
+            ).astype(bf16)
+        if i == 0:
+            copies[1].wait()
+        range_out[span, :] = dot(filled_out[span, :], sketch_buf[...]).astype(range_out.dtype)
 
 
 def front(panel, start_week, left_in, right_in, sketch, range_type):
     rows, cols = panel.shape
     rank = left_in.shape[1]
     block = next(b for b in (256, 128) if rows % b == 0)
-    per = block // LANES
-    start = start_week.reshape(rows // block, per, LANES)
+    count = rows // block
+    hbm = pl.BlockSpec(memory_space=pl.ANY)
     return pl.pallas_call(
         front_body,
-        grid=(rows // block,),
-        in_specs=[
-            pl.BlockSpec((block, cols), lambda i: (i, 0)),
-            pl.BlockSpec((1, per, LANES), lambda i: (i, 0, 0)),
-            pl.BlockSpec((block, rank), lambda i: (i, 0)),
-            pl.BlockSpec((rank, cols), lambda i: (0, 0)),
-            pl.BlockSpec((cols, rank), lambda i: (0, 0)),
+        in_specs=[hbm, VMEM, hbm, hbm, hbm],
+        out_specs=[VMEM, VMEM],
+        out_shape=[pltpu.VMEM((rows, cols), bf16), pltpu.VMEM((rows, rank), range_type)],
+        scratch_shapes=[
+            pltpu.VMEM((rows, cols), bf16),
+            pltpu.VMEM((rows, rank), f32),
+            pltpu.VMEM((rank, cols), f32),
+            pltpu.VMEM((cols, rank), bf16),
+            pltpu.VMEM((rank, cols), bf16),
+            pltpu.VMEM((rank, cols), bf16),
+            pltpu.SemaphoreType.DMA((2,)),
+            pltpu.SemaphoreType.DMA((count,)),
+            pltpu.SemaphoreType.DMA((count,)),
         ],
-        out_specs=[
-            pl.BlockSpec((block, cols), lambda i: (i, 0)),
-            pl.BlockSpec((block, rank), lambda i: (i, 0)),
-        ],
-        out_shape=[
-            jax.ShapeDtypeStruct((rows, cols), bf16),
-            jax.ShapeDtypeStruct((rows, rank), range_type),
-        ],
-        scratch_shapes=[pltpu.VMEM((rank, cols), bf16), pltpu.VMEM((rank, cols), bf16)],
+        compiler_params=GRANT,
         name="front",
-    )(panel, start, left_in, right_in, sketch)
+    )(far(panel), start_week, far(left_in), far(right_in), far(sketch))
 
 
 def digits_of(size):
@@ -196,10 +226,11 @@
         body,
         in_specs=[VMEM] * len(ins),
         out_specs=[VMEM] * len(outs),
-        out_shape=[jax.ShapeDtypeStruct(shape, kind) for shape, kind in outs],
+        out_shape=[pltpu.VMEM(shape, kind) for shape, kind in outs],
         scratch_shapes=[pltpu.VMEM(shape, kind) for shape, kind in scratch],
+        compiler_params=GRANT,
         name=name,
-    )(*ins)
+    )(*[resident(x) for x in ins])
 
 
 def sums_by_exchange(part, filled, units):
@@ -374,49 +405,59 @@
 def final_body(count, total, *refs):
     inverse, *rest = refs
     outers, rest = rest[:count], rest[count:]
-    projected, ranged, left_out, estimate, basis_hi, basis_lo, map_hi, map_lo = rest
-
-    @pl.when(pl.program_id(0) == 0)
-    def _():
-        scaled = inverse[...] * jnp.sqrt(f32(total))
-        basis_hi[...], basis_lo[...] = split2(scaled)
-        outer = outers[0][...]
-        if count == 2:
-            outer = outer + outers[1][...]
-        map_hi[...], map_lo[...] = split2(shrink_map(inverse[...], outer, projected[...]))
-
-    rows = ranged[...]
-    left_out[...] = dot(rows, basis_hi[...], NT) + dot(rows, basis_lo[...], NT)
-    estimate[...] = (dot(rows, map_hi[...]) + dot(rows, map_lo[...])).astype(bf16)
+    projected, ranged, left_out, estimate, left_buf, estimate_buf, left_sems, estimate_sems = rest
+    chunks = left_sems.shape[0]
+    block = ranged.shape[0] // chunks
+    spans = [pl.ds(i * block, block) for i in range(chunks)]
+    lefts = [
+        pltpu.make_async_copy(left_buf.at[s], left_out.at[s], left_sems.at[i])
+        for i, s in enumerate(spans)
+    ]
+    estimates = [
+        pltpu.make_async_copy(estimate_buf.at[s], estimate.at[s], estimate_sems.at[i])
+        for i, s in enumerate(spans)
+    ]
+    factor = inverse[...]
+    hi, lo = split2(factor * jnp.sqrt(f32(total)))
+    for copy, span in zip(lefts, spans):
+        rows = ranged[span, :]
+        left_buf[span, :] = dot(rows, hi, NT) + dot(rows, lo, NT)
+        copy.start()
+    outer = outers[0][...]
+    if count == 2:
+        outer = outer + outers[1][...]
+    hi, lo = split2(shrink_map(factor, outer, projected[...]))
+    for copy, span in zip(estimates, spans):
+        rows = ranged[span, :]
+        estimate_buf[span, :] = (dot(rows, hi) + dot(rows, lo)).astype(bf16)
+        copy.start()
+    for copy in lefts + estimates:
+        copy.wait()
 
 
 def final(inverse, outers, projected, ranged, total):
     rows, rank = ranged.shape
     cols = projected.shape[1]
     block = next(b for b in (256, 128) if rows % b == 0)
-    count = len(outers)
-    whole = lambda i: (0, 0)
+    ins = [inverse, *outers, projected, ranged]
+    hbm = pl.BlockSpec(memory_space=pl.ANY)
     return pl.pallas_call(
-        functools.partial(final_body, count, total),
-        grid=(rows // block,),
-        in_specs=[pl.BlockSpec((rank, rank), whole)] * (1 + count)
-        + [pl.BlockSpec((rank, cols), whole), pl.BlockSpec((block, rank), lambda i: (i, 0))],
-        out_specs=[
-            pl.BlockSpec((block, rank), lambda i: (i, 0)),
-            pl.BlockSpec((block, cols), lambda i: (i, 0)),
-        ],
+        functools.partial(final_body, len(outers), total),
+        in_specs=[VMEM] * len(ins),
+        out_specs=[hbm, hbm],
         out_shape=[
             jax.ShapeDtypeStruct((rows, rank), f32),
             jax.ShapeDtypeStruct((rows, cols), bf16),
         ],
         scratch_shapes=[
-            pltpu.VMEM((rank, rank), bf16),
-            pltpu.VMEM((rank, rank), bf16),
-            pltpu.VMEM((rank, cols), bf16),
-            pltpu.VMEM((rank, cols), bf16),
+            pltpu.VMEM((rows, rank), f32),
+            pltpu.VMEM((rows, cols), bf16),
+            pltpu.SemaphoreType.DMA((rows // block,)),
+            pltpu.SemaphoreType.DMA((rows // block,)),
         ],
+        compiler_params=GRANT,
         name="final",
-    )(inverse, *outers, projected, ranged)
+    )(*[resident(x) for x in ins])
 
 
 def on_device(panel, start_week, left_in, right_in, sketch):

time: 82.3 us -> 62 us (0.75)
  Pallas kernels: 36.4 us -> 23 us
  local copies, waits for them, and re-layouts: 6.38 us -> 0.69 us
  waiting for transfers between devices: 20.6 us -> 19.3 us
    pallas_call x6, Pallas kernels: 19.4 us -> 8.95 us  [call(): pl.pallas_call(body, in_specs=[VMEM] * len(ins), out_specs=[VMEM] * len(o...]
    unnamed x30 -> x2, local copies, waits for them, and re-layouts: 5.08 us -> 0.69 us
    pallas_call x2, Pallas kernels: 17 us -> 14.1 us  [the longest x1 7.16 us: front(): pl.pallas_call(front_body, in_specs=[hbm, VMEM, hbm, hbm, hbm], out_specs...]
    reshape x1 -> x0, local copies, waits for them, and re-layouts: 1.3 us -> none  [front(): start = start_week.reshape(rows // block, per, LANES)]
    ppermute x12, waiting for transfers between devices: 17 us -> 16.2 us  [exchange(): return lax.ppermute(value, 'unit', [(u, partner(u)) for u in range(size)])]
  transfers between devices with their start and end apart: 15 -> 15, of which waited for: 12 -> 12; matrix products, arithmetic and copies ran while one was open for 0% -> 0% of each run, Pallas kernels for 11% -> 12%
where the time goes in v2:
time: 62 us; the launch traced here: 61.7 us
  Pallas kernels  23 us (37%)
  waiting for transfers between devices  19.3 us (31%)
  starting transfers between devices  18 us (29%)
  between operations  0.71 us (1%)
  local copies, waits for them, and re-layouts  0.69 us (1%)
    ppermute x12, starting transfers between devices, exchange(): return lax.ppermute(value, 'unit', [(u, partner(u)) for u in range(size)])  16.9 us
    ppermute x12, waiting for transfers between devices, exchange(): return lax.ppermute(value, 'unit', [(u, partner(u)) for u in range(size)])  16.2 us
    pallas_call x6, Pallas kernels, call(): pl.pallas_call(body, in_specs=[VMEM] * len(ins), out_specs=[VMEM] * len(o...  8.95 us
    pallas_call x1, Pallas kernels, front(): pl.pallas_call(front_body, in_specs=[hbm, VMEM, hbm, hbm, hbm], out_specs...  7.16 us
    pallas_call x1, Pallas kernels, final(): pl.pallas_call(functools.partial(final_body, len(outers), total), in_spec...  6.91 us
    ppermute x1, waiting for transfers between devices, sums_by_exchange(): other = lax.ppermute(part, 'week', swap)  1.91 us
  transfers between devices with their start and end apart: 15, of which 12 were waited for; matrix products, arithmetic and copies ran while one was open for 0% of the time, Pallas kernels for 12%

profile of v2, /device:TPU:0, one launch (start us, length us, event | category | flops | bytes accessed | tf_op | source)
XLA Modules:
  0.0 61.7 jit_solution(2148729461167394787)
XLA Ops:
  0.6 0.7 %copy-done = s32[1536]{0:T(1024)S(1)} copy-done((s32[1536]{0:T(1024)S(1)}, s32[1536]{0:T(1024)}, u32[]{:S(2)}) %copy-start) | copy-done | bytes 6168
  1.3 7.2 %front.1 = (bf16[1536,512]{1,0:T(8,128)(2,1)S(1)}, bf16[1536,256]{1,0:T(8,128)(2,1)S(1)}) custom-call(bf16[1536,512]{1,0:T(8,128)(2,1)} %panel.1, s32[1536]{0:T(1024)S(1)} %copy-done, f32[1536,256]{1,0:T(8,128)} %left.1, f32[256,512]{1,0:T(8,128)} %right.1, bf16[512,256]{1,0:T(8,128)(2,1)} %sketch.1), custom_call_target="tpu_custom_call" | custom-call | tf_op jit(solution)/shard_map/front/pallas_call | solution.py:116
  9.1 1.9 %collective-permute-done.refs_1_ = bf16[1536,256]{1,0:T(8,128)(2,1)S(1)} collective-permute-done((bf16[1536,256]{1,0:T(8,128)(2,1)S(1)}, bf16[1536,256]{1,0:T(8,128)(2,1)S(1)}, u32[]{:S(2)}, u32[]{:S(2)}) %collective-permute-start) | collective-permute-done | bytes 786464 | tf_op jit(solution)/shard_map/ppermute | solution.py:243
  11.0 0.9 %moments.1 = (bf16[1536,256]{1,0:T(8,128)(2,1)S(1)}, bf16[64,768]{1,0:T(8,128)(2,1)S(1)}, bf16[64,768]{1,0:T(8,128)(2,1)S(1)}, bf16[64,768]{1,0:T(8,128)(2,1)S(1)}, bf16[64,768]{1,0:T(8,128)(2,1)S(1)}) custom-call(bf16[1536,256]{1,0:T(8,128)(2,1)S(1)} %get-tuple-element.16.refs_0_, bf16[1536,256]{1,0:T(8,128)(2,1)S(1)} %collective-permute-done.refs_1_, ...), custom_call_target="tpu_custom_call" | custom-call | tf_op jit(solution)/shard_map/moments/pallas_call | solution.py:225
  11.9 2.9 %collective-permute-start.1 = (bf16[64,768]{1,0:T(8,128)(2,1)S(1)}, bf16[64,768]{1,0:T(8,128)(2,1)S(1)}, u32[]{:S(2)}, u32[]{:S(2)}) collective-permute-start(bf16[64,768]{1,0:T(8,128)(2,1)S(1)} %get-tuple-element.19), channel_id=1, source_target_pairs={{0,2},{2,0},{4,6},{6,4},{8,10},{10,8},{12,14},{14,12},{16,18},{18,... | collective-permute-start | bytes 294920 | tf_op jit(solution)/shard_map/ppermute | solution.py:151
  14.8 1.5 %collective-permute-start.2 = (bf16[64,768]{1,0:T(8,128)(2,1)S(1)}, bf16[64,768]{1,0:T(8,128)(2,1)S(1)}, u32[]{:S(2)}, u32[]{:S(2)}) collective-permute-start(bf16[64,768]{1,0:T(8,128)(2,1)S(1)} %get-tuple-element.20), channel_id=1, source_target_pairs={{0,4},{2,6},{4,0},{6,2},{8,12},{10,14},{12,8},{14,10},{16,20},{18,... | collective-permute-start | bytes 294920 | tf_op jit(solution)/shard_map/ppermute | solution.py:151
  16.3 1.6 %collective-permute-done.1.refs_1_ = bf16[64,768]{1,0:T(8,128)(2,1)S(1)} collective-permute-done((bf16[64,768]{1,0:T(8,128)(2,1)S(1)}, bf16[64,768]{1,0:T(8,128)(2,1)S(1)}, u32[]{:S(2)}, u32[]{:S(2)}) %collective-permute-start.1) | collective-permute-done | bytes 98336 | tf_op jit(solution)/shard_map/ppermute | solution.py:151
  18.0 2.6 %collective-permute-done.2.refs_2_ = bf16[64,768]{1,0:T(8,128)(2,1)S(1)} collective-permute-done((bf16[64,768]{1,0:T(8,128)(2,1)S(1)}, bf16[64,768]{1,0:T(8,128)(2,1)S(1)}, u32[]{:S(2)}, u32[]{:S(2)}) %collective-permute-start.2) | collective-permute-done | bytes 98336 | tf_op jit(solution)/shard_map/ppermute | solution.py:151
  20.6 1.3 %collective-permute-done.3.refs_3_ = bf16[64,768]{1,0:T(8,128)(2,1)S(1)} collective-permute-done((bf16[64,768]{1,0:T(8,128)(2,1)S(1)}, bf16[64,768]{1,0:T(8,128)(2,1)S(1)}, u32[]{:S(2)}, u32[]{:S(2)}) %collective-permute-start.3) | collective-permute-done | bytes 98336 | tf_op jit(solution)/shard_map/ppermute | solution.py:151
  21.9 1.6 %collective-permute-start.4 = (bf16[16,768]{1,0:T(8,128)(2,1)S(1)}, bf16[16,768]{1,0:T(8,128)(2,1)S(1)}, u32[]{:S(2)}, u32[]{:S(2)}) collective-permute-start(bf16[16,768]{1,0:T(8,128)(2,1)S(1)} %get-tuple-element.23), channel_id=1, source_target_pairs={{0,8},{2,10},{4,12},{6,14},{8,0},{10,2},{12,4},{14,6},{16,24},{18,... | collective-permute-start | bytes 73736 | tf_op jit(solution)/shard_map/ppermute | solution.py:151
  23.6 2.6 %collective-permute-start.5 = (bf16[16,768]{1,0:T(8,128)(2,1)S(1)}, bf16[16,768]{1,0:T(8,128)(2,1)S(1)}, u32[]{:S(2)}, u32[]{:S(2)}) collective-permute-start(bf16[16,768]{1,0:T(8,128)(2,1)S(1)} %get-tuple-element.24), channel_id=1, source_target_pairs={{0,16},{2,18},{4,20},{6,22},{8,24},{10,26},{12,28},{14,30},{16,0},... | collective-permute-start | bytes 73736 | tf_op jit(solution)/shard_map/ppermute | solution.py:151
  26.4 2.1 %collective-permute-done.5.refs_2_ = bf16[16,768]{1,0:T(8,128)(2,1)S(1)} collective-permute-done((bf16[16,768]{1,0:T(8,128)(2,1)S(1)}, bf16[16,768]{1,0:T(8,128)(2,1)S(1)}, u32[]{:S(2)}, u32[]{:S(2)}) %collective-permute-start.5) | collective-permute-done | bytes 24608 | tf_op jit(solution)/shard_map/ppermute | solution.py:151
  28.4 3.3 %collective-permute-done.6.refs_3_ = bf16[16,768]{1,0:T(8,128)(2,1)S(1)} collective-permute-done((bf16[16,768]{1,0:T(8,128)(2,1)S(1)}, bf16[16,768]{1,0:T(8,128)(2,1)S(1)}, u32[]{:S(2)}, u32[]{:S(2)}) %collective-permute-start.6) | collective-permute-done | bytes 24608 | tf_op jit(solution)/shard_map/ppermute | solution.py:151
  32.2 4.0 %collective-permute-start.7 = (bf16[16,768]{1,0:T(8,128)(2,1)S(1)}, bf16[16,768]{1,0:T(8,128)(2,1)S(1)}, u32[]{:S(2)}, u32[]{:S(2)}) collective-permute-start(bf16[16,768]{1,0:T(8,128)(2,1)S(1)} %reduce1.1.refs_0_), channel_id=1, source_target_pairs={{0,8},{2,10},{4,12},{6,14},{8,0},{10,2},{12,4},{14,6},{16,24},{18,... | collective-permute-start | bytes 73736 | tf_op jit(solution)/shard_map/ppermute | solution.py:151
  36.2 1.2 %collective-permute-done.9.refs_3_ = bf16[16,768]{1,0:T(8,128)(2,1)S(1)} collective-permute-done((bf16[16,768]{1,0:T(8,128)(2,1)S(1)}, bf16[16,768]{1,0:T(8,128)(2,1)S(1)}, u32[]{:S(2)}, u32[]{:S(2)}) %collective-permute-start.9) | collective-permute-done | bytes 24608 | tf_op jit(solution)/shard_map/ppermute | solution.py:151
  37.5 0.6 collective-permute-done.7.refs_1_
  38.1 1.2 %collective-permute-start.12 = (bf16[64,768]{1,0:T(8,128)(2,1)S(1)}, bf16[64,768]{1,0:T(8,128)(2,1)S(1)}, u32[]{:S(2)}, u32[]{:S(2)}) collective-permute-start(bf16[64,768]{1,0:T(8,128)(2,1)S(1)} %join.1.refs_0_), channel_id=1, source_target_pairs={{0,6},{2,4},{4,2},{6,0},{8,14},{10,12},{12,10},{14,8},{16,22},{18,... | collective-permute-start | bytes 294920 | tf_op jit(solution)/shard_map/ppermute | solution.py:151
  39.3 1.1 %collective-permute-start.11 = (bf16[64,768]{1,0:T(8,128)(2,1)S(1)}, bf16[64,768]{1,0:T(8,128)(2,1)S(1)}, u32[]{:S(2)}, u32[]{:S(2)}) collective-permute-start(bf16[64,768]{1,0:T(8,128)(2,1)S(1)} %join.1.refs_0_), channel_id=1, source_target_pairs={{0,4},{2,6},{4,0},{6,2},{8,12},{10,14},{12,8},{14,10},{16,20},{18,... | collective-permute-start | bytes 294920 | tf_op jit(solution)/shard_map/ppermute | solution.py:151
  40.5 1.2 %collective-permute-start.10 = (bf16[64,768]{1,0:T(8,128)(2,1)S(1)}, bf16[64,768]{1,0:T(8,128)(2,1)S(1)}, u32[]{:S(2)}, u32[]{:S(2)}) collective-permute-start(bf16[64,768]{1,0:T(8,128)(2,1)S(1)} %join.1.refs_0_), channel_id=1, source_target_pairs={{0,2},{2,0},{4,6},{6,4},{8,10},{10,8},{12,14},{14,12},{16,18},{18,... | collective-permute-start | bytes 294920 | tf_op jit(solution)/shard_map/ppermute | solution.py:151
  41.6 2.1 %collective-permute-done.12.refs_3_ = bf16[64,768]{1,0:T(8,128)(2,1)S(1)} collective-permute-done((bf16[64,768]{1,0:T(8,128)(2,1)S(1)}, bf16[64,768]{1,0:T(8,128)(2,1)S(1)}, u32[]{:S(2)}, u32[]{:S(2)}) %collective-permute-start.12) | collective-permute-done | bytes 98336 | tf_op jit(solution)/shard_map/ppermute | solution.py:151
  43.7 1.0 %collective-permute-done.11.refs_2_ = bf16[64,768]{1,0:T(8,128)(2,1)S(1)} collective-permute-done((bf16[64,768]{1,0:T(8,128)(2,1)S(1)}, bf16[64,768]{1,0:T(8,128)(2,1)S(1)}, u32[]{:S(2)}, u32[]{:S(2)}) %collective-permute-start.11) | collective-permute-done | bytes 98336 | tf_op jit(solution)/shard_map/ppermute | solution.py:151
  46.0 1.2 %collective-permute-done.13.refs_1_ = f32[256,128]{1,0:T(8,128)S(1)} collective-permute-done((f32[256,128]{1,0:T(8,128)S(1)}, f32[256,128]{1,0:T(8,128)S(1)}, u32[]{:S(2)}, u32[]{:S(2)}) %collective-permute-start.13) | collective-permute-done | bytes 131104 | tf_op jit(solution)/shard_map/ppermute | solution.py:294
  47.2 7.6 %factor.1.refs_0_ = f32[256,256]{1,0:T(8,128)S(1)} custom-call(f32[256,128]{1,0:T(8,128)S(1)} %get-tuple-element.26.refs_0_, f32[256,128]{1,0:T(8,128)S(1)} %collective-permute-done.13.refs_1_), custom_call_target="tpu_custom_call" | custom-call | tf_op jit(solution)/shard_map/factor/pallas_call | solution.py:225
  54.8 6.9 %final.1 = (f32[1536,256]{1,0:T(8,128)}, bf16[1536,512]{1,0:T(8,128)(2,1)}) custom-call(f32[256,256]{1,0:T(8,128)S(1)} %factor.1.refs_0_, f32[256,256]{1,0:T(8,128)S(1)} %get-tuple-element.27.refs_1_, f32[256,256]{1,0:T(8,128)S(1)} %collective-permute-done.14.refs_2_, bf16[256,512]{1,0:T(8,128)(2,1)S(1)} %get-tuple-element.28.refs_3_, ...), custom_call_target="tpu_custom_call" | custom-call | tf_op jit(solution)/shard_map/final/pallas_call | solution.py:444
  (16 shorter events, 2.6 us)
Async XLA Ops:
  0.6 0.7 %copy-start = (s32[1536]{0:T(1024)S(1)}, s32[1536]{0:T(1024)}, u32[]{:S(2)}) copy-start(s32[1536]{0:T(1024)} %start.1) | copy-start | bytes 18436
  8.5 2.5 %collective-permute-start = (bf16[1536,256]{1,0:T(8,128)(2,1)S(1)}, bf16[1536,256]{1,0:T(8,128)(2,1)S(1)}, u32[]{:S(2)}, u32[]{:S(2)}) collective-permute-start(bf16[1536,256]{1,0:T(8,128)(2,1)S(1)} %get-tuple-element.16.refs_0_), channel_id=1, source_target_pairs={{0,1},{1,0},{2,3},{3,2},{4,5},{5,4},{6,7},{7,6},{8,9},{9,8},{10,11... | collective-permute-start | bytes 2359304 | tf_op jit(solution)/shard_map/ppermute | solution.py:243
  11.9 6.1 %collective-permute-start.1 = (bf16[64,768]{1,0:T(8,128)(2,1)S(1)}, bf16[64,768]{1,0:T(8,128)(2,1)S(1)}, u32[]{:S(2)}, u32[]{:S(2)}) collective-permute-start(bf16[64,768]{1,0:T(8,128)(2,1)S(1)} %get-tuple-element.19), channel_id=1, source_target_pairs={{0,2},{2,0},{4,6},{6,4},{8,10},{10,8},{12,14},{14,12},{16,18},{18,... | collective-permute-start | bytes 294920 | tf_op jit(solution)/shard_map/ppermute | solution.py:151
  14.8 5.8 %collective-permute-start.2 = (bf16[64,768]{1,0:T(8,128)(2,1)S(1)}, bf16[64,768]{1,0:T(8,128)(2,1)S(1)}, u32[]{:S(2)}, u32[]{:S(2)}) collective-permute-start(bf16[64,768]{1,0:T(8,128)(2,1)S(1)} %get-tuple-element.20), channel_id=1, source_target_pairs={{0,4},{2,6},{4,0},{6,2},{8,12},{10,14},{12,8},{14,10},{16,20},{18,... | collective-permute-start | bytes 294920 | tf_op jit(solution)/shard_map/ppermute | solution.py:151
  16.3 5.5 %collective-permute-start.3 = (bf16[64,768]{1,0:T(8,128)(2,1)S(1)}, bf16[64,768]{1,0:T(8,128)(2,1)S(1)}, u32[]{:S(2)}, u32[]{:S(2)}) collective-permute-start(bf16[64,768]{1,0:T(8,128)(2,1)S(1)} %get-tuple-element.21), channel_id=1, source_target_pairs={{0,6},{2,4},{4,2},{6,0},{8,14},{10,12},{12,10},{14,8},{16,22},{18,... | collective-permute-start | bytes 294920 | tf_op jit(solution)/shard_map/ppermute | solution.py:151
  21.9 4.5 %collective-permute-start.4 = (bf16[16,768]{1,0:T(8,128)(2,1)S(1)}, bf16[16,768]{1,0:T(8,128)(2,1)S(1)}, u32[]{:S(2)}, u32[]{:S(2)}) collective-permute-start(bf16[16,768]{1,0:T(8,128)(2,1)S(1)} %get-tuple-element.23), channel_id=1, source_target_pairs={{0,8},{2,10},{4,12},{6,14},{8,0},{10,2},{12,4},{14,6},{16,24},{18,... | collective-permute-start | bytes 73736 | tf_op jit(solution)/shard_map/ppermute | solution.py:151
  23.6 4.9 %collective-permute-start.5 = (bf16[16,768]{1,0:T(8,128)(2,1)S(1)}, bf16[16,768]{1,0:T(8,128)(2,1)S(1)}, u32[]{:S(2)}, u32[]{:S(2)}) collective-permute-start(bf16[16,768]{1,0:T(8,128)(2,1)S(1)} %get-tuple-element.24), channel_id=1, source_target_pairs={{0,16},{2,18},{4,20},{6,22},{8,24},{10,26},{12,28},{14,30},{16,0},... | collective-permute-start | bytes 73736 | tf_op jit(solution)/shard_map/ppermute | solution.py:151
  26.1 5.6 %collective-permute-start.6 = (bf16[16,768]{1,0:T(8,128)(2,1)S(1)}, bf16[16,768]{1,0:T(8,128)(2,1)S(1)}, u32[]{:S(2)}, u32[]{:S(2)}) collective-permute-start(bf16[16,768]{1,0:T(8,128)(2,1)S(1)} %get-tuple-element.25), channel_id=1, source_target_pairs={{0,24},{2,26},{4,28},{6,30},{8,16},{10,18},{12,20},{14,22},{16,8},... | collective-permute-start | bytes 73736 | tf_op jit(solution)/shard_map/ppermute | solution.py:151
  31.8 5.7 %collective-permute-start.9 = (bf16[16,768]{1,0:T(8,128)(2,1)S(1)}, bf16[16,768]{1,0:T(8,128)(2,1)S(1)}, u32[]{:S(2)}, u32[]{:S(2)}) collective-permute-start(bf16[16,768]{1,0:T(8,128)(2,1)S(1)} %reduce1.1.refs_0_), channel_id=1, source_target_pairs={{0,24},{2,26},{4,28},{6,30},{8,16},{10,18},{12,20},{14,22},{16,8},... | collective-permute-start | bytes 73736 | tf_op jit(solution)/shard_map/ppermute | solution.py:151
  32.2 5.3 %collective-permute-start.8 = (bf16[16,768]{1,0:T(8,128)(2,1)S(1)}, bf16[16,768]{1,0:T(8,128)(2,1)S(1)}, u32[]{:S(2)}, u32[]{:S(2)}) collective-permute-start(bf16[16,768]{1,0:T(8,128)(2,1)S(1)} %reduce1.1.refs_0_), channel_id=1, source_target_pairs={{0,16},{2,18},{4,20},{6,22},{8,24},{10,26},{12,28},{14,30},{16,0},... | collective-permute-start | bytes 73736 | tf_op jit(solution)/shard_map/ppermute | solution.py:151
  32.2 5.8 %collective-permute-start.7 = (bf16[16,768]{1,0:T(8,128)(2,1)S(1)}, bf16[16,768]{1,0:T(8,128)(2,1)S(1)}, u32[]{:S(2)}, u32[]{:S(2)}) collective-permute-start(bf16[16,768]{1,0:T(8,128)(2,1)S(1)} %reduce1.1.refs_0_), channel_id=1, source_target_pairs={{0,8},{2,10},{4,12},{6,14},{8,0},{10,2},{12,4},{14,6},{16,24},{18,... | collective-permute-start | bytes 73736 | tf_op jit(solution)/shard_map/ppermute | solution.py:151
  38.1 5.7 %collective-permute-start.12 = (bf16[64,768]{1,0:T(8,128)(2,1)S(1)}, bf16[64,768]{1,0:T(8,128)(2,1)S(1)}, u32[]{:S(2)}, u32[]{:S(2)}) collective-permute-start(bf16[64,768]{1,0:T(8,128)(2,1)S(1)} %join.1.refs_0_), channel_id=1, source_target_pairs={{0,6},{2,4},{4,2},{6,0},{8,14},{10,12},{12,10},{14,8},{16,22},{18,... | collective-permute-start | bytes 294920 | tf_op jit(solution)/shard_map/ppermute | solution.py:151
  39.3 5.4 %collective-permute-start.11 = (bf16[64,768]{1,0:T(8,128)(2,1)S(1)}, bf16[64,768]{1,0:T(8,128)(2,1)S(1)}, u32[]{:S(2)}, u32[]{:S(2)}) collective-permute-start(bf16[64,768]{1,0:T(8,128)(2,1)S(1)} %join.1.refs_0_), channel_id=1, source_target_pairs={{0,4},{2,6},{4,0},{6,2},{8,12},{10,14},{12,8},{14,10},{16,20},{18,... | collective-permute-start | bytes 294920 | tf_op jit(solution)/shard_map/ppermute | solution.py:151
  40.5 4.6 %collective-permute-start.10 = (bf16[64,768]{1,0:T(8,128)(2,1)S(1)}, bf16[64,768]{1,0:T(8,128)(2,1)S(1)}, u32[]{:S(2)}, u32[]{:S(2)}) collective-permute-start(bf16[64,768]{1,0:T(8,128)(2,1)S(1)} %join.1.refs_0_), channel_id=1, source_target_pairs={{0,2},{2,0},{4,6},{6,4},{8,10},{10,8},{12,14},{14,12},{16,18},{18,... | collective-permute-start | bytes 294920 | tf_op jit(solution)/shard_map/ppermute | solution.py:151
  45.4 9.4 %collective-permute-start.14 = (f32[256,256]{1,0:T(8,128)S(1)}, f32[256,256]{1,0:T(8,128)S(1)}, u32[]{:S(2)}, u32[]{:S(2)}) collective-permute-start(f32[256,256]{1,0:T(8,128)S(1)} %get-tuple-element.27.refs_1_), channel_id=1, source_target_pairs={{0,1},{1,0},{2,3},{3,2},{4,5},{5,4},{6,7},{7,6},{8,9},{9,8},{10,11... | collective-permute-start | bytes 786440 | tf_op jit(solution)/shard_map/ppermute | solution.py:295
  45.5 1.7 %collective-permute-start.13 = (f32[256,128]{1,0:T(8,128)S(1)}, f32[256,128]{1,0:T(8,128)S(1)}, u32[]{:S(2)}, u32[]{:S(2)}) collective-permute-start(f32[256,128]{1,0:T(8,128)S(1)} %get-tuple-element.26.refs_0_), channel_id=1, source_target_pairs={{0,1},{1,0},{2,3},{3,2},{4,5},{5,4},{6,7},{7,6},{8,9},{9,8},{10,11... | collective-permute-start | bytes 393224 | tf_op jit(solution)/shard_map/ppermute | solution.py:294

commit v3 on v2

--- a/solution.py
+++ b/solution.py
@@ -59,7 +59,7 @@
 
 def front_body(
     panel, start, left, right, sketch, filled_out, range_out,
-    panel_in, left_buf, right_buf, sketch_buf, right_hi, right_lo, small_sems, panel_sems, left_sems,
+    start_in, panel_in, left_buf, right_buf, sketch_buf, right_hi, right_lo, small_sems, panel_sems, left_sems,
 ):
     rows, cols = panel.shape
     block = left_buf.shape[0] // panel_sems.shape[0]
@@ -67,6 +67,7 @@
     copies = [
         pltpu.make_async_copy(right, right_buf, small_sems.at[0]),
         pltpu.make_async_copy(sketch, sketch_buf, small_sems.at[1]),
+        pltpu.make_async_copy(start, start_in, small_sems.at[2]),
     ]
     spans = [pl.ds(i * block, block) for i in range(count)]
     lefts = [
@@ -78,6 +79,7 @@
         for i, s in enumerate(spans)
     ]
     copies[0].start()
+    copies[2].start()
     lefts[0].start()
     panels[0].start()
     copies[1].start()
@@ -85,6 +87,7 @@
         lefts[i].start()
         panels[i].start()
     copies[0].wait()
+    copies[2].wait()
     right_hi[...], right_lo[...] = split2(right_buf[...])
     offset = lax.axis_index("week") * cols
     weeks = offset + lax.broadcasted_iota(jnp.int32, (LANES, cols), 1)
@@ -94,7 +97,7 @@
         current = dot(lh, right_hi[...]) + (dot(lh, right_lo[...]) + dot(ll, right_hi[...]))
         panels[i].wait()
         for t in range(block // LANES):
-            row = start[pl.ds(i * block + t * LANES, LANES)].reshape(1, LANES).astype(f32)
+            row = start_in[pl.ds(i * block + t * LANES, LANES)].reshape(1, LANES).astype(f32)
             limit = jnp.broadcast_to(row, (LANES, LANES)).T.astype(jnp.int32)
             limit = jnp.concatenate([limit] * (cols // LANES), axis=1)
             at = pl.ds(i * block + t * LANES, LANES)
@@ -115,23 +118,24 @@
     hbm = pl.BlockSpec(memory_space=pl.ANY)
     return pl.pallas_call(
         front_body,
-        in_specs=[hbm, VMEM, hbm, hbm, hbm],
+        in_specs=[hbm] * 5,
         out_specs=[VMEM, VMEM],
         out_shape=[pltpu.VMEM((rows, cols), bf16), pltpu.VMEM((rows, rank), range_type)],
         scratch_shapes=[
+            pltpu.VMEM((rows,), jnp.int32),
             pltpu.VMEM((rows, cols), bf16),
             pltpu.VMEM((rows, rank), f32),
             pltpu.VMEM((rank, cols), f32),
             pltpu.VMEM((cols, rank), bf16),
             pltpu.VMEM((rank, cols), bf16),
             pltpu.VMEM((rank, cols), bf16),
-            pltpu.SemaphoreType.DMA((2,)),
+            pltpu.SemaphoreType.DMA((3,)),
             pltpu.SemaphoreType.DMA((count,)),
             pltpu.SemaphoreType.DMA((count,)),
         ],
         compiler_params=GRANT,
         name="front",
-    )(far(panel), start_week, far(left_in), far(right_in), far(sketch))
+    )(far(panel), far(start_week), far(left_in), far(right_in), far(sketch))
 
 
 def digits_of(size):
@@ -151,22 +155,11 @@
     return lax.ppermute(value, "unit", [(u, partner(u)) for u in range(size)])
 
 
-def unpack(piece, half):
-    gram = piece[:, :half].astype(f32) + piece[:, half : 2 * half].astype(f32)
-    return gram, piece[:, 2 * half :].astype(f32)
-
-
-def pack(gram, projected):
-    hi, lo = split2(gram)
-    return jnp.concatenate([hi, lo, projected.astype(bf16)], axis=1)
-
-
-def sum_pieces(pieces, half):
-    gram, projected = unpack(pieces[0][...], half)
-    for piece in pieces[1:]:
-        g, p = unpack(piece[...], half)
-        gram, projected = gram + g, projected + p
-    return pack(gram, projected)
+def sum_pieces(pieces):
+    values = [piece[...].astype(f32) for piece in pieces]
+    while len(values) > 1:
+        values = [a + b for a, b in zip(values[::2], values[1::2])]
+    return values[0].astype(bf16)
 
 
 def scatter_rows(packed, outs, stride, radix, scratch):
@@ -186,38 +179,44 @@
         scratch[pl.ds(at, length), :] = piece[...]
 
 
-def moments_body(stride, radix, half, *refs):
-    mine, other, filled, ranged_out, *rest = refs
-    outs, scratch = rest[:radix], rest[radix]
+def dealt(digit, length, cols):
+    radix = digit[0][1] if digit else 1
+    return [((length // radix, cols), bf16)] * radix
+
+
+def deal(packed, outs, digit, scratch):
+    if digit:
+        scatter_rows(packed, outs, *digit[0], scratch)
+    else:
+        outs[0][...] = packed
+
+
+def moments_body(digit, mine, other, filled, ranged_out, *rest):
+    *outs, scratch = rest
     ranged = (mine[...].astype(f32) + other[...].astype(f32)).astype(bf16)
     ranged_out[...] = ranged
-    week = lax.axis_index("week")
-    share = jnp.where(week == 0, ranged[:, :half], ranged[:, half:])
-    gram = dot(ranged, share, TN)
-    projected = dot(ranged, filled[...], TN)
-    scatter_rows(pack(gram, projected), outs, stride, radix, scratch)
-
-
-def reduce_body(count, stride, radix, half, *refs):
-    pieces, outs, scratch = refs[:count], refs[count : count + radix], refs[count + radix]
-    scatter_rows(sum_pieces(pieces, half), outs, stride, radix, scratch)
-
-
-def last_reduce_body(count, half, *refs):
-    refs[count][...] = sum_pieces(refs[:count], half)
-
-
-def join_body(count, stride, radix, *refs):
-    gather_rows(refs[:count], stride, radix, refs[count])
-
-
-def last_join_body(count, stride, radix, half, *refs):
-    pieces, (gram_out, projected_out, outer_out, scratch) = refs[:count], refs[count:]
-    gather_rows(pieces, stride, radix, scratch)
-    packed = scratch[...]
-    gram_out[...] = packed[:, :half].astype(f32) + packed[:, half : 2 * half].astype(f32)
-    projected = packed[:, 2 * half :]
-    projected_out[...] = projected
+    deal(dot(ranged, filled[...], TN).astype(bf16), outs, digit, scratch)
+
+
+def reduce_body(count, digit, *refs):
+    *outs, scratch = refs[count:]
+    deal(sum_pieces(refs[:count]), outs, digit, scratch)
+
+
+def reduce_all_body(count, *refs):
+    refs[count][...] = sum_pieces(refs[:count])
+
+
+def join_body(place, *refs):
+    *pieces, out = refs
+    gather_rows(pieces, *place, out)
+
+
+def last_join_body(place, sketch, *refs):
+    *pieces, projected_out, gram_out, outer_out = refs
+    gather_rows(pieces, *place, projected_out)
+    projected = projected_out[...]
+    gram_out[...] = dot(projected, sketch[...])
     outer_out[...] = dot(projected, projected, NT)
 
 
@@ -233,63 +232,60 @@
     )(*[resident(x) for x in ins])
 
 
-def sums_by_exchange(part, filled, units):
+def sums_by_exchange(part, filled, sketch, units):
     rows, cols = filled.shape
     rank = part.shape[1]
-    half = rank // 2
-    width = 2 * half + cols
     swap = [(0, 1), (1, 0)]
     digits = digits_of(units)
     other = lax.ppermute(part, "week", swap)
-    stride, radix = digits[0]
-    length = rank // radix
+    *outer_digits, (last_stride, last_radix) = digits
+    length = rank
     ranged, *pieces = call(
-        functools.partial(moments_body, stride, radix, half),
+        functools.partial(moments_body, outer_digits[:1]),
         (part, other, filled),
-        [((rows, rank), bf16)] + [((length, width), bf16)] * radix,
+        [((rows, rank), bf16)] + dealt(outer_digits[:1], rank, cols),
         "moments",
-        [((rank, width), bf16)],
+        [((rank, cols), bf16)],
     )
-    for at, (stride, radix) in enumerate(digits):
+    for at, (stride, radix) in enumerate(outer_digits):
+        length //= radix
         pieces = [pieces[0]] + [
             exchange(pieces[step], stride, radix, step, units) for step in range(1, radix)
         ]
-        if at + 1 < len(digits):
-            stride2, radix2 = digits[at + 1]
-            shorter = length // radix2
-            pieces = call(
-                functools.partial(reduce_body, radix, stride2, radix2, half),
+        following = outer_digits[at + 1 : at + 2]
+        pieces = call(
+            functools.partial(reduce_body, radix, following),
+            pieces,
+            dealt(following, length, cols),
+            f"reduce{at}",
+            [((length, cols), bf16)],
+        )
+    packed = pieces[0]
+    pieces = [packed] + [
+        exchange(packed, last_stride, last_radix, step, units) for step in range(1, last_radix)
+    ]
+    (packed,) = call(
+        functools.partial(reduce_all_body, last_radix), pieces, [((length, cols), bf16)], "total"
+    )
+    pieces, place = [packed], (1, 1)
+    for stride, radix in reversed(outer_digits):
+        if len(pieces) > 1:
+            (packed,) = call(
+                functools.partial(join_body, place),
                 pieces,
-                [((shorter, width), bf16)] * radix2,
-                f"reduce{at}",
-                [((length, width), bf16)],
+                [((length, cols), bf16)],
+                "join",
             )
-            length = shorter
-        else:
-            (packed,) = call(
-                functools.partial(last_reduce_body, radix, half),
-                pieces,
-                [((length, width), bf16)],
-                f"reduce{at}",
-            )
-    for stride, radix in reversed(digits):
         pieces = [packed] + [
             exchange(packed, stride, radix, step, units) for step in range(1, radix)
         ]
-        if length * radix < rank:
-            (packed,) = call(
-                functools.partial(join_body, radix, stride, radix),
-                pieces,
-                [((length * radix, width), bf16)],
-                "join",
-            )
-            length *= radix
-    gram, projected, outer = call(
-        functools.partial(last_join_body, radix, stride, radix, half),
-        pieces,
-        [((rank, half), f32), ((rank, cols), bf16), ((rank, rank), f32)],
+        place = (stride, radix)
+        length *= radix
+    projected, gram, outer = call(
+        functools.partial(last_join_body, place),
+        [sketch, *pieces],
+        [((rank, cols), bf16), ((rank, rank), f32), ((rank, rank), f32)],
         "last_join",
-        [((rank, width), bf16)],
     )
     gram_other = lax.ppermute(gram, "week", swap)
     outer_other = lax.ppermute(outer, "week", swap)
@@ -311,14 +307,10 @@
     n = out.shape[0]
     tiles = n // LANES
     sub = lax.broadcasted_iota(jnp.int32, (8, LANES), 0)
-    if len(grams) == 1:
-        work[:, :n] = grams[0][...]
-    else:
-        mine, other = grams
-        week = lax.axis_index("week")
-        a, b = mine[...], other[...]
-        work[:, : n // 2] = jnp.where(week == 0, a, b)
-        work[:, n // 2 : n] = jnp.where(week == 0, b, a)
+    gram = grams[0][...]
+    for other in grams[1:]:
+        gram = gram + other[...]
+    work[:, :n] = gram
     square = (n, n)
     same = lax.broadcasted_iota(jnp.int32, square, 0) == lax.broadcasted_iota(jnp.int32, square, 1)
     work[:, n:] = jnp.where(same, 1.0, 0.0).astype(f32)
@@ -464,10 +456,10 @@
     rows = panel.shape[0]
     rank = left_in.shape[1]
     units, weeks = lax.axis_size("unit"), lax.axis_size("week")
-    small = weeks == 2 and units & (units - 1) == 0 and rank // units >= 16
+    small = weeks == 2 and units in (2, 4, 8, 16)
     filled, part = front(panel, start_week, left_in, right_in, sketch, bf16 if small else f32)
     if small:
-        sums = sums_by_exchange(part, filled, units)
+        sums = sums_by_exchange(part, filled, sketch, units)
     else:
         sums = sums_by_psum(part, filled)
     ranged, grams, projected, outers = sums

time: 62 us -> 52.2 us (0.84)
  starting transfers between devices: 18 us -> 13.6 us
  waiting for transfers between devices: 19.3 us -> 15.2 us
  local copies, waits for them, and re-layouts: 0.69 us -> 0.01 us
    ppermute x12 -> x9, starting transfers between devices: 16.9 us -> 12.5 us  [exchange(): return lax.ppermute(value, 'unit', [(u, partner(u)) for u in range(size)])]
    ppermute x12 -> x9, waiting for transfers between devices: 16.2 us -> 12.3 us  [exchange(): return lax.ppermute(value, 'unit', [(u, partner(u)) for u in range(size)])]
    unnamed x2, local copies, waits for them, and re-layouts: 0.69 us -> 0.01 us
    pallas_call x6 -> x5, Pallas kernels: 8.95 us -> 8.64 us  [call(): pl.pallas_call(body, in_specs=[VMEM] * len(ins), out_specs=[VMEM] * len(o...]
  transfers between devices with their start and end apart: 15 -> 12, of which waited for: 12 -> 10; matrix products, arithmetic and copies ran while one was open for 0% -> 0% of each run, Pallas kernels for 12% -> 15%
where the time goes in v3:
time: 52.2 us; the launch traced here: 52.1 us
  Pallas kernels  22.6 us (43%)
  waiting for transfers between devices  15.2 us (29%)
  starting transfers between devices  13.6 us (26%)
  between operations  0.69 us (1%)
    ppermute x9, starting transfers between devices, exchange(): return lax.ppermute(value, 'unit', [(u, partner(u)) for u in range(size)])  12.5 us
    ppermute x9, waiting for transfers between devices, exchange(): return lax.ppermute(value, 'unit', [(u, partner(u)) for u in range(size)])  12.3 us
    pallas_call x5, Pallas kernels, call(): pl.pallas_call(body, in_specs=[VMEM] * len(ins), out_specs=[VMEM] * len(o...  8.64 us
    pallas_call x1, Pallas kernels, front(): pl.pallas_call(front_body, in_specs=[hbm] * 5, out_specs=[VMEM, VMEM], ou...  7.02 us
    pallas_call x1, Pallas kernels, final(): pl.pallas_call(functools.partial(final_body, len(outers), total), in_spec...  6.91 us
    ppermute x1, waiting for transfers between devices, sums_by_exchange(): other = lax.ppermute(part, 'week', swap)  1.91 us
  transfers between devices with their start and end apart: 12, of which 10 were waited for; matrix products, arithmetic and copies ran while one was open for 0% of the time, Pallas kernels for 15%

profile of v3, /device:TPU:0, one launch (start us, length us, event | category | flops | bytes accessed | tf_op | source)
XLA Modules:
  0.0 52.1 jit_solution(11778625446528826245)
XLA Ops:
  0.6 7.0 %front.1 = (bf16[1536,512]{1,0:T(8,128)(2,1)S(1)}, bf16[1536,256]{1,0:T(8,128)(2,1)S(1)}) custom-call(bf16[1536,512]{1,0:T(8,128)(2,1)} %panel.1, s32[1536]{0:T(1024)} %start.1, f32[1536,256]{1,0:T(8,128)} %left.1, f32[256,512]{1,0:T(8,128)} %right.1, bf16[512,256]{1,0:T(8,128)(2,1)} %sketch.3), custom_call_target="tpu_custom_call" | custom-call | tf_op jit(solution)/shard_map/front/pallas_call | solution.py:119
  7.7 0.6 %collective-permute-start = (bf16[1536,256]{1,0:T(8,128)(2,1)S(1)}, bf16[1536,256]{1,0:T(8,128)(2,1)S(1)}, u32[]{:S(2)}, u32[]{:S(2)}) collective-permute-start(bf16[1536,256]{1,0:T(8,128)(2,1)S(1)} %get-tuple-element.12.mine), channel_id=1, source_target_pairs={{0,1},{1,0},{2,3},{3,2},{4,5},{5,4},{6,7},{7,6},{8,9},{9,8},{10,11... | collective-permute-start | bytes 2359304 | tf_op jit(solution)/shard_map/ppermute | solution.py:240
  8.2 1.9 %collective-permute-done.other = bf16[1536,256]{1,0:T(8,128)(2,1)S(1)} collective-permute-done((bf16[1536,256]{1,0:T(8,128)(2,1)S(1)}, bf16[1536,256]{1,0:T(8,128)(2,1)S(1)}, u32[]{:S(2)}, u32[]{:S(2)}) %collective-permute-start) | collective-permute-done | bytes 786464 | tf_op jit(solution)/shard_map/ppermute | solution.py:240
  10.1 0.6 %moments.1 = (bf16[1536,256]{1,0:T(8,128)(2,1)S(1)}, bf16[64,512]{1,0:T(8,128)(2,1)S(1)}, bf16[64,512]{1,0:T(8,128)(2,1)S(1)}, bf16[64,512]{1,0:T(8,128)(2,1)S(1)}, bf16[64,512]{1,0:T(8,128)(2,1)S(1)}) custom-call(bf16[1536,256]{1,0:T(8,128)(2,1)S(1)} %get-tuple-element.12.mine, bf16[1536,256]{1,0:T(8,128)(2,1)S(1)} %collective-permute-done.other, ...), custom_call_target="tpu_custom_call" | custom-call | tf_op jit(solution)/shard_map/moments/pallas_call | solution.py:224
  10.8 2.9 %collective-permute-start.1 = (bf16[64,512]{1,0:T(8,128)(2,1)S(1)}, bf16[64,512]{1,0:T(8,128)(2,1)S(1)}, u32[]{:S(2)}, u32[]{:S(2)}) collective-permute-start(bf16[64,512]{1,0:T(8,128)(2,1)S(1)} %get-tuple-element.15), channel_id=1, source_target_pairs={{0,2},{2,0},{4,6},{6,4},{8,10},{10,8},{12,14},{14,12},{16,18},{18,... | collective-permute-start | bytes 196616 | tf_op jit(solution)/shard_map/ppermute | solution.py:155
  13.7 1.5 %collective-permute-start.2 = (bf16[64,512]{1,0:T(8,128)(2,1)S(1)}, bf16[64,512]{1,0:T(8,128)(2,1)S(1)}, u32[]{:S(2)}, u32[]{:S(2)}) collective-permute-start(bf16[64,512]{1,0:T(8,128)(2,1)S(1)} %get-tuple-element.16), channel_id=1, source_target_pairs={{0,4},{2,6},{4,0},{6,2},{8,12},{10,14},{12,8},{14,10},{16,20},{18,... | collective-permute-start | bytes 196616 | tf_op jit(solution)/shard_map/ppermute | solution.py:155
  15.2 0.9 %collective-permute-done.1.refs_1_ = bf16[64,512]{1,0:T(8,128)(2,1)S(1)} collective-permute-done((bf16[64,512]{1,0:T(8,128)(2,1)S(1)}, bf16[64,512]{1,0:T(8,128)(2,1)S(1)}, u32[]{:S(2)}, u32[]{:S(2)}) %collective-permute-start.1) | collective-permute-done | bytes 65568 | tf_op jit(solution)/shard_map/ppermute | solution.py:155
  16.1 1.9 %collective-permute-done.2.refs_2_ = bf16[64,512]{1,0:T(8,128)(2,1)S(1)} collective-permute-done((bf16[64,512]{1,0:T(8,128)(2,1)S(1)}, bf16[64,512]{1,0:T(8,128)(2,1)S(1)}, u32[]{:S(2)}, u32[]{:S(2)}) %collective-permute-start.2) | collective-permute-done | bytes 65568 | tf_op jit(solution)/shard_map/ppermute | solution.py:155
  17.9 2.4 %collective-permute-done.3.refs_3_ = bf16[64,512]{1,0:T(8,128)(2,1)S(1)} collective-permute-done((bf16[64,512]{1,0:T(8,128)(2,1)S(1)}, bf16[64,512]{1,0:T(8,128)(2,1)S(1)}, u32[]{:S(2)}, u32[]{:S(2)}) %collective-permute-start.3) | collective-permute-done | bytes 65568 | tf_op jit(solution)/shard_map/ppermute | solution.py:155
  20.4 3.7 %collective-permute-start.6 = (bf16[64,512]{1,0:T(8,128)(2,1)S(1)}, bf16[64,512]{1,0:T(8,128)(2,1)S(1)}, u32[]{:S(2)}, u32[]{:S(2)}) collective-permute-start(bf16[64,512]{1,0:T(8,128)(2,1)S(1)} %reduce0.1.refs_0_), channel_id=1, source_target_pairs={{0,24},{2,26},{4,28},{6,30},{8,16},{10,18},{12,20},{14,22},{16,8},... | collective-permute-start | bytes 196616 | tf_op jit(solution)/shard_map/ppermute | solution.py:155
  24.1 0.8 %collective-permute-start.4 = (bf16[64,512]{1,0:T(8,128)(2,1)S(1)}, bf16[64,512]{1,0:T(8,128)(2,1)S(1)}, u32[]{:S(2)}, u32[]{:S(2)}) collective-permute-start(bf16[64,512]{1,0:T(8,128)(2,1)S(1)} %reduce0.1.refs_0_), channel_id=1, source_target_pairs={{0,8},{2,10},{4,12},{6,14},{8,0},{10,2},{12,4},{14,6},{16,24},{18,... | collective-permute-start | bytes 196616 | tf_op jit(solution)/shard_map/ppermute | solution.py:155
  24.9 1.7 %collective-permute-done.6.refs_3_ = bf16[64,512]{1,0:T(8,128)(2,1)S(1)} collective-permute-done((bf16[64,512]{1,0:T(8,128)(2,1)S(1)}, bf16[64,512]{1,0:T(8,128)(2,1)S(1)}, u32[]{:S(2)}, u32[]{:S(2)}) %collective-permute-start.6) | collective-permute-done | bytes 65568 | tf_op jit(solution)/shard_map/ppermute | solution.py:155
  26.5 2.7 %collective-permute-done.5.refs_2_ = bf16[64,512]{1,0:T(8,128)(2,1)S(1)} collective-permute-done((bf16[64,512]{1,0:T(8,128)(2,1)S(1)}, bf16[64,512]{1,0:T(8,128)(2,1)S(1)}, u32[]{:S(2)}, u32[]{:S(2)}) %collective-permute-start.5) | collective-permute-done | bytes 65568 | tf_op jit(solution)/shard_map/ppermute | solution.py:155
  29.3 0.5 %collective-permute-start.9 = (bf16[64,512]{1,0:T(8,128)(2,1)S(1)}, bf16[64,512]{1,0:T(8,128)(2,1)S(1)}, u32[]{:S(2)}, u32[]{:S(2)}) collective-permute-start(bf16[64,512]{1,0:T(8,128)(2,1)S(1)} %total.1.refs_0_), channel_id=1, source_target_pairs={{0,6},{2,4},{4,2},{6,0},{8,14},{10,12},{12,10},{14,8},{16,22},{18,... | collective-permute-start | bytes 196616 | tf_op jit(solution)/shard_map/ppermute | solution.py:155
  29.8 1.5 %collective-permute-start.8 = (bf16[64,512]{1,0:T(8,128)(2,1)S(1)}, bf16[64,512]{1,0:T(8,128)(2,1)S(1)}, u32[]{:S(2)}, u32[]{:S(2)}) collective-permute-start(bf16[64,512]{1,0:T(8,128)(2,1)S(1)} %total.1.refs_0_), channel_id=1, source_target_pairs={{0,4},{2,6},{4,0},{6,2},{8,12},{10,14},{12,8},{14,10},{16,20},{18,... | collective-permute-start | bytes 196616 | tf_op jit(solution)/shard_map/ppermute | solution.py:155
  31.3 1.5 %collective-permute-start.7 = (bf16[64,512]{1,0:T(8,128)(2,1)S(1)}, bf16[64,512]{1,0:T(8,128)(2,1)S(1)}, u32[]{:S(2)}, u32[]{:S(2)}) collective-permute-start(bf16[64,512]{1,0:T(8,128)(2,1)S(1)} %total.1.refs_0_), channel_id=1, source_target_pairs={{0,2},{2,0},{4,6},{6,4},{8,10},{10,8},{12,14},{14,12},{16,18},{18,... | collective-permute-start | bytes 196616 | tf_op jit(solution)/shard_map/ppermute | solution.py:155
  32.8 1.8 %collective-permute-done.9.refs_3_ = bf16[64,512]{1,0:T(8,128)(2,1)S(1)} collective-permute-done((bf16[64,512]{1,0:T(8,128)(2,1)S(1)}, bf16[64,512]{1,0:T(8,128)(2,1)S(1)}, u32[]{:S(2)}, u32[]{:S(2)}) %collective-permute-start.9) | collective-permute-done | bytes 65568 | tf_op jit(solution)/shard_map/ppermute | solution.py:155
  34.6 0.2 collective-permute-done.8.refs_2_
  34.8 0.8 %collective-permute-done.7.refs_1_ = bf16[64,512]{1,0:T(8,128)(2,1)S(1)} collective-permute-done((bf16[64,512]{1,0:T(8,128)(2,1)S(1)}, bf16[64,512]{1,0:T(8,128)(2,1)S(1)}, u32[]{:S(2)}, u32[]{:S(2)}) %collective-permute-start.7) | collective-permute-done | bytes 65568 | tf_op jit(solution)/shard_map/ppermute | solution.py:155
  35.6 0.3 last_join.1
  36.0 0.5 collective-permute-start.11
  36.5 1.0 %collective-permute-done.10.refs_1_ = f32[256,256]{1,0:T(8,128)S(1)} collective-permute-done((f32[256,256]{1,0:T(8,128)S(1)}, f32[256,256]{1,0:T(8,128)S(1)}, u32[]{:S(2)}, u32[]{:S(2)}) %collective-permute-start.10) | collective-permute-done | bytes 262176 | tf_op jit(solution)/shard_map/ppermute | solution.py:290
  37.5 7.6 %factor.1.refs_0_ = f32[256,256]{1,0:T(8,128)S(1)} custom-call(f32[256,256]{1,0:T(8,128)S(1)} %get-tuple-element.18.refs_0_, f32[256,256]{1,0:T(8,128)S(1)} %collective-permute-done.10.refs_1_), custom_call_target="tpu_custom_call" | custom-call | tf_op jit(solution)/shard_map/factor/pallas_call | solution.py:224
  45.2 6.9 %final.1 = (f32[1536,256]{1,0:T(8,128)}, bf16[1536,512]{1,0:T(8,128)(2,1)}) custom-call(f32[256,256]{1,0:T(8,128)S(1)} %factor.1.refs_0_, f32[256,256]{1,0:T(8,128)S(1)} %get-tuple-element.19.refs_1_, f32[256,256]{1,0:T(8,128)S(1)} %collective-permute-done.11.refs_2_, bf16[256,512]{1,0:T(8,128)(2,1)S(1)} %get-tuple-element.20.refs_3_, ...), custom_call_target="tpu_custom_call" | custom-call | tf_op jit(solution)/shard_map/final/pallas_call | solution.py:436
  (9 shorter events, 0.2 us)
Async XLA Ops:
  7.7 2.5 %collective-permute-start = (bf16[1536,256]{1,0:T(8,128)(2,1)S(1)}, bf16[1536,256]{1,0:T(8,128)(2,1)S(1)}, u32[]{:S(2)}, u32[]{:S(2)}) collective-permute-start(bf16[1536,256]{1,0:T(8,128)(2,1)S(1)} %get-tuple-element.12.mine), channel_id=1, source_target_pairs={{0,1},{1,0},{2,3},{3,2},{4,5},{5,4},{6,7},{7,6},{8,9},{9,8},{10,11... | collective-permute-start | bytes 2359304 | tf_op jit(solution)/shard_map/ppermute | solution.py:240
  10.1 25.5 %copy-start = (bf16[512,256]{1,0:T(8,128)(2,1)S(1)}, bf16[512,256]{1,0:T(8,128)(2,1)}, u32[]{:S(2)}) copy-start(bf16[512,256]{1,0:T(8,128)(2,1)} %sketch.3) | copy-start | bytes 786436
  10.8 5.3 %collective-permute-start.1 = (bf16[64,512]{1,0:T(8,128)(2,1)S(1)}, bf16[64,512]{1,0:T(8,128)(2,1)S(1)}, u32[]{:S(2)}, u32[]{:S(2)}) collective-permute-start(bf16[64,512]{1,0:T(8,128)(2,1)S(1)} %get-tuple-element.15), channel_id=1, source_target_pairs={{0,2},{2,0},{4,6},{6,4},{8,10},{10,8},{12,14},{14,12},{16,18},{18,... | collective-permute-start | bytes 196616 | tf_op jit(solution)/shard_map/ppermute | solution.py:155
  13.7 4.3 %collective-permute-start.2 = (bf16[64,512]{1,0:T(8,128)(2,1)S(1)}, bf16[64,512]{1,0:T(8,128)(2,1)S(1)}, u32[]{:S(2)}, u32[]{:S(2)}) collective-permute-start(bf16[64,512]{1,0:T(8,128)(2,1)S(1)} %get-tuple-element.16), channel_id=1, source_target_pairs={{0,4},{2,6},{4,0},{6,2},{8,12},{10,14},{12,8},{14,10},{16,20},{18,... | collective-permute-start | bytes 196616 | tf_op jit(solution)/shard_map/ppermute | solution.py:155
  15.2 5.2 %collective-permute-start.3 = (bf16[64,512]{1,0:T(8,128)(2,1)S(1)}, bf16[64,512]{1,0:T(8,128)(2,1)S(1)}, u32[]{:S(2)}, u32[]{:S(2)}) collective-permute-start(bf16[64,512]{1,0:T(8,128)(2,1)S(1)} %get-tuple-element.17), channel_id=1, source_target_pairs={{0,6},{2,4},{4,2},{6,0},{8,14},{10,12},{12,10},{14,8},{16,22},{18,... | collective-permute-start | bytes 196616 | tf_op jit(solution)/shard_map/ppermute | solution.py:155
  20.4 6.1 %collective-permute-start.6 = (bf16[64,512]{1,0:T(8,128)(2,1)S(1)}, bf16[64,512]{1,0:T(8,128)(2,1)S(1)}, u32[]{:S(2)}, u32[]{:S(2)}) collective-permute-start(bf16[64,512]{1,0:T(8,128)(2,1)S(1)} %reduce0.1.refs_0_), channel_id=1, source_target_pairs={{0,24},{2,26},{4,28},{6,30},{8,16},{10,18},{12,20},{14,22},{16,8},... | collective-permute-start | bytes 196616 | tf_op jit(solution)/shard_map/ppermute | solution.py:155
  24.1 5.2 %collective-permute-start.5 = (bf16[64,512]{1,0:T(8,128)(2,1)S(1)}, bf16[64,512]{1,0:T(8,128)(2,1)S(1)}, u32[]{:S(2)}, u32[]{:S(2)}) collective-permute-start(bf16[64,512]{1,0:T(8,128)(2,1)S(1)} %reduce0.1.refs_0_), channel_id=1, source_target_pairs={{0,16},{2,18},{4,20},{6,22},{8,24},{10,26},{12,28},{14,30},{16,0},... | collective-permute-start | bytes 196616 | tf_op jit(solution)/shard_map/ppermute | solution.py:155
  24.1 5.2 %collective-permute-start.4 = (bf16[64,512]{1,0:T(8,128)(2,1)S(1)}, bf16[64,512]{1,0:T(8,128)(2,1)S(1)}, u32[]{:S(2)}, u32[]{:S(2)}) collective-permute-start(bf16[64,512]{1,0:T(8,128)(2,1)S(1)} %reduce0.1.refs_0_), channel_id=1, source_target_pairs={{0,8},{2,10},{4,12},{6,14},{8,0},{10,2},{12,4},{14,6},{16,24},{18,... | collective-permute-start | bytes 196616 | tf_op jit(solution)/shard_map/ppermute | solution.py:155
  29.3 5.3 %collective-permute-start.9 = (bf16[64,512]{1,0:T(8,128)(2,1)S(1)}, bf16[64,512]{1,0:T(8,128)(2,1)S(1)}, u32[]{:S(2)}, u32[]{:S(2)}) collective-permute-start(bf16[64,512]{1,0:T(8,128)(2,1)S(1)} %total.1.refs_0_), channel_id=1, source_target_pairs={{0,6},{2,4},{4,2},{6,0},{8,14},{10,12},{12,10},{14,8},{16,22},{18,... | collective-permute-start | bytes 196616 | tf_op jit(solution)/shard_map/ppermute | solution.py:155
  29.8 5.0 %collective-permute-start.8 = (bf16[64,512]{1,0:T(8,128)(2,1)S(1)}, bf16[64,512]{1,0:T(8,128)(2,1)S(1)}, u32[]{:S(2)}, u32[]{:S(2)}) collective-permute-start(bf16[64,512]{1,0:T(8,128)(2,1)S(1)} %total.1.refs_0_), channel_id=1, source_target_pairs={{0,4},{2,6},{4,0},{6,2},{8,12},{10,14},{12,8},{14,10},{16,20},{18,... | collective-permute-start | bytes 196616 | tf_op jit(solution)/shard_map/ppermute | solution.py:155
  31.3 4.3 %collective-permute-start.7 = (bf16[64,512]{1,0:T(8,128)(2,1)S(1)}, bf16[64,512]{1,0:T(8,128)(2,1)S(1)}, u32[]{:S(2)}, u32[]{:S(2)}) collective-permute-start(bf16[64,512]{1,0:T(8,128)(2,1)S(1)} %total.1.refs_0_), channel_id=1, source_target_pairs={{0,2},{2,0},{4,6},{6,4},{8,10},{10,8},{12,14},{14,12},{16,18},{18,... | collective-permute-start | bytes 196616 | tf_op jit(solution)/shard_map/ppermute | solution.py:155
  35.9 1.6 %collective-permute-start.10 = (f32[256,256]{1,0:T(8,128)S(1)}, f32[256,256]{1,0:T(8,128)S(1)}, u32[]{:S(2)}, u32[]{:S(2)}) collective-permute-start(f32[256,256]{1,0:T(8,128)S(1)} %get-tuple-element.18.refs_0_), channel_id=1, source_target_pairs={{0,1},{1,0},{2,3},{3,2},{4,5},{5,4},{6,7},{7,6},{8,9},{9,8},{10,11... | collective-permute-start | bytes 786440 | tf_op jit(solution)/shard_map/ppermute | solution.py:290
  36.0 9.1 %collective-permute-start.11 = (f32[256,256]{1,0:T(8,128)S(1)}, f32[256,256]{1,0:T(8,128)S(1)}, u32[]{:S(2)}, u32[]{:S(2)}) collective-permute-start(f32[256,256]{1,0:T(8,128)S(1)} %get-tuple-element.19.refs_1_), channel_id=1, source_target_pairs={{0,1},{1,0},{2,3},{3,2},{4,5},{5,4},{6,7},{7,6},{8,9},{9,8},{10,11... | collective-permute-start | bytes 786440 | tf_op jit(solution)/shard_map/ppermute | solution.py:291

commit v4 on v3

--- a/solution.py
+++ b/solution.py
@@ -36,17 +36,18 @@
     return lax.dot_general(a, b, dims, preferred_element_type=f32)
 
 
-def dot3(a, b, dims=NN):
-    ah, al = split2(a)
-    bh, bl = split2(b)
-    return dot(ah, bh, dims) + (dot(ah, bl, dims) + dot(al, bh, dims))
-
-
-def dot6(a, b, dims=NN):
-    ah, am, al = split3(a)
-    bh, bm, bl = split3(b)
-    small = dot(ah, bl, dims) + dot(al, bh, dims) + dot(am, bm, dims)
-    return dot(ah, bh, dims) + (dot(ah, bm, dims) + dot(am, bh, dims) + small)
+def left3(a):
+    high, low = split2(a)
+    return jnp.concatenate([high, high, low], axis=1)
+
+
+def right3(b, axis=0):
+    high, low = split2(b)
+    return jnp.concatenate([high, low, high], axis=axis)
+
+
+def dot3(a, b):
+    return dot(left3(a), right3(b))
 
 
 def resident(x):
@@ -59,7 +60,7 @@
 
 def front_body(
     panel, start, left, right, sketch, filled_out, range_out,
-    start_in, panel_in, left_buf, right_buf, sketch_buf, right_hi, right_lo, small_sems, panel_sems, left_sems,
+    start_in, panel_in, left_buf, right_buf, sketch_buf, right_cat, small_sems, panel_sems, left_sems,
 ):
     rows, cols = panel.shape
     block = left_buf.shape[0] // panel_sems.shape[0]
@@ -88,14 +89,21 @@
         panels[i].start()
     copies[0].wait()
     copies[2].wait()
-    right_hi[...], right_lo[...] = split2(right_buf[...])
+    right_cat[...] = right3(right_buf[...])
     offset = lax.axis_index("week") * cols
     weeks = offset + lax.broadcasted_iota(jnp.int32, (LANES, cols), 1)
+
+    def range_of(span):
+        range_out[span, :] = dot(filled_out[span, :], sketch_buf[...]).astype(range_out.dtype)
+
     for i, span in enumerate(spans):
         lefts[i].wait()
-        lh, ll = split2(left_buf[span, :])
-        current = dot(lh, right_hi[...]) + (dot(lh, right_lo[...]) + dot(ll, right_hi[...]))
         panels[i].wait()
+        if i == 1:
+            copies[1].wait()
+        current = dot(left3(left_buf[span, :]), right_cat[...])
+        if i > 0:
+            range_of(spans[i - 1])
         for t in range(block // LANES):
             row = start_in[pl.ds(i * block + t * LANES, LANES)].reshape(1, LANES).astype(f32)
             limit = jnp.broadcast_to(row, (LANES, LANES)).T.astype(jnp.int32)
@@ -105,15 +113,15 @@
             filled_out[at, :] = jnp.where(
                 weeks < limit, known, current[t * LANES : (t + 1) * LANES, :]
             ).astype(bf16)
-        if i == 0:
-            copies[1].wait()
-        range_out[span, :] = dot(filled_out[span, :], sketch_buf[...]).astype(range_out.dtype)
+    if count == 1:
+        copies[1].wait()
+    range_of(spans[-1])
 
 
 def front(panel, start_week, left_in, right_in, sketch, range_type):
     rows, cols = panel.shape
     rank = left_in.shape[1]
-    block = next(b for b in (256, 128) if rows % b == 0)
+    block = next(b for b in (768, 512, 256, 128) if rows % b == 0)
     count = rows // block
     hbm = pl.BlockSpec(memory_space=pl.ANY)
     return pl.pallas_call(
@@ -127,8 +135,7 @@
             pltpu.VMEM((rows, rank), f32),
             pltpu.VMEM((rank, cols), f32),
             pltpu.VMEM((cols, rank), bf16),
-            pltpu.VMEM((rank, cols), bf16),
-            pltpu.VMEM((rank, cols), bf16),
+            pltpu.VMEM((3 * rank, cols), bf16),
             pltpu.SemaphoreType.DMA((3,)),
             pltpu.SemaphoreType.DMA((count,)),
             pltpu.SemaphoreType.DMA((count,)),
@@ -366,32 +373,36 @@
             work[r1:, n:end] = work[r1:, n:end] - change[top:, wide:]
 
 
-def shrink_map(inverse, outer, projected):
+def shrink_map(inverse, turned, outer, projected):
     n = inverse.shape[0]
-    spectrum = dot6(dot6(inverse, outer), inverse, NT)
+    half = dot3(inverse, outer)
+    products = jnp.sum(half * inverse, axis=1, keepdims=True)
+    level = jnp.sum(products, axis=0, keepdims=True) / n
+    spectrum = dot(left3(half), right3(inverse, axis=1), NT)
+    ih, il = split2(inverse)
+    coeffs = dot(
+        jnp.concatenate([ih, il], axis=1), jnp.concatenate([projected, projected], axis=0)
+    )
+    coeffs3 = right3(coeffs)
+    kept = dot(left3(turned), coeffs3)
+    low, high = 1.0, n + 1.0
+    top = (high + low) / (high - low)
+    step = 2.0 / (high + low)
     square = (n, n)
     same = lax.broadcasted_iota(jnp.int32, square, 0) == lax.broadcasted_iota(jnp.int32, square, 1)
-    trace = jnp.sum(jnp.where(same, spectrum, 0.0), axis=1, keepdims=True)
-    level = jnp.sum(trace, axis=0, keepdims=True) / n
-    low, high = 1.0, n + 1.0
-    top = (high + low) / (high - low)
-    eye = jnp.where(same, 1.0, 0.0).astype(f32)
-    residual = eye - (eye + spectrum / level) * (2.0 / (high + low))
-    solve = None
+    residual = jnp.where(same, 1.0 - step, 0.0) - spectrum * (step / level)
+    solve = turned * step
     while True:
-        gain = 2.0 * top * top / (2.0 * top * top - 1.0)
-        if solve is None:
-            solve = (eye + residual) * (gain * 2.0 / (high + low))
-        else:
+        after = 2.0 * top * top - 1.0
+        gain = 1.0 + 1.0 / after
+        if after > 1.0e6:
             solve = gain * (solve + dot3(solve, residual))
-        if 2.0 * top * top - 1.0 > 1.0e6:
             break
-        residual = gain * dot3(residual, residual) - eye * (1.0 / (2.0 * top * top - 1.0))
-        top = 2.0 * top * top - 1.0
-    kept = inverse - dot3(solve, inverse)
-    kh, kl = split2(kept)
-    middle = dot(kh, projected) + dot(kl, projected)
-    return dot3(inverse, middle, TN)
+        pair = right3(residual)
+        solve = gain * (solve + dot(left3(solve), pair))
+        residual = gain * dot(left3(residual), pair) - jnp.where(same, 1.0 / after, 0.0)
+        top = after
+    return kept - dot(left3(solve), coeffs3)
 
 
 def final_body(count, total, *refs):
@@ -409,19 +420,23 @@
         pltpu.make_async_copy(estimate_buf.at[s], estimate.at[s], estimate_sems.at[i])
         for i, s in enumerate(spans)
     ]
+
+    def times(span, pair):
+        rows = ranged[span, :]
+        return dot(jnp.concatenate([rows, rows], axis=1), pair)
+
     factor = inverse[...]
-    hi, lo = split2(factor * jnp.sqrt(f32(total)))
+    turned = factor.T
+    pair = jnp.concatenate(split2(turned * jnp.sqrt(f32(total))), axis=0)
     for copy, span in zip(lefts, spans):
-        rows = ranged[span, :]
-        left_buf[span, :] = dot(rows, hi, NT) + dot(rows, lo, NT)
+        left_buf[span, :] = times(span, pair)
         copy.start()
     outer = outers[0][...]
     if count == 2:
         outer = outer + outers[1][...]
-    hi, lo = split2(shrink_map(factor, outer, projected[...]))
+    pair = jnp.concatenate(split2(shrink_map(factor, turned, outer, projected[...])), axis=0)
     for copy, span in zip(estimates, spans):
-        rows = ranged[span, :]
-        estimate_buf[span, :] = (dot(rows, hi) + dot(rows, lo)).astype(bf16)
+        estimate_buf[span, :] = times(span, pair).astype(bf16)
         copy.start()
     for copy in lefts + estimates:
         copy.wait()
@@ -430,7 +445,7 @@
 def final(inverse, outers, projected, ranged, total):
     rows, rank = ranged.shape
     cols = projected.shape[1]
-    block = next(b for b in (256, 128) if rows % b == 0)
+    block = next(b for b in (384, 256, 128) if rows % b == 0)
     ins = [inverse, *outers, projected, ranged]
     hbm = pl.BlockSpec(memory_space=pl.ANY)
     return pl.pallas_call(

time: 52.2 us -> 47.8 us (0.916)
  Pallas kernels: 22.6 us -> 18.1 us
    pallas_call x1, Pallas kernels: 7.02 us -> 3.62 us  [front(): pl.pallas_call(front_body, in_specs=[hbm] * 5, out_specs=[VMEM, VMEM], ou...]
    pallas_call x1, Pallas kernels: 6.91 us -> 5.86 us  [final(): pl.pallas_call(functools.partial(final_body, len(outers), total), in_spec...]
  transfers between devices with their start and end apart: 12 -> 12, of which waited for: 10 -> 10; matrix products, arithmetic and copies ran while one was open for 0% -> 0% of each run, Pallas kernels for 15% -> 16%
where the time goes in v4:
time: 47.8 us; the launch traced here: 47.6 us
  Pallas kernels  18.1 us (38%)
  waiting for transfers between devices  15.2 us (32%)
  starting transfers between devices  13.6 us (28%)
  between operations  0.69 us (1%)
    ppermute x9, starting transfers between devices, exchange(): return lax.ppermute(value, 'unit', [(u, partner(u)) for u in range(size)])  12.5 us
    ppermute x9, waiting for transfers between devices, exchange(): return lax.ppermute(value, 'unit', [(u, partner(u)) for u in range(size)])  12.3 us
    pallas_call x5, Pallas kernels, call(): pl.pallas_call(body, in_specs=[VMEM] * len(ins), out_specs=[VMEM] * len(o...  8.64 us
    pallas_call x1, Pallas kernels, final(): pl.pallas_call(functools.partial(final_body, len(outers), total), in_spec...  5.86 us
    pallas_call x1, Pallas kernels, front(): pl.pallas_call(front_body, in_specs=[hbm] * 5, out_specs=[VMEM, VMEM], ou...  3.62 us
    ppermute x1, waiting for transfers between devices, sums_by_exchange(): other = lax.ppermute(part, 'week', swap)  1.91 us
    ppermute x1, waiting for transfers between devices, sums_by_exchange(): gram_other = lax.ppermute(gram, 'week', swap)  1.02 us
  transfers between devices with their start and end apart: 12, of which 10 were waited for; matrix products, arithmetic and copies ran while one was open for 0% of the time, Pallas kernels for 16%

profile of v4, /device:TPU:0, one launch (start us, length us, event | category | flops | bytes accessed | tf_op | source)
XLA Modules:
  0.0 47.6 jit_solution(4777410371177421972)
XLA Ops:
  0.6 3.6 %front.1 = (bf16[1536,512]{1,0:T(8,128)(2,1)S(1)}, bf16[1536,256]{1,0:T(8,128)(2,1)S(1)}) custom-call(bf16[1536,512]{1,0:T(8,128)(2,1)} %panel.1, s32[1536]{0:T(1024)} %start.1, f32[1536,256]{1,0:T(8,128)} %left.1, f32[256,512]{1,0:T(8,128)} %right.1, bf16[512,256]{1,0:T(8,128)(2,1)} %sketch.3), custom_call_target="tpu_custom_call" | custom-call | tf_op jit(solution)/shard_map/front/pallas_call | solution.py:127
  4.3 0.6 %collective-permute-start = (bf16[1536,256]{1,0:T(8,128)(2,1)S(1)}, bf16[1536,256]{1,0:T(8,128)(2,1)S(1)}, u32[]{:S(2)}, u32[]{:S(2)}) collective-permute-start(bf16[1536,256]{1,0:T(8,128)(2,1)S(1)} %get-tuple-element.12.mine), channel_id=1, source_target_pairs={{0,1},{1,0},{2,3},{3,2},{4,5},{5,4},{6,7},{7,6},{8,9},{9,8},{10,11... | collective-permute-start | bytes 2359304 | tf_op jit(solution)/shard_map/ppermute | solution.py:247
  4.8 1.9 %collective-permute-done.other = bf16[1536,256]{1,0:T(8,128)(2,1)S(1)} collective-permute-done((bf16[1536,256]{1,0:T(8,128)(2,1)S(1)}, bf16[1536,256]{1,0:T(8,128)(2,1)S(1)}, u32[]{:S(2)}, u32[]{:S(2)}) %collective-permute-start) | collective-permute-done | bytes 786464 | tf_op jit(solution)/shard_map/ppermute | solution.py:247
  6.7 0.6 %moments.1 = (bf16[1536,256]{1,0:T(8,128)(2,1)S(1)}, bf16[64,512]{1,0:T(8,128)(2,1)S(1)}, bf16[64,512]{1,0:T(8,128)(2,1)S(1)}, bf16[64,512]{1,0:T(8,128)(2,1)S(1)}, bf16[64,512]{1,0:T(8,128)(2,1)S(1)}) custom-call(bf16[1536,256]{1,0:T(8,128)(2,1)S(1)} %get-tuple-element.12.mine, bf16[1536,256]{1,0:T(8,128)(2,1)S(1)} %collective-permute-done.other, ...), custom_call_target="tpu_custom_call" | custom-call | tf_op jit(solution)/shard_map/moments/pallas_call | solution.py:231
  7.4 2.9 %collective-permute-start.1 = (bf16[64,512]{1,0:T(8,128)(2,1)S(1)}, bf16[64,512]{1,0:T(8,128)(2,1)S(1)}, u32[]{:S(2)}, u32[]{:S(2)}) collective-permute-start(bf16[64,512]{1,0:T(8,128)(2,1)S(1)} %get-tuple-element.15), channel_id=1, source_target_pairs={{0,2},{2,0},{4,6},{6,4},{8,10},{10,8},{12,14},{14,12},{16,18},{18,... | collective-permute-start | bytes 196616 | tf_op jit(solution)/shard_map/ppermute | solution.py:162
  10.3 1.5 %collective-permute-start.2 = (bf16[64,512]{1,0:T(8,128)(2,1)S(1)}, bf16[64,512]{1,0:T(8,128)(2,1)S(1)}, u32[]{:S(2)}, u32[]{:S(2)}) collective-permute-start(bf16[64,512]{1,0:T(8,128)(2,1)S(1)} %get-tuple-element.16), channel_id=1, source_target_pairs={{0,4},{2,6},{4,0},{6,2},{8,12},{10,14},{12,8},{14,10},{16,20},{18,... | collective-permute-start | bytes 196616 | tf_op jit(solution)/shard_map/ppermute | solution.py:162
  11.8 0.9 %collective-permute-done.1.refs_1_ = bf16[64,512]{1,0:T(8,128)(2,1)S(1)} collective-permute-done((bf16[64,512]{1,0:T(8,128)(2,1)S(1)}, bf16[64,512]{1,0:T(8,128)(2,1)S(1)}, u32[]{:S(2)}, u32[]{:S(2)}) %collective-permute-start.1) | collective-permute-done | bytes 65568 | tf_op jit(solution)/shard_map/ppermute | solution.py:162
  12.7 1.9 %collective-permute-done.2.refs_2_ = bf16[64,512]{1,0:T(8,128)(2,1)S(1)} collective-permute-done((bf16[64,512]{1,0:T(8,128)(2,1)S(1)}, bf16[64,512]{1,0:T(8,128)(2,1)S(1)}, u32[]{:S(2)}, u32[]{:S(2)}) %collective-permute-start.2) | collective-permute-done | bytes 65568 | tf_op jit(solution)/shard_map/ppermute | solution.py:162
  14.5 2.4 %collective-permute-done.3.refs_3_ = bf16[64,512]{1,0:T(8,128)(2,1)S(1)} collective-permute-done((bf16[64,512]{1,0:T(8,128)(2,1)S(1)}, bf16[64,512]{1,0:T(8,128)(2,1)S(1)}, u32[]{:S(2)}, u32[]{:S(2)}) %collective-permute-start.3) | collective-permute-done | bytes 65568 | tf_op jit(solution)/shard_map/ppermute | solution.py:162
  17.0 3.7 %collective-permute-start.6 = (bf16[64,512]{1,0:T(8,128)(2,1)S(1)}, bf16[64,512]{1,0:T(8,128)(2,1)S(1)}, u32[]{:S(2)}, u32[]{:S(2)}) collective-permute-start(bf16[64,512]{1,0:T(8,128)(2,1)S(1)} %reduce0.1.refs_0_), channel_id=1, source_target_pairs={{0,24},{2,26},{4,28},{6,30},{8,16},{10,18},{12,20},{14,22},{16,8},... | collective-permute-start | bytes 196616 | tf_op jit(solution)/shard_map/ppermute | solution.py:162
  20.7 0.8 %collective-permute-start.4 = (bf16[64,512]{1,0:T(8,128)(2,1)S(1)}, bf16[64,512]{1,0:T(8,128)(2,1)S(1)}, u32[]{:S(2)}, u32[]{:S(2)}) collective-permute-start(bf16[64,512]{1,0:T(8,128)(2,1)S(1)} %reduce0.1.refs_0_), channel_id=1, source_target_pairs={{0,8},{2,10},{4,12},{6,14},{8,0},{10,2},{12,4},{14,6},{16,24},{18,... | collective-permute-start | bytes 196616 | tf_op jit(solution)/shard_map/ppermute | solution.py:162
  21.5 1.7 %collective-permute-done.6.refs_3_ = bf16[64,512]{1,0:T(8,128)(2,1)S(1)} collective-permute-done((bf16[64,512]{1,0:T(8,128)(2,1)S(1)}, bf16[64,512]{1,0:T(8,128)(2,1)S(1)}, u32[]{:S(2)}, u32[]{:S(2)}) %collective-permute-start.6) | collective-permute-done | bytes 65568 | tf_op jit(solution)/shard_map/ppermute | solution.py:162
  23.1 2.7 %collective-permute-done.5.refs_2_ = bf16[64,512]{1,0:T(8,128)(2,1)S(1)} collective-permute-done((bf16[64,512]{1,0:T(8,128)(2,1)S(1)}, bf16[64,512]{1,0:T(8,128)(2,1)S(1)}, u32[]{:S(2)}, u32[]{:S(2)}) %collective-permute-start.5) | collective-permute-done | bytes 65568 | tf_op jit(solution)/shard_map/ppermute | solution.py:162
  25.9 0.5 %collective-permute-start.9 = (bf16[64,512]{1,0:T(8,128)(2,1)S(1)}, bf16[64,512]{1,0:T(8,128)(2,1)S(1)}, u32[]{:S(2)}, u32[]{:S(2)}) collective-permute-start(bf16[64,512]{1,0:T(8,128)(2,1)S(1)} %total.1.refs_0_), channel_id=1, source_target_pairs={{0,6},{2,4},{4,2},{6,0},{8,14},{10,12},{12,10},{14,8},{16,22},{18,... | collective-permute-start | bytes 196616 | tf_op jit(solution)/shard_map/ppermute | solution.py:162
  26.4 1.5 %collective-permute-start.8 = (bf16[64,512]{1,0:T(8,128)(2,1)S(1)}, bf16[64,512]{1,0:T(8,128)(2,1)S(1)}, u32[]{:S(2)}, u32[]{:S(2)}) collective-permute-start(bf16[64,512]{1,0:T(8,128)(2,1)S(1)} %total.1.refs_0_), channel_id=1, source_target_pairs={{0,4},{2,6},{4,0},{6,2},{8,12},{10,14},{12,8},{14,10},{16,20},{18,... | collective-permute-start | bytes 196616 | tf_op jit(solution)/shard_map/ppermute | solution.py:162
  27.9 1.5 %collective-permute-start.7 = (bf16[64,512]{1,0:T(8,128)(2,1)S(1)}, bf16[64,512]{1,0:T(8,128)(2,1)S(1)}, u32[]{:S(2)}, u32[]{:S(2)}) collective-permute-start(bf16[64,512]{1,0:T(8,128)(2,1)S(1)} %total.1.refs_0_), channel_id=1, source_target_pairs={{0,2},{2,0},{4,6},{6,4},{8,10},{10,8},{12,14},{14,12},{16,18},{18,... | collective-permute-start | bytes 196616 | tf_op jit(solution)/shard_map/ppermute | solution.py:162
  29.4 1.8 %collective-permute-done.9.refs_3_ = bf16[64,512]{1,0:T(8,128)(2,1)S(1)} collective-permute-done((bf16[64,512]{1,0:T(8,128)(2,1)S(1)}, bf16[64,512]{1,0:T(8,128)(2,1)S(1)}, u32[]{:S(2)}, u32[]{:S(2)}) %collective-permute-start.9) | collective-permute-done | bytes 65568 | tf_op jit(solution)/shard_map/ppermute | solution.py:162
  31.2 0.2 collective-permute-done.8.refs_2_
  31.4 0.8 %collective-permute-done.7.refs_1_ = bf16[64,512]{1,0:T(8,128)(2,1)S(1)} collective-permute-done((bf16[64,512]{1,0:T(8,128)(2,1)S(1)}, bf16[64,512]{1,0:T(8,128)(2,1)S(1)}, u32[]{:S(2)}, u32[]{:S(2)}) %collective-permute-start.7) | collective-permute-done | bytes 65568 | tf_op jit(solution)/shard_map/ppermute | solution.py:162
  32.2 0.3 last_join.1
  32.6 0.5 %collective-permute-start.11 = (f32[256,256]{1,0:T(8,128)S(1)}, f32[256,256]{1,0:T(8,128)S(1)}, u32[]{:S(2)}, u32[]{:S(2)}) collective-permute-start(f32[256,256]{1,0:T(8,128)S(1)} %get-tuple-element.19.refs_1_), channel_id=1, source_target_pairs={{0,1},{1,0},{2,3},{3,2},{4,5},{5,4},{6,7},{7,6},{8,9},{9,8},{10,11... | collective-permute-start | bytes 786440 | tf_op jit(solution)/shard_map/ppermute | solution.py:298
  33.1 1.0 %collective-permute-done.10.refs_1_ = f32[256,256]{1,0:T(8,128)S(1)} collective-permute-done((f32[256,256]{1,0:T(8,128)S(1)}, f32[256,256]{1,0:T(8,128)S(1)}, u32[]{:S(2)}, u32[]{:S(2)}) %collective-permute-start.10) | collective-permute-done | bytes 262176 | tf_op jit(solution)/shard_map/ppermute | solution.py:297
  34.1 7.6 %factor.1.refs_0_ = f32[256,256]{1,0:T(8,128)S(1)} custom-call(f32[256,256]{1,0:T(8,128)S(1)} %get-tuple-element.18.refs_0_, f32[256,256]{1,0:T(8,128)S(1)} %collective-permute-done.10.refs_1_), custom_call_target="tpu_custom_call" | custom-call | tf_op jit(solution)/shard_map/factor/pallas_call | solution.py:231
  41.8 5.9 %final.1 = (f32[1536,256]{1,0:T(8,128)}, bf16[1536,512]{1,0:T(8,128)(2,1)}) custom-call(f32[256,256]{1,0:T(8,128)S(1)} %factor.1.refs_0_, f32[256,256]{1,0:T(8,128)S(1)} %get-tuple-element.19.refs_1_, f32[256,256]{1,0:T(8,128)S(1)} %collective-permute-done.11.refs_2_, bf16[256,512]{1,0:T(8,128)(2,1)S(1)} %get-tuple-element.20.refs_3_, ...), custom_call_target="tpu_custom_call" | custom-call | tf_op jit(solution)/shard_map/final/pallas_call | solution.py:451
  (9 shorter events, 0.2 us)
Async XLA Ops:
  4.3 2.5 %collective-permute-start = (bf16[1536,256]{1,0:T(8,128)(2,1)S(1)}, bf16[1536,256]{1,0:T(8,128)(2,1)S(1)}, u32[]{:S(2)}, u32[]{:S(2)}) collective-permute-start(bf16[1536,256]{1,0:T(8,128)(2,1)S(1)} %get-tuple-element.12.mine), channel_id=1, source_target_pairs={{0,1},{1,0},{2,3},{3,2},{4,5},{5,4},{6,7},{7,6},{8,9},{9,8},{10,11... | collective-permute-start | bytes 2359304 | tf_op jit(solution)/shard_map/ppermute | solution.py:247
  6.7 25.5 %copy-start = (bf16[512,256]{1,0:T(8,128)(2,1)S(1)}, bf16[512,256]{1,0:T(8,128)(2,1)}, u32[]{:S(2)}) copy-start(bf16[512,256]{1,0:T(8,128)(2,1)} %sketch.3) | copy-start | bytes 786436
  7.4 5.3 %collective-permute-start.1 = (bf16[64,512]{1,0:T(8,128)(2,1)S(1)}, bf16[64,512]{1,0:T(8,128)(2,1)S(1)}, u32[]{:S(2)}, u32[]{:S(2)}) collective-permute-start(bf16[64,512]{1,0:T(8,128)(2,1)S(1)} %get-tuple-element.15), channel_id=1, source_target_pairs={{0,2},{2,0},{4,6},{6,4},{8,10},{10,8},{12,14},{14,12},{16,18},{18,... | collective-permute-start | bytes 196616 | tf_op jit(solution)/shard_map/ppermute | solution.py:162
  10.3 4.3 %collective-permute-start.2 = (bf16[64,512]{1,0:T(8,128)(2,1)S(1)}, bf16[64,512]{1,0:T(8,128)(2,1)S(1)}, u32[]{:S(2)}, u32[]{:S(2)}) collective-permute-start(bf16[64,512]{1,0:T(8,128)(2,1)S(1)} %get-tuple-element.16), channel_id=1, source_target_pairs={{0,4},{2,6},{4,0},{6,2},{8,12},{10,14},{12,8},{14,10},{16,20},{18,... | collective-permute-start | bytes 196616 | tf_op jit(solution)/shard_map/ppermute | solution.py:162
  11.8 5.2 %collective-permute-start.3 = (bf16[64,512]{1,0:T(8,128)(2,1)S(1)}, bf16[64,512]{1,0:T(8,128)(2,1)S(1)}, u32[]{:S(2)}, u32[]{:S(2)}) collective-permute-start(bf16[64,512]{1,0:T(8,128)(2,1)S(1)} %get-tuple-element.17), channel_id=1, source_target_pairs={{0,6},{2,4},{4,2},{6,0},{8,14},{10,12},{12,10},{14,8},{16,22},{18,... | collective-permute-start | bytes 196616 | tf_op jit(solution)/shard_map/ppermute | solution.py:162
  17.0 6.1 %collective-permute-start.6 = (bf16[64,512]{1,0:T(8,128)(2,1)S(1)}, bf16[64,512]{1,0:T(8,128)(2,1)S(1)}, u32[]{:S(2)}, u32[]{:S(2)}) collective-permute-start(bf16[64,512]{1,0:T(8,128)(2,1)S(1)} %reduce0.1.refs_0_), channel_id=1, source_target_pairs={{0,24},{2,26},{4,28},{6,30},{8,16},{10,18},{12,20},{14,22},{16,8},... | collective-permute-start | bytes 196616 | tf_op jit(solution)/shard_map/ppermute | solution.py:162
  20.7 5.2 %collective-permute-start.5 = (bf16[64,512]{1,0:T(8,128)(2,1)S(1)}, bf16[64,512]{1,0:T(8,128)(2,1)S(1)}, u32[]{:S(2)}, u32[]{:S(2)}) collective-permute-start(bf16[64,512]{1,0:T(8,128)(2,1)S(1)} %reduce0.1.refs_0_), channel_id=1, source_target_pairs={{0,16},{2,18},{4,20},{6,22},{8,24},{10,26},{12,28},{14,30},{16,0},... | collective-permute-start | bytes 196616 | tf_op jit(solution)/shard_map/ppermute | solution.py:162
  20.7 5.2 %collective-permute-start.4 = (bf16[64,512]{1,0:T(8,128)(2,1)S(1)}, bf16[64,512]{1,0:T(8,128)(2,1)S(1)}, u32[]{:S(2)}, u32[]{:S(2)}) collective-permute-start(bf16[64,512]{1,0:T(8,128)(2,1)S(1)} %reduce0.1.refs_0_), channel_id=1, source_target_pairs={{0,8},{2,10},{4,12},{6,14},{8,0},{10,2},{12,4},{14,6},{16,24},{18,... | collective-permute-start | bytes 196616 | tf_op jit(solution)/shard_map/ppermute | solution.py:162
  25.9 5.3 %collective-permute-start.9 = (bf16[64,512]{1,0:T(8,128)(2,1)S(1)}, bf16[64,512]{1,0:T(8,128)(2,1)S(1)}, u32[]{:S(2)}, u32[]{:S(2)}) collective-permute-start(bf16[64,512]{1,0:T(8,128)(2,1)S(1)} %total.1.refs_0_), channel_id=1, source_target_pairs={{0,6},{2,4},{4,2},{6,0},{8,14},{10,12},{12,10},{14,8},{16,22},{18,... | collective-permute-start | bytes 196616 | tf_op jit(solution)/shard_map/ppermute | solution.py:162
  26.4 5.0 %collective-permute-start.8 = (bf16[64,512]{1,0:T(8,128)(2,1)S(1)}, bf16[64,512]{1,0:T(8,128)(2,1)S(1)}, u32[]{:S(2)}, u32[]{:S(2)}) collective-permute-start(bf16[64,512]{1,0:T(8,128)(2,1)S(1)} %total.1.refs_0_), channel_id=1, source_target_pairs={{0,4},{2,6},{4,0},{6,2},{8,12},{10,14},{12,8},{14,10},{16,20},{18,... | collective-permute-start | bytes 196616 | tf_op jit(solution)/shard_map/ppermute | solution.py:162
  27.9 4.3 %collective-permute-start.7 = (bf16[64,512]{1,0:T(8,128)(2,1)S(1)}, bf16[64,512]{1,0:T(8,128)(2,1)S(1)}, u32[]{:S(2)}, u32[]{:S(2)}) collective-permute-start(bf16[64,512]{1,0:T(8,128)(2,1)S(1)} %total.1.refs_0_), channel_id=1, source_target_pairs={{0,2},{2,0},{4,6},{6,4},{8,10},{10,8},{12,14},{14,12},{16,18},{18,... | collective-permute-start | bytes 196616 | tf_op jit(solution)/shard_map/ppermute | solution.py:162
  32.5 1.6 %collective-permute-start.10 = (f32[256,256]{1,0:T(8,128)S(1)}, f32[256,256]{1,0:T(8,128)S(1)}, u32[]{:S(2)}, u32[]{:S(2)}) collective-permute-start(f32[256,256]{1,0:T(8,128)S(1)} %get-tuple-element.18.refs_0_), channel_id=1, source_target_pairs={{0,1},{1,0},{2,3},{3,2},{4,5},{5,4},{6,7},{7,6},{8,9},{9,8},{10,11... | collective-permute-start | bytes 786440 | tf_op jit(solution)/shard_map/ppermute | solution.py:297
  32.6 9.1 %collective-permute-start.11 = (f32[256,256]{1,0:T(8,128)S(1)}, f32[256,256]{1,0:T(8,128)S(1)}, u32[]{:S(2)}, u32[]{:S(2)}) collective-permute-start(f32[256,256]{1,0:T(8,128)S(1)} %get-tuple-element.19.refs_1_), channel_id=1, source_target_pairs={{0,1},{1,0},{2,3},{3,2},{4,5},{5,4},{6,7},{7,6},{8,9},{9,8},{10,11... | collective-permute-start | bytes 786440 | tf_op jit(solution)/shard_map/ppermute | solution.py:298

commit v5 on v4

--- a/solution.py
+++ b/solution.py
@@ -10,7 +10,7 @@
 f32 = jnp.float32
 bf16 = jnp.bfloat16
 LANES = 128
-PANEL = 16
+PANEL, SUB = 32, 16
 VMEM = pl.BlockSpec(memory_space=pltpu.VMEM)
 GRANT = pltpu.CompilerParams(vmem_limit_bytes=24 << 20)
 
@@ -332,27 +332,37 @@
             for t in range(parts)
         ]
         at = r0 - first * LANES
-        pivots = [
-            [jnp.broadcast_to(rows[t][0][:, at + j : at + j + 1], (8, LANES)) for t in range(parts)]
-            for j in range(PANEL)
-        ]
-        for j in range(PANEL):
-            tj, sj = divmod(j, 8)
-            scale = lax.rsqrt(jnp.broadcast_to(pivots[j][tj][sj : sj + 1, :], (8, LANES)))
-            times = {}
-            for t in range(tj, parts):
-                value = pivots[j][t] * scale
-                times[t] = jnp.where(sub > sj, value, 0.0) if t == tj else value
-            for k in range(j + 1, PANEL):
-                line = jnp.broadcast_to(pivots[k][tj][sj : sj + 1, :], (8, LANES)) * scale
+        for s in range(0, PANEL, SUB):
+            pivots = {
+                s + j: {
+                    t: jnp.broadcast_to(rows[t][0][:, at + s + j : at + s + j + 1], (8, LANES))
+                    for t in range(s // 8, parts)
+                }
+                for j in range(SUB)
+            }
+            scales = {t: jnp.zeros((8, LANES), f32) for t in range(s // 8, (s + SUB) // 8)}
+            for j in range(s, s + SUB):
+                tj, sj = divmod(j, 8)
+                line = jnp.broadcast_to(pivots[j][tj][sj : sj + 1, :], (8, LANES))
+                scale = lax.rsqrt(line)
+                scales[tj] = jnp.where(sub == sj, scale, scales[tj])
+                inverse = scale * scale
+                times = {}
                 for t in range(tj, parts):
-                    if t > tj or sj < 7:
-                        pivots[k][t] = pivots[k][t] - times[t] * line
-            for p in range(len(places)):
-                line = jnp.broadcast_to(rows[tj][p][sj : sj + 1, :], (8, LANES)) * scale
-                for t in range(tj, parts):
-                    updated = rows[t][p] - times[t] * line
-                    rows[t][p] = jnp.where(sub == sj, line, updated) if t == tj else updated
+                    value = pivots[j][t] * inverse
+                    times[t] = jnp.where(sub > sj, value, 0.0) if t == tj else value
+                for k in range(j + 1, s + SUB):
+                    line = jnp.broadcast_to(pivots[k][tj][sj : sj + 1, :], (8, LANES))
+                    for t in range(tj, parts):
+                        if t > tj or sj < 7:
+                            pivots[k][t] = pivots[k][t] - times[t] * line
+                for p in range(len(places)):
+                    line = jnp.broadcast_to(rows[tj][p][sj : sj + 1, :], (8, LANES))
+                    for t in range(tj, parts):
+                        if t > tj or sj < 7:
+                            rows[t][p] = rows[t][p] - times[t] * line
+            for t in scales:
+                rows[t] = [r * scales[t] for r in rows[t]]
         done = jnp.concatenate([jnp.concatenate(r, axis=1) for r in rows], axis=0)
         ahead = tiles - first
         for k in range(first + 1):
@@ -365,12 +375,14 @@
             skip = (nxt - first) * LANES
             lhs = jnp.concatenate([hi, hi, mid, mid, hi, lo], axis=0)[:, skip : LANES * ahead]
             rhs = jnp.concatenate([hi, mid, hi, mid, lo, hi], axis=0)[:, skip:]
-            change = dot(lhs, rhs, TN)
-            top = r1 - nxt * LANES
             wide = LANES * (tiles - nxt)
             end = n + LANES * (first + 1)
-            work[r1:, LANES * nxt : n] = work[r1:, LANES * nxt : n] - change[top:, :wide]
-            work[r1:, n:end] = work[r1:, n:end] - change[top:, wide:]
+            lhs = lhs.T
+            for at, to in ((r1, r1 + PANEL), (r1 + PANEL, n)):
+                if at < to:
+                    change = dot(lhs[at - nxt * LANES : to - nxt * LANES, :], rhs)
+                    work[at:to, LANES * nxt : n] = work[at:to, LANES * nxt : n] - change[:, :wide]
+                    work[at:to, n:end] = work[at:to, n:end] - change[:, wide:]
 
 
 def shrink_map(inverse, turned, outer, projected):

time: 47.8 us -> 46.7 us (0.977)
  Pallas kernels: 18.1 us -> 17.1 us
    pallas_call x5, Pallas kernels: 8.64 us -> 7.59 us  [call(): pl.pallas_call(body, in_specs=[VMEM] * len(ins), out_specs=[VMEM] * len(o...]
  transfers between devices with their start and end apart: 12 -> 12, of which waited for: 10 -> 10; matrix products, arithmetic and copies ran while one was open for 0% -> 0% of each run, Pallas kernels for 16% -> 14%
where the time goes in v5:
time: 46.7 us; the launch traced here: 46.6 us
  Pallas kernels  17.1 us (37%)
  waiting for transfers between devices  15.2 us (33%)
  starting transfers between devices  13.6 us (29%)
  between operations  0.68 us (1%)
    ppermute x9, starting transfers between devices, exchange(): return lax.ppermute(value, 'unit', [(u, partner(u)) for u in range(size)])  12.5 us
    ppermute x9, waiting for transfers between devices, exchange(): return lax.ppermute(value, 'unit', [(u, partner(u)) for u in range(size)])  12.3 us
    pallas_call x5, Pallas kernels, call(): pl.pallas_call(body, in_specs=[VMEM] * len(ins), out_specs=[VMEM] * len(o...  7.59 us
    pallas_call x1, Pallas kernels, final(): pl.pallas_call(functools.partial(final_body, len(outers), total), in_spec...  5.86 us
    pallas_call x1, Pallas kernels, front(): pl.pallas_call(front_body, in_specs=[hbm] * 5, out_specs=[VMEM, VMEM], ou...  3.62 us
    ppermute x1, waiting for transfers between devices, sums_by_exchange(): other = lax.ppermute(part, 'week', swap)  1.91 us
    ppermute x1, waiting for transfers between devices, sums_by_exchange(): gram_other = lax.ppermute(gram, 'week', swap)  1.02 us
  transfers between devices with their start and end apart: 12, of which 10 were waited for; matrix products, arithmetic and copies ran while one was open for 0% of the time, Pallas kernels for 14%

profile of v5, /device:TPU:0, one launch (start us, length us, event | category | flops | bytes accessed | tf_op | source)
XLA Modules:
  0.0 46.6 jit_solution(17471393958505703291)
XLA Ops:
  0.6 3.6 %front.1 = (bf16[1536,512]{1,0:T(8,128)(2,1)S(1)}, bf16[1536,256]{1,0:T(8,128)(2,1)S(1)}) custom-call(bf16[1536,512]{1,0:T(8,128)(2,1)} %panel.1, s32[1536]{0:T(1024)} %start.1, f32[1536,256]{1,0:T(8,128)} %left.1, f32[256,512]{1,0:T(8,128)} %right.1, bf16[512,256]{1,0:T(8,128)(2,1)} %sketch.3), custom_call_target="tpu_custom_call" | custom-call | tf_op jit(solution)/shard_map/front/pallas_call | solution.py:127
  4.3 0.6 %collective-permute-start = (bf16[1536,256]{1,0:T(8,128)(2,1)S(1)}, bf16[1536,256]{1,0:T(8,128)(2,1)S(1)}, u32[]{:S(2)}, u32[]{:S(2)}) collective-permute-start(bf16[1536,256]{1,0:T(8,128)(2,1)S(1)} %get-tuple-element.12.mine), channel_id=1, source_target_pairs={{0,1},{1,0},{2,3},{3,2},{4,5},{5,4},{6,7},{7,6},{8,9},{9,8},{10,11... | collective-permute-start | bytes 2359304 | tf_op jit(solution)/shard_map/ppermute | solution.py:247
  4.8 1.9 %collective-permute-done.other = bf16[1536,256]{1,0:T(8,128)(2,1)S(1)} collective-permute-done((bf16[1536,256]{1,0:T(8,128)(2,1)S(1)}, bf16[1536,256]{1,0:T(8,128)(2,1)S(1)}, u32[]{:S(2)}, u32[]{:S(2)}) %collective-permute-start) | collective-permute-done | bytes 786464 | tf_op jit(solution)/shard_map/ppermute | solution.py:247
  6.7 0.6 %moments.1 = (bf16[1536,256]{1,0:T(8,128)(2,1)S(1)}, bf16[64,512]{1,0:T(8,128)(2,1)S(1)}, bf16[64,512]{1,0:T(8,128)(2,1)S(1)}, bf16[64,512]{1,0:T(8,128)(2,1)S(1)}, bf16[64,512]{1,0:T(8,128)(2,1)S(1)}) custom-call(bf16[1536,256]{1,0:T(8,128)(2,1)S(1)} %get-tuple-element.12.mine, bf16[1536,256]{1,0:T(8,128)(2,1)S(1)} %collective-permute-done.other, ...), custom_call_target="tpu_custom_call" | custom-call | tf_op jit(solution)/shard_map/moments/pallas_call | solution.py:231
  7.4 2.9 %collective-permute-start.1 = (bf16[64,512]{1,0:T(8,128)(2,1)S(1)}, bf16[64,512]{1,0:T(8,128)(2,1)S(1)}, u32[]{:S(2)}, u32[]{:S(2)}) collective-permute-start(bf16[64,512]{1,0:T(8,128)(2,1)S(1)} %get-tuple-element.15), channel_id=1, source_target_pairs={{0,2},{2,0},{4,6},{6,4},{8,10},{10,8},{12,14},{14,12},{16,18},{18,... | collective-permute-start | bytes 196616 | tf_op jit(solution)/shard_map/ppermute | solution.py:162
  10.3 1.5 %collective-permute-start.2 = (bf16[64,512]{1,0:T(8,128)(2,1)S(1)}, bf16[64,512]{1,0:T(8,128)(2,1)S(1)}, u32[]{:S(2)}, u32[]{:S(2)}) collective-permute-start(bf16[64,512]{1,0:T(8,128)(2,1)S(1)} %get-tuple-element.16), channel_id=1, source_target_pairs={{0,4},{2,6},{4,0},{6,2},{8,12},{10,14},{12,8},{14,10},{16,20},{18,... | collective-permute-start | bytes 196616 | tf_op jit(solution)/shard_map/ppermute | solution.py:162
  11.8 0.9 %collective-permute-done.1.refs_1_ = bf16[64,512]{1,0:T(8,128)(2,1)S(1)} collective-permute-done((bf16[64,512]{1,0:T(8,128)(2,1)S(1)}, bf16[64,512]{1,0:T(8,128)(2,1)S(1)}, u32[]{:S(2)}, u32[]{:S(2)}) %collective-permute-start.1) | collective-permute-done | bytes 65568 | tf_op jit(solution)/shard_map/ppermute | solution.py:162
  12.7 1.9 %collective-permute-done.2.refs_2_ = bf16[64,512]{1,0:T(8,128)(2,1)S(1)} collective-permute-done((bf16[64,512]{1,0:T(8,128)(2,1)S(1)}, bf16[64,512]{1,0:T(8,128)(2,1)S(1)}, u32[]{:S(2)}, u32[]{:S(2)}) %collective-permute-start.2) | collective-permute-done | bytes 65568 | tf_op jit(solution)/shard_map/ppermute | solution.py:162
  14.5 2.4 %collective-permute-done.3.refs_3_ = bf16[64,512]{1,0:T(8,128)(2,1)S(1)} collective-permute-done((bf16[64,512]{1,0:T(8,128)(2,1)S(1)}, bf16[64,512]{1,0:T(8,128)(2,1)S(1)}, u32[]{:S(2)}, u32[]{:S(2)}) %collective-permute-start.3) | collective-permute-done | bytes 65568 | tf_op jit(solution)/shard_map/ppermute | solution.py:162
  17.0 3.7 %collective-permute-start.6 = (bf16[64,512]{1,0:T(8,128)(2,1)S(1)}, bf16[64,512]{1,0:T(8,128)(2,1)S(1)}, u32[]{:S(2)}, u32[]{:S(2)}) collective-permute-start(bf16[64,512]{1,0:T(8,128)(2,1)S(1)} %reduce0.1.refs_0_), channel_id=1, source_target_pairs={{0,24},{2,26},{4,28},{6,30},{8,16},{10,18},{12,20},{14,22},{16,8},... | collective-permute-start | bytes 196616 | tf_op jit(solution)/shard_map/ppermute | solution.py:162
  20.7 0.8 %collective-permute-start.4 = (bf16[64,512]{1,0:T(8,128)(2,1)S(1)}, bf16[64,512]{1,0:T(8,128)(2,1)S(1)}, u32[]{:S(2)}, u32[]{:S(2)}) collective-permute-start(bf16[64,512]{1,0:T(8,128)(2,1)S(1)} %reduce0.1.refs_0_), channel_id=1, source_target_pairs={{0,8},{2,10},{4,12},{6,14},{8,0},{10,2},{12,4},{14,6},{16,24},{18,... | collective-permute-start | bytes 196616 | tf_op jit(solution)/shard_map/ppermute | solution.py:162
  21.5 1.7 %collective-permute-done.6.refs_3_ = bf16[64,512]{1,0:T(8,128)(2,1)S(1)} collective-permute-done((bf16[64,512]{1,0:T(8,128)(2,1)S(1)}, bf16[64,512]{1,0:T(8,128)(2,1)S(1)}, u32[]{:S(2)}, u32[]{:S(2)}) %collective-permute-start.6) | collective-permute-done | bytes 65568 | tf_op jit(solution)/shard_map/ppermute | solution.py:162
  23.1 2.7 %collective-permute-done.5.refs_2_ = bf16[64,512]{1,0:T(8,128)(2,1)S(1)} collective-permute-done((bf16[64,512]{1,0:T(8,128)(2,1)S(1)}, bf16[64,512]{1,0:T(8,128)(2,1)S(1)}, u32[]{:S(2)}, u32[]{:S(2)}) %collective-permute-start.5) | collective-permute-done | bytes 65568 | tf_op jit(solution)/shard_map/ppermute | solution.py:162
  25.9 0.5 %collective-permute-start.9 = (bf16[64,512]{1,0:T(8,128)(2,1)S(1)}, bf16[64,512]{1,0:T(8,128)(2,1)S(1)}, u32[]{:S(2)}, u32[]{:S(2)}) collective-permute-start(bf16[64,512]{1,0:T(8,128)(2,1)S(1)} %total.1.refs_0_), channel_id=1, source_target_pairs={{0,6},{2,4},{4,2},{6,0},{8,14},{10,12},{12,10},{14,8},{16,22},{18,... | collective-permute-start | bytes 196616 | tf_op jit(solution)/shard_map/ppermute | solution.py:162
  26.4 1.5 %collective-permute-start.8 = (bf16[64,512]{1,0:T(8,128)(2,1)S(1)}, bf16[64,512]{1,0:T(8,128)(2,1)S(1)}, u32[]{:S(2)}, u32[]{:S(2)}) collective-permute-start(bf16[64,512]{1,0:T(8,128)(2,1)S(1)} %total.1.refs_0_), channel_id=1, source_target_pairs={{0,4},{2,6},{4,0},{6,2},{8,12},{10,14},{12,8},{14,10},{16,20},{18,... | collective-permute-start | bytes 196616 | tf_op jit(solution)/shard_map/ppermute | solution.py:162
  27.9 1.5 %collective-permute-start.7 = (bf16[64,512]{1,0:T(8,128)(2,1)S(1)}, bf16[64,512]{1,0:T(8,128)(2,1)S(1)}, u32[]{:S(2)}, u32[]{:S(2)}) collective-permute-start(bf16[64,512]{1,0:T(8,128)(2,1)S(1)} %total.1.refs_0_), channel_id=1, source_target_pairs={{0,2},{2,0},{4,6},{6,4},{8,10},{10,8},{12,14},{14,12},{16,18},{18,... | collective-permute-start | bytes 196616 | tf_op jit(solution)/shard_map/ppermute | solution.py:162
  29.4 1.8 %collective-permute-done.9.refs_3_ = bf16[64,512]{1,0:T(8,128)(2,1)S(1)} collective-permute-done((bf16[64,512]{1,0:T(8,128)(2,1)S(1)}, bf16[64,512]{1,0:T(8,128)(2,1)S(1)}, u32[]{:S(2)}, u32[]{:S(2)}) %collective-permute-start.9) | collective-permute-done | bytes 65568 | tf_op jit(solution)/shard_map/ppermute | solution.py:162
  31.2 0.2 collective-permute-done.8.refs_2_
  31.4 0.8 %collective-permute-done.7.refs_1_ = bf16[64,512]{1,0:T(8,128)(2,1)S(1)} collective-permute-done((bf16[64,512]{1,0:T(8,128)(2,1)S(1)}, bf16[64,512]{1,0:T(8,128)(2,1)S(1)}, u32[]{:S(2)}, u32[]{:S(2)}) %collective-permute-start.7) | collective-permute-done | bytes 65568 | tf_op jit(solution)/shard_map/ppermute | solution.py:162
  32.2 0.3 last_join.1
  32.6 0.5 %collective-permute-start.11 = (f32[256,256]{1,0:T(8,128)S(1)}, f32[256,256]{1,0:T(8,128)S(1)}, u32[]{:S(2)}, u32[]{:S(2)}) collective-permute-start(f32[256,256]{1,0:T(8,128)S(1)} %get-tuple-element.19.refs_1_), channel_id=1, source_target_pairs={{0,1},{1,0},{2,3},{3,2},{4,5},{5,4},{6,7},{7,6},{8,9},{9,8},{10,11... | collective-permute-start | bytes 786440 | tf_op jit(solution)/shard_map/ppermute | solution.py:298
  33.1 1.0 %collective-permute-done.10.refs_1_ = f32[256,256]{1,0:T(8,128)S(1)} collective-permute-done((f32[256,256]{1,0:T(8,128)S(1)}, f32[256,256]{1,0:T(8,128)S(1)}, u32[]{:S(2)}, u32[]{:S(2)}) %collective-permute-start.10) | collective-permute-done | bytes 262176 | tf_op jit(solution)/shard_map/ppermute | solution.py:297
  34.1 6.5 %factor.1.refs_0_ = f32[256,256]{1,0:T(8,128)S(1)} custom-call(f32[256,256]{1,0:T(8,128)S(1)} %get-tuple-element.18.refs_0_, f32[256,256]{1,0:T(8,128)S(1)} %collective-permute-done.10.refs_1_), custom_call_target="tpu_custom_call" | custom-call | tf_op jit(solution)/shard_map/factor/pallas_call | solution.py:231
  40.7 5.9 %final.1 = (f32[1536,256]{1,0:T(8,128)}, bf16[1536,512]{1,0:T(8,128)(2,1)}) custom-call(f32[256,256]{1,0:T(8,128)S(1)} %factor.1.refs_0_, f32[256,256]{1,0:T(8,128)S(1)} %get-tuple-element.19.refs_1_, f32[256,256]{1,0:T(8,128)S(1)} %collective-permute-done.11.refs_2_, bf16[256,512]{1,0:T(8,128)(2,1)S(1)} %get-tuple-element.20.refs_3_, ...), custom_call_target="tpu_custom_call" | custom-call | tf_op jit(solution)/shard_map/final/pallas_call | solution.py:463
  (9 shorter events, 0.2 us)
Async XLA Ops:
  4.3 2.5 %collective-permute-start = (bf16[1536,256]{1,0:T(8,128)(2,1)S(1)}, bf16[1536,256]{1,0:T(8,128)(2,1)S(1)}, u32[]{:S(2)}, u32[]{:S(2)}) collective-permute-start(bf16[1536,256]{1,0:T(8,128)(2,1)S(1)} %get-tuple-element.12.mine), channel_id=1, source_target_pairs={{0,1},{1,0},{2,3},{3,2},{4,5},{5,4},{6,7},{7,6},{8,9},{9,8},{10,11... | collective-permute-start | bytes 2359304 | tf_op jit(solution)/shard_map/ppermute | solution.py:247
  6.7 25.5 %copy-start = (bf16[512,256]{1,0:T(8,128)(2,1)S(1)}, bf16[512,256]{1,0:T(8,128)(2,1)}, u32[]{:S(2)}) copy-start(bf16[512,256]{1,0:T(8,128)(2,1)} %sketch.3) | copy-start | bytes 786436
  7.4 5.3 %collective-permute-start.1 = (bf16[64,512]{1,0:T(8,128)(2,1)S(1)}, bf16[64,512]{1,0:T(8,128)(2,1)S(1)}, u32[]{:S(2)}, u32[]{:S(2)}) collective-permute-start(bf16[64,512]{1,0:T(8,128)(2,1)S(1)} %get-tuple-element.15), channel_id=1, source_target_pairs={{0,2},{2,0},{4,6},{6,4},{8,10},{10,8},{12,14},{14,12},{16,18},{18,... | collective-permute-start | bytes 196616 | tf_op jit(solution)/shard_map/ppermute | solution.py:162
  10.3 4.3 %collective-permute-start.2 = (bf16[64,512]{1,0:T(8,128)(2,1)S(1)}, bf16[64,512]{1,0:T(8,128)(2,1)S(1)}, u32[]{:S(2)}, u32[]{:S(2)}) collective-permute-start(bf16[64,512]{1,0:T(8,128)(2,1)S(1)} %get-tuple-element.16), channel_id=1, source_target_pairs={{0,4},{2,6},{4,0},{6,2},{8,12},{10,14},{12,8},{14,10},{16,20},{18,... | collective-permute-start | bytes 196616 | tf_op jit(solution)/shard_map/ppermute | solution.py:162
  11.8 5.2 %collective-permute-start.3 = (bf16[64,512]{1,0:T(8,128)(2,1)S(1)}, bf16[64,512]{1,0:T(8,128)(2,1)S(1)}, u32[]{:S(2)}, u32[]{:S(2)}) collective-permute-start(bf16[64,512]{1,0:T(8,128)(2,1)S(1)} %get-tuple-element.17), channel_id=1, source_target_pairs={{0,6},{2,4},{4,2},{6,0},{8,14},{10,12},{12,10},{14,8},{16,22},{18,... | collective-permute-start | bytes 196616 | tf_op jit(solution)/shard_map/ppermute | solution.py:162
  17.0 6.1 %collective-permute-start.6 = (bf16[64,512]{1,0:T(8,128)(2,1)S(1)}, bf16[64,512]{1,0:T(8,128)(2,1)S(1)}, u32[]{:S(2)}, u32[]{:S(2)}) collective-permute-start(bf16[64,512]{1,0:T(8,128)(2,1)S(1)} %reduce0.1.refs_0_), channel_id=1, source_target_pairs={{0,24},{2,26},{4,28},{6,30},{8,16},{10,18},{12,20},{14,22},{16,8},... | collective-permute-start | bytes 196616 | tf_op jit(solution)/shard_map/ppermute | solution.py:162
  20.7 5.2 %collective-permute-start.5 = (bf16[64,512]{1,0:T(8,128)(2,1)S(1)}, bf16[64,512]{1,0:T(8,128)(2,1)S(1)}, u32[]{:S(2)}, u32[]{:S(2)}) collective-permute-start(bf16[64,512]{1,0:T(8,128)(2,1)S(1)} %reduce0.1.refs_0_), channel_id=1, source_target_pairs={{0,16},{2,18},{4,20},{6,22},{8,24},{10,26},{12,28},{14,30},{16,0},... | collective-permute-start | bytes 196616 | tf_op jit(solution)/shard_map/ppermute | solution.py:162
  20.7 5.2 %collective-permute-start.4 = (bf16[64,512]{1,0:T(8,128)(2,1)S(1)}, bf16[64,512]{1,0:T(8,128)(2,1)S(1)}, u32[]{:S(2)}, u32[]{:S(2)}) collective-permute-start(bf16[64,512]{1,0:T(8,128)(2,1)S(1)} %reduce0.1.refs_0_), channel_id=1, source_target_pairs={{0,8},{2,10},{4,12},{6,14},{8,0},{10,2},{12,4},{14,6},{16,24},{18,... | collective-permute-start | bytes 196616 | tf_op jit(solution)/shard_map/ppermute | solution.py:162
  25.9 5.3 %collective-permute-start.9 = (bf16[64,512]{1,0:T(8,128)(2,1)S(1)}, bf16[64,512]{1,0:T(8,128)(2,1)S(1)}, u32[]{:S(2)}, u32[]{:S(2)}) collective-permute-start(bf16[64,512]{1,0:T(8,128)(2,1)S(1)} %total.1.refs_0_), channel_id=1, source_target_pairs={{0,6},{2,4},{4,2},{6,0},{8,14},{10,12},{12,10},{14,8},{16,22},{18,... | collective-permute-start | bytes 196616 | tf_op jit(solution)/shard_map/ppermute | solution.py:162
  26.4 5.0 %collective-permute-start.8 = (bf16[64,512]{1,0:T(8,128)(2,1)S(1)}, bf16[64,512]{1,0:T(8,128)(2,1)S(1)}, u32[]{:S(2)}, u32[]{:S(2)}) collective-permute-start(bf16[64,512]{1,0:T(8,128)(2,1)S(1)} %total.1.refs_0_), channel_id=1, source_target_pairs={{0,4},{2,6},{4,0},{6,2},{8,12},{10,14},{12,8},{14,10},{16,20},{18,... | collective-permute-start | bytes 196616 | tf_op jit(solution)/shard_map/ppermute | solution.py:162
  27.9 4.3 %collective-permute-start.7 = (bf16[64,512]{1,0:T(8,128)(2,1)S(1)}, bf16[64,512]{1,0:T(8,128)(2,1)S(1)}, u32[]{:S(2)}, u32[]{:S(2)}) collective-permute-start(bf16[64,512]{1,0:T(8,128)(2,1)S(1)} %total.1.refs_0_), channel_id=1, source_target_pairs={{0,2},{2,0},{4,6},{6,4},{8,10},{10,8},{12,14},{14,12},{16,18},{18,... | collective-permute-start | bytes 196616 | tf_op jit(solution)/shard_map/ppermute | solution.py:162
  32.5 1.6 %collective-permute-start.10 = (f32[256,256]{1,0:T(8,128)S(1)}, f32[256,256]{1,0:T(8,128)S(1)}, u32[]{:S(2)}, u32[]{:S(2)}) collective-permute-start(f32[256,256]{1,0:T(8,128)S(1)} %get-tuple-element.18.refs_0_), channel_id=1, source_target_pairs={{0,1},{1,0},{2,3},{3,2},{4,5},{5,4},{6,7},{7,6},{8,9},{9,8},{10,11... | collective-permute-start | bytes 786440 | tf_op jit(solution)/shard_map/ppermute | solution.py:297
  32.6 8.1 %collective-permute-start.11 = (f32[256,256]{1,0:T(8,128)S(1)}, f32[256,256]{1,0:T(8,128)S(1)}, u32[]{:S(2)}, u32[]{:S(2)}) collective-permute-start(f32[256,256]{1,0:T(8,128)S(1)} %get-tuple-element.19.refs_1_), channel_id=1, source_target_pairs={{0,1},{1,0},{2,3},{3,2},{4,5},{5,4},{6,7},{7,6},{8,9},{9,8},{10,11... | collective-permute-start | bytes 786440 | tf_op jit(solution)/shard_map/ppermute | solution.py:298

commit v6 on v5

--- a/solution.py
+++ b/solution.py
@@ -220,11 +220,13 @@
 
 
 def last_join_body(place, sketch, *refs):
-    *pieces, projected_out, gram_out, outer_out = refs
+    *pieces, projected_out, gram_out = refs
     gather_rows(pieces, *place, projected_out)
-    projected = projected_out[...]
-    gram_out[...] = dot(projected, sketch[...])
-    outer_out[...] = dot(projected, projected, NT)
+    gram_out[...] = dot(projected_out[...], sketch[...])
+
+
+def outer_body(projected, outer_out):
+    outer_out[...] = dot(projected[...], projected[...], NT)
 
 
 def call(body, ins, outs, name, scratch=()):
@@ -288,13 +290,14 @@
         ]
         place = (stride, radix)
         length *= radix
-    projected, gram, outer = call(
+    projected, gram = call(
         functools.partial(last_join_body, place),
         [sketch, *pieces],
-        [((rank, cols), bf16), ((rank, rank), f32), ((rank, rank), f32)],
+        [((rank, cols), bf16), ((rank, rank), f32)],
         "last_join",
     )
     gram_other = lax.ppermute(gram, "week", swap)
+    (outer,) = call(outer_body, [projected], [((rank, rank), f32)], "outer")
     outer_other = lax.ppermute(outer, "week", swap)
     return ranged, (gram, gram_other), projected, (outer, outer_other)
 
@@ -407,12 +410,17 @@
     while True:
         after = 2.0 * top * top - 1.0
         gain = 1.0 + 1.0 / after
+        if top > 16.0:
+            small = residual.astype(bf16)
+            solve = gain * (solve + dot(solve.astype(bf16), small))
+            square_of = dot(small, small)
+        else:
+            pair = right3(residual)
+            solve = gain * (solve + dot(left3(solve), pair))
+            square_of = dot(left3(residual), pair)
         if after > 1.0e6:
-            solve = gain * (solve + dot3(solve, residual))
             break
-        pair = right3(residual)
-        solve = gain * (solve + dot(left3(solve), pair))
-        residual = gain * dot(left3(residual), pair) - jnp.where(same, 1.0 / after, 0.0)
+        residual = gain * square_of - jnp.where(same, 1.0 / after, 0.0)
         top = after
     return kept - dot(left3(solve), coeffs3)
 

time: 46.7 us -> 46.4 us (level)
    pallas_call x5 -> x6, Pallas kernels: 7.59 us -> 7.73 us  [call(): pl.pallas_call(body, in_specs=[VMEM] * len(ins), out_specs=[VMEM] * len(o...]
  transfers between devices with their start and end apart: 12 -> 12, of which waited for: 10 -> 10; matrix products, arithmetic and copies ran while one was open for 0% -> 0% of each run, Pallas kernels for 14% -> 15%
where the time goes in v6:
time: 46.4 us; the launch traced here: 46.2 us
  Pallas kernels  17 us (37%)
  waiting for transfers between devices  14.9 us (32%)
  starting transfers between devices  13.7 us (30%)
  between operations  0.7 us (2%)
    ppermute x9, starting transfers between devices, exchange(): return lax.ppermute(value, 'unit', [(u, partner(u)) for u in range(size)])  12.5 us
    ppermute x9, waiting for transfers between devices, exchange(): return lax.ppermute(value, 'unit', [(u, partner(u)) for u in range(size)])  12.3 us
    pallas_call x6, Pallas kernels, call(): pl.pallas_call(body, in_specs=[VMEM] * len(ins), out_specs=[VMEM] * len(o...  7.73 us
    pallas_call x1, Pallas kernels, final(): pl.pallas_call(functools.partial(final_body, len(outers), total), in_spec...  5.63 us
    pallas_call x1, Pallas kernels, front(): pl.pallas_call(front_body, in_specs=[hbm] * 5, out_specs=[VMEM, VMEM], ou...  3.62 us
    ppermute x1, waiting for transfers between devices, sums_by_exchange(): other = lax.ppermute(part, 'week', swap)  1.91 us
  transfers between devices with their start and end apart: 12, of which 10 were waited for; matrix products, arithmetic and copies ran while one was open for 0% of the time, Pallas kernels for 15%

profile of v6, /device:TPU:0, one launch (start us, length us, event | category | flops | bytes accessed | tf_op | source)
XLA Modules:
  0.0 46.2 jit_solution(5119910845059388674)
XLA Ops:
  0.6 3.6 %front.1 = (bf16[1536,512]{1,0:T(8,128)(2,1)S(1)}, bf16[1536,256]{1,0:T(8,128)(2,1)S(1)}) custom-call(bf16[1536,512]{1,0:T(8,128)(2,1)} %panel.1, s32[1536]{0:T(1024)} %start.1, f32[1536,256]{1,0:T(8,128)} %left.1, f32[256,512]{1,0:T(8,128)} %right.1, bf16[512,256]{1,0:T(8,128)(2,1)} %sketch.3), custom_call_target="tpu_custom_call" | custom-call | tf_op jit(solution)/shard_map/front/pallas_call | solution.py:127
  4.3 0.6 %collective-permute-start = (bf16[1536,256]{1,0:T(8,128)(2,1)S(1)}, bf16[1536,256]{1,0:T(8,128)(2,1)S(1)}, u32[]{:S(2)}, u32[]{:S(2)}) collective-permute-start(bf16[1536,256]{1,0:T(8,128)(2,1)S(1)} %get-tuple-element.11.mine), channel_id=1, source_target_pairs={{0,1},{1,0},{2,3},{3,2},{4,5},{5,4},{6,7},{7,6},{8,9},{9,8},{10,11... | collective-permute-start | bytes 2359304 | tf_op jit(solution)/shard_map/ppermute | solution.py:249
  4.8 1.9 %collective-permute-done.other = bf16[1536,256]{1,0:T(8,128)(2,1)S(1)} collective-permute-done((bf16[1536,256]{1,0:T(8,128)(2,1)S(1)}, bf16[1536,256]{1,0:T(8,128)(2,1)S(1)}, u32[]{:S(2)}, u32[]{:S(2)}) %collective-permute-start) | collective-permute-done | bytes 786464 | tf_op jit(solution)/shard_map/ppermute | solution.py:249
  6.7 0.6 %moments.1 = (bf16[1536,256]{1,0:T(8,128)(2,1)S(1)}, bf16[64,512]{1,0:T(8,128)(2,1)S(1)}, bf16[64,512]{1,0:T(8,128)(2,1)S(1)}, bf16[64,512]{1,0:T(8,128)(2,1)S(1)}, bf16[64,512]{1,0:T(8,128)(2,1)S(1)}) custom-call(bf16[1536,256]{1,0:T(8,128)(2,1)S(1)} %get-tuple-element.11.mine, bf16[1536,256]{1,0:T(8,128)(2,1)S(1)} %collective-permute-done.other, ...), custom_call_target="tpu_custom_call" | custom-call | tf_op jit(solution)/shard_map/moments/pallas_call | solution.py:233
  7.4 2.9 %collective-permute-start.1 = (bf16[64,512]{1,0:T(8,128)(2,1)S(1)}, bf16[64,512]{1,0:T(8,128)(2,1)S(1)}, u32[]{:S(2)}, u32[]{:S(2)}) collective-permute-start(bf16[64,512]{1,0:T(8,128)(2,1)S(1)} %get-tuple-element.14), channel_id=1, source_target_pairs={{0,2},{2,0},{4,6},{6,4},{8,10},{10,8},{12,14},{14,12},{16,18},{18,... | collective-permute-start | bytes 196616 | tf_op jit(solution)/shard_map/ppermute | solution.py:162
  10.3 1.5 %collective-permute-start.2 = (bf16[64,512]{1,0:T(8,128)(2,1)S(1)}, bf16[64,512]{1,0:T(8,128)(2,1)S(1)}, u32[]{:S(2)}, u32[]{:S(2)}) collective-permute-start(bf16[64,512]{1,0:T(8,128)(2,1)S(1)} %get-tuple-element.15), channel_id=1, source_target_pairs={{0,4},{2,6},{4,0},{6,2},{8,12},{10,14},{12,8},{14,10},{16,20},{18,... | collective-permute-start | bytes 196616 | tf_op jit(solution)/shard_map/ppermute | solution.py:162
  11.8 0.9 %collective-permute-done.1.refs_1_ = bf16[64,512]{1,0:T(8,128)(2,1)S(1)} collective-permute-done((bf16[64,512]{1,0:T(8,128)(2,1)S(1)}, bf16[64,512]{1,0:T(8,128)(2,1)S(1)}, u32[]{:S(2)}, u32[]{:S(2)}) %collective-permute-start.1) | collective-permute-done | bytes 65568 | tf_op jit(solution)/shard_map/ppermute | solution.py:162
  12.7 1.9 %collective-permute-done.2.refs_2_ = bf16[64,512]{1,0:T(8,128)(2,1)S(1)} collective-permute-done((bf16[64,512]{1,0:T(8,128)(2,1)S(1)}, bf16[64,512]{1,0:T(8,128)(2,1)S(1)}, u32[]{:S(2)}, u32[]{:S(2)}) %collective-permute-start.2) | collective-permute-done | bytes 65568 | tf_op jit(solution)/shard_map/ppermute | solution.py:162
  14.5 2.4 %collective-permute-done.3.refs_3_ = bf16[64,512]{1,0:T(8,128)(2,1)S(1)} collective-permute-done((bf16[64,512]{1,0:T(8,128)(2,1)S(1)}, bf16[64,512]{1,0:T(8,128)(2,1)S(1)}, u32[]{:S(2)}, u32[]{:S(2)}) %collective-permute-start.3) | collective-permute-done | bytes 65568 | tf_op jit(solution)/shard_map/ppermute | solution.py:162
  17.0 3.7 %collective-permute-start.6 = (bf16[64,512]{1,0:T(8,128)(2,1)S(1)}, bf16[64,512]{1,0:T(8,128)(2,1)S(1)}, u32[]{:S(2)}, u32[]{:S(2)}) collective-permute-start(bf16[64,512]{1,0:T(8,128)(2,1)S(1)} %reduce0.1.refs_0_), channel_id=1, source_target_pairs={{0,24},{2,26},{4,28},{6,30},{8,16},{10,18},{12,20},{14,22},{16,8},... | collective-permute-start | bytes 196616 | tf_op jit(solution)/shard_map/ppermute | solution.py:162
  20.7 0.8 %collective-permute-start.4 = (bf16[64,512]{1,0:T(8,128)(2,1)S(1)}, bf16[64,512]{1,0:T(8,128)(2,1)S(1)}, u32[]{:S(2)}, u32[]{:S(2)}) collective-permute-start(bf16[64,512]{1,0:T(8,128)(2,1)S(1)} %reduce0.1.refs_0_), channel_id=1, source_target_pairs={{0,8},{2,10},{4,12},{6,14},{8,0},{10,2},{12,4},{14,6},{16,24},{18,... | collective-permute-start | bytes 196616 | tf_op jit(solution)/shard_map/ppermute | solution.py:162
  21.5 1.7 %collective-permute-done.6.refs_3_ = bf16[64,512]{1,0:T(8,128)(2,1)S(1)} collective-permute-done((bf16[64,512]{1,0:T(8,128)(2,1)S(1)}, bf16[64,512]{1,0:T(8,128)(2,1)S(1)}, u32[]{:S(2)}, u32[]{:S(2)}) %collective-permute-start.6) | collective-permute-done | bytes 65568 | tf_op jit(solution)/shard_map/ppermute | solution.py:162
  23.1 2.7 %collective-permute-done.5.refs_2_ = bf16[64,512]{1,0:T(8,128)(2,1)S(1)} collective-permute-done((bf16[64,512]{1,0:T(8,128)(2,1)S(1)}, bf16[64,512]{1,0:T(8,128)(2,1)S(1)}, u32[]{:S(2)}, u32[]{:S(2)}) %collective-permute-start.5) | collective-permute-done | bytes 65568 | tf_op jit(solution)/shard_map/ppermute | solution.py:162
  25.9 0.5 %collective-permute-start.9 = (bf16[64,512]{1,0:T(8,128)(2,1)S(1)}, bf16[64,512]{1,0:T(8,128)(2,1)S(1)}, u32[]{:S(2)}, u32[]{:S(2)}) collective-permute-start(bf16[64,512]{1,0:T(8,128)(2,1)S(1)} %total.1.refs_0_), channel_id=1, source_target_pairs={{0,6},{2,4},{4,2},{6,0},{8,14},{10,12},{12,10},{14,8},{16,22},{18,... | collective-permute-start | bytes 196616 | tf_op jit(solution)/shard_map/ppermute | solution.py:162
  26.4 1.5 %collective-permute-start.8 = (bf16[64,512]{1,0:T(8,128)(2,1)S(1)}, bf16[64,512]{1,0:T(8,128)(2,1)S(1)}, u32[]{:S(2)}, u32[]{:S(2)}) collective-permute-start(bf16[64,512]{1,0:T(8,128)(2,1)S(1)} %total.1.refs_0_), channel_id=1, source_target_pairs={{0,4},{2,6},{4,0},{6,2},{8,12},{10,14},{12,8},{14,10},{16,20},{18,... | collective-permute-start | bytes 196616 | tf_op jit(solution)/shard_map/ppermute | solution.py:162
  27.9 1.5 %collective-permute-start.7 = (bf16[64,512]{1,0:T(8,128)(2,1)S(1)}, bf16[64,512]{1,0:T(8,128)(2,1)S(1)}, u32[]{:S(2)}, u32[]{:S(2)}) collective-permute-start(bf16[64,512]{1,0:T(8,128)(2,1)S(1)} %total.1.refs_0_), channel_id=1, source_target_pairs={{0,2},{2,0},{4,6},{6,4},{8,10},{10,8},{12,14},{14,12},{16,18},{18,... | collective-permute-start | bytes 196616 | tf_op jit(solution)/shard_map/ppermute | solution.py:162
  29.4 1.8 %collective-permute-done.9.refs_3_ = bf16[64,512]{1,0:T(8,128)(2,1)S(1)} collective-permute-done((bf16[64,512]{1,0:T(8,128)(2,1)S(1)}, bf16[64,512]{1,0:T(8,128)(2,1)S(1)}, u32[]{:S(2)}, u32[]{:S(2)}) %collective-permute-start.9) | collective-permute-done | bytes 65568 | tf_op jit(solution)/shard_map/ppermute | solution.py:162
  31.4 0.8 %collective-permute-done.7.refs_1_ = bf16[64,512]{1,0:T(8,128)(2,1)S(1)} collective-permute-done((bf16[64,512]{1,0:T(8,128)(2,1)S(1)}, bf16[64,512]{1,0:T(8,128)(2,1)S(1)}, u32[]{:S(2)}, u32[]{:S(2)}) %collective-permute-start.7) | collective-permute-done | bytes 65568 | tf_op jit(solution)/shard_map/ppermute | solution.py:162
  32.2 0.2 last_join.1
  32.5 0.3 outer.1.refs_1_
  32.8 0.6 %collective-permute-start.11 = (f32[256,256]{1,0:T(8,128)S(1)}, f32[256,256]{1,0:T(8,128)S(1)}, u32[]{:S(2)}, u32[]{:S(2)}) collective-permute-start(f32[256,256]{1,0:T(8,128)S(1)} %outer.1.refs_1_), channel_id=1, source_target_pairs={{0,1},{1,0},{2,3},{3,2},{4,5},{5,4},{6,7},{7,6},{8,9},{9,8},{10,11... | collective-permute-start | bytes 786440 | tf_op jit(solution)/shard_map/ppermute | solution.py:301
  33.4 0.7 %collective-permute-done.10.refs_1_ = f32[256,256]{1,0:T(8,128)S(1)} collective-permute-done((f32[256,256]{1,0:T(8,128)S(1)}, f32[256,256]{1,0:T(8,128)S(1)}, u32[]{:S(2)}, u32[]{:S(2)}) %collective-permute-start.10) | collective-permute-done | bytes 262176 | tf_op jit(solution)/shard_map/ppermute | solution.py:299
  34.0 6.5 %factor.1.refs_0_ = f32[256,256]{1,0:T(8,128)S(1)} custom-call(f32[256,256]{1,0:T(8,128)S(1)} %get-tuple-element.17.refs_0_, f32[256,256]{1,0:T(8,128)S(1)} %collective-permute-done.10.refs_1_), custom_call_target="tpu_custom_call" | custom-call | tf_op jit(solution)/shard_map/factor/pallas_call | solution.py:233
  40.6 5.6 %final.1 = (f32[1536,256]{1,0:T(8,128)}, bf16[1536,512]{1,0:T(8,128)(2,1)}) custom-call(f32[256,256]{1,0:T(8,128)S(1)} %factor.1.refs_0_, f32[256,256]{1,0:T(8,128)S(1)} %outer.1.refs_1_, f32[256,256]{1,0:T(8,128)S(1)} %collective-permute-done.11.refs_2_, bf16[256,512]{1,0:T(8,128)(2,1)S(1)} %get-tuple-element.18.projected.refs_3_, ...), custom_call_target="tpu_custom_call" | custom-call | tf_op jit(solution)/shard_map/final/pallas_call | solution.py:471
  (10 shorter events, 0.3 us)
Async XLA Ops:
  4.3 2.5 %collective-permute-start = (bf16[1536,256]{1,0:T(8,128)(2,1)S(1)}, bf16[1536,256]{1,0:T(8,128)(2,1)S(1)}, u32[]{:S(2)}, u32[]{:S(2)}) collective-permute-start(bf16[1536,256]{1,0:T(8,128)(2,1)S(1)} %get-tuple-element.11.mine), channel_id=1, source_target_pairs={{0,1},{1,0},{2,3},{3,2},{4,5},{5,4},{6,7},{7,6},{8,9},{9,8},{10,11... | collective-permute-start | bytes 2359304 | tf_op jit(solution)/shard_map/ppermute | solution.py:249
  6.7 25.5 %copy-start = (bf16[512,256]{1,0:T(8,128)(2,1)S(1)}, bf16[512,256]{1,0:T(8,128)(2,1)}, u32[]{:S(2)}) copy-start(bf16[512,256]{1,0:T(8,128)(2,1)} %sketch.3) | copy-start | bytes 786436
  7.4 5.3 %collective-permute-start.1 = (bf16[64,512]{1,0:T(8,128)(2,1)S(1)}, bf16[64,512]{1,0:T(8,128)(2,1)S(1)}, u32[]{:S(2)}, u32[]{:S(2)}) collective-permute-start(bf16[64,512]{1,0:T(8,128)(2,1)S(1)} %get-tuple-element.14), channel_id=1, source_target_pairs={{0,2},{2,0},{4,6},{6,4},{8,10},{10,8},{12,14},{14,12},{16,18},{18,... | collective-permute-start | bytes 196616 | tf_op jit(solution)/shard_map/ppermute | solution.py:162
  10.3 4.3 %collective-permute-start.2 = (bf16[64,512]{1,0:T(8,128)(2,1)S(1)}, bf16[64,512]{1,0:T(8,128)(2,1)S(1)}, u32[]{:S(2)}, u32[]{:S(2)}) collective-permute-start(bf16[64,512]{1,0:T(8,128)(2,1)S(1)} %get-tuple-element.15), channel_id=1, source_target_pairs={{0,4},{2,6},{4,0},{6,2},{8,12},{10,14},{12,8},{14,10},{16,20},{18,... | collective-permute-start | bytes 196616 | tf_op jit(solution)/shard_map/ppermute | solution.py:162
  11.8 5.2 %collective-permute-start.3 = (bf16[64,512]{1,0:T(8,128)(2,1)S(1)}, bf16[64,512]{1,0:T(8,128)(2,1)S(1)}, u32[]{:S(2)}, u32[]{:S(2)}) collective-permute-start(bf16[64,512]{1,0:T(8,128)(2,1)S(1)} %get-tuple-element.16), channel_id=1, source_target_pairs={{0,6},{2,4},{4,2},{6,0},{8,14},{10,12},{12,10},{14,8},{16,22},{18,... | collective-permute-start | bytes 196616 | tf_op jit(solution)/shard_map/ppermute | solution.py:162
  17.0 6.1 %collective-permute-start.6 = (bf16[64,512]{1,0:T(8,128)(2,1)S(1)}, bf16[64,512]{1,0:T(8,128)(2,1)S(1)}, u32[]{:S(2)}, u32[]{:S(2)}) collective-permute-start(bf16[64,512]{1,0:T(8,128)(2,1)S(1)} %reduce0.1.refs_0_), channel_id=1, source_target_pairs={{0,24},{2,26},{4,28},{6,30},{8,16},{10,18},{12,20},{14,22},{16,8},... | collective-permute-start | bytes 196616 | tf_op jit(solution)/shard_map/ppermute | solution.py:162
  20.7 5.2 %collective-permute-start.5 = (bf16[64,512]{1,0:T(8,128)(2,1)S(1)}, bf16[64,512]{1,0:T(8,128)(2,1)S(1)}, u32[]{:S(2)}, u32[]{:S(2)}) collective-permute-start(bf16[64,512]{1,0:T(8,128)(2,1)S(1)} %reduce0.1.refs_0_), channel_id=1, source_target_pairs={{0,16},{2,18},{4,20},{6,22},{8,24},{10,26},{12,28},{14,30},{16,0},... | collective-permute-start | bytes 196616 | tf_op jit(solution)/shard_map/ppermute | solution.py:162
  20.7 5.2 %collective-permute-start.4 = (bf16[64,512]{1,0:T(8,128)(2,1)S(1)}, bf16[64,512]{1,0:T(8,128)(2,1)S(1)}, u32[]{:S(2)}, u32[]{:S(2)}) collective-permute-start(bf16[64,512]{1,0:T(8,128)(2,1)S(1)} %reduce0.1.refs_0_), channel_id=1, source_target_pairs={{0,8},{2,10},{4,12},{6,14},{8,0},{10,2},{12,4},{14,6},{16,24},{18,... | collective-permute-start | bytes 196616 | tf_op jit(solution)/shard_map/ppermute | solution.py:162
  25.9 5.3 %collective-permute-start.9 = (bf16[64,512]{1,0:T(8,128)(2,1)S(1)}, bf16[64,512]{1,0:T(8,128)(2,1)S(1)}, u32[]{:S(2)}, u32[]{:S(2)}) collective-permute-start(bf16[64,512]{1,0:T(8,128)(2,1)S(1)} %total.1.refs_0_), channel_id=1, source_target_pairs={{0,6},{2,4},{4,2},{6,0},{8,14},{10,12},{12,10},{14,8},{16,22},{18,... | collective-permute-start | bytes 196616 | tf_op jit(solution)/shard_map/ppermute | solution.py:162
  26.4 5.0 %collective-permute-start.8 = (bf16[64,512]{1,0:T(8,128)(2,1)S(1)}, bf16[64,512]{1,0:T(8,128)(2,1)S(1)}, u32[]{:S(2)}, u32[]{:S(2)}) collective-permute-start(bf16[64,512]{1,0:T(8,128)(2,1)S(1)} %total.1.refs_0_), channel_id=1, source_target_pairs={{0,4},{2,6},{4,0},{6,2},{8,12},{10,14},{12,8},{14,10},{16,20},{18,... | collective-permute-start | bytes 196616 | tf_op jit(solution)/shard_map/ppermute | solution.py:162
  27.9 4.3 %collective-permute-start.7 = (bf16[64,512]{1,0:T(8,128)(2,1)S(1)}, bf16[64,512]{1,0:T(8,128)(2,1)S(1)}, u32[]{:S(2)}, u32[]{:S(2)}) collective-permute-start(bf16[64,512]{1,0:T(8,128)(2,1)S(1)} %total.1.refs_0_), channel_id=1, source_target_pairs={{0,2},{2,0},{4,6},{6,4},{8,10},{10,8},{12,14},{14,12},{16,18},{18,... | collective-permute-start | bytes 196616 | tf_op jit(solution)/shard_map/ppermute | solution.py:162
  32.4 1.6 %collective-permute-start.10 = (f32[256,256]{1,0:T(8,128)S(1)}, f32[256,256]{1,0:T(8,128)S(1)}, u32[]{:S(2)}, u32[]{:S(2)}) collective-permute-start(f32[256,256]{1,0:T(8,128)S(1)} %get-tuple-element.17.refs_0_), channel_id=1, source_target_pairs={{0,1},{1,0},{2,3},{3,2},{4,5},{5,4},{6,7},{7,6},{8,9},{9,8},{10,11... | collective-permute-start | bytes 786440 | tf_op jit(solution)/shard_map/ppermute | solution.py:299
  32.8 7.8 %collective-permute-start.11 = (f32[256,256]{1,0:T(8,128)S(1)}, f32[256,256]{1,0:T(8,128)S(1)}, u32[]{:S(2)}, u32[]{:S(2)}) collective-permute-start(f32[256,256]{1,0:T(8,128)S(1)} %outer.1.refs_1_), channel_id=1, source_target_pairs={{0,1},{1,0},{2,3},{3,2},{4,5},{5,4},{6,7},{7,6},{8,9},{9,8},{10,11... | collective-permute-start | bytes 786440 | tf_op jit(solution)/shard_map/ppermute | solution.py:301
